TPU v7x, 32 devices: a 4x2x2 block of a 4x4x8 slice. The times are simulated.
32 devices in a mesh: data: 4 (over y, z), model: 8 (over x, core).
Axes of the slice: x: 4, y: 2, z: 2, core: 2. Of those that a mesh axis runs over, the one named last changes fastest.
The devices are a block of a 4x4x8 slice.
Arguments:
- hidden_in: bfloat16 [4, 2048, 2560], P('data', 'model'), parts along dimension 0
- seg_ids: int32 [4, 2048], P('data'), parts along dimension 0
- gain_attn: bfloat16 [2560], replicated
- w_qkv: bfloat16 [2560, 32, 3, 80], P(None, 'model')
- w_out: bfloat16 [32, 80, 2560], P('model')
- gain_mlp: bfloat16 [2560], replicated
- w_up: bfloat16 [2560, 10240], P(None, 'model')
- w_down: bfloat16 [10240, 2560], P('model')
- grad_out: bfloat16 [4, 2048, 2560], P('data', 'model'), parts along dimension 0
Outputs:
- output 1: bfloat16 [4, 2048, 2560], P('data', 'model'), parts along dimension 0
- output 2: bfloat16 [4, 2048, 2560], P('data', 'model'), parts along dimension 0
- output 3: bfloat16 [10240, 32, 3, 80], P('data', 'model'), parts along dimension 0
- output 4: bfloat16 [128, 80, 2560], P(('data', 'model')), parts along dimension 0
- output 5: bfloat16 [10240, 10240], P('data', 'model'), parts along dimension 0
- output 6: bfloat16 [40960, 2560], P(('data', 'model')), parts along dimension 0
- output 7: bfloat16 [10240], P('data'), parts along dimension 0
- output 8: bfloat16 [10240], P('data'), parts along dimension 0
There are 4 independent parts. A program takes and returns all parts, laid end to end along the dimension named above; an argument that names none is the same for every part.
All inputs are finite; a program needn't handle non-finite values.
Results may differ from a plain program's by a relative error of at most 0.02.
Values are sent between devices in bfloat16 or wider.
A program may use at most 768 MiB of HBM per device.

v0:
```python
import jax
import jax.numpy as jnp
from jax import lax
from jax.sharding import PartitionSpec as P

LN_EPS = 1e-5


def layer_norm(x_f32, gain_f32):
    mean_val = jnp.mean(x_f32, axis=-1, keepdims=True)
    centered = x_f32 - mean_val
    variance = jnp.mean(centered * centered, axis=-1, keepdims=True)
    return centered * lax.rsqrt(variance + LN_EPS) * gain_f32


def gelu_tanh(pre_act):
    return jax.nn.gelu(pre_act, approximate=True)


def attention_fwd(qkv_vals, attn_mask, attn_scale):
    q_part = qkv_vals[:, :, :, 0]
    k_part = qkv_vals[:, :, :, 1]
    v_part = qkv_vals[:, :, :, 2]
    scores = jnp.einsum('bqhe,bkhe->bhqk', q_part, k_part, preferred_element_type=jnp.float32) * attn_scale
    attn_prob = jax.nn.softmax(jnp.where(attn_mask[:, None], scores, -1e30), axis=-1)
    prob_lo = attn_prob.astype(jnp.bfloat16)
    attn_out = jnp.einsum('bhqk,bkhe->bqhe', prob_lo, v_part, preferred_element_type=jnp.float32).astype(jnp.bfloat16)
    return attn_out, attn_prob, prob_lo


def attention_bwd(qkv_vals, attn_out, d_out, attn_prob, prob_lo, attn_scale):
    q_part = qkv_vals[:, :, :, 0]
    k_part = qkv_vals[:, :, :, 1]
    v_part = qkv_vals[:, :, :, 2]
    d_prob = jnp.einsum('bqhe,bkhe->bhqk', d_out, v_part, preferred_element_type=jnp.float32)
    row_delta = jnp.einsum('bqhe,bqhe->bhq', d_out, attn_out, preferred_element_type=jnp.float32)
    d_scores = (attn_prob * (d_prob - row_delta[..., None]) * attn_scale).astype(jnp.bfloat16)
    d_q = jnp.einsum('bhqk,bkhe->bqhe', d_scores, k_part, preferred_element_type=jnp.float32).astype(jnp.bfloat16)
    d_k = jnp.einsum('bhqk,bqhe->bkhe', d_scores, q_part, preferred_element_type=jnp.float32).astype(jnp.bfloat16)
    d_v = jnp.einsum('bhqk,bqhe->bkhe', prob_lo, d_out, preferred_element_type=jnp.float32).astype(jnp.bfloat16)
    return jnp.stack([d_q, d_k, d_v], axis=3)


def local_layer(hidden_in, seg_ids, gain_attn, w_qkv, w_out, gain_mlp, w_up, w_down, grad_out):
    attn_scale = w_out.shape[1] ** -0.5
    seq_len = seg_ids.shape[1]
    positions = jnp.arange(seq_len)
    attn_mask = (positions[:, None] >= positions[None, :])[None] & (seg_ids[:, :, None] == seg_ids[:, None, :])
    x_f32 = hidden_in.astype(jnp.float32)
    ln1_out, ln1_vjp = jax.vjp(layer_norm, x_f32, gain_attn.astype(jnp.float32))
    attn_in = lax.all_gather(ln1_out.astype(jnp.bfloat16), 'model', axis=1, tiled=True)
    qkv_vals = jnp.einsum('bsd,dhce->bshce', attn_in, w_qkv, preferred_element_type=jnp.float32).astype(jnp.bfloat16)
    attn_out, attn_prob, prob_lo = attention_fwd(qkv_vals, attn_mask, attn_scale)
    attn_part = jnp.einsum('bshe,hed->bsd', attn_out, w_out, preferred_element_type=jnp.float32).astype(jnp.bfloat16)
    attn_sum = lax.psum_scatter(attn_part, 'model', scatter_dimension=1, tiled=True)
    mid_loc = (x_f32 + attn_sum.astype(jnp.float32)).astype(jnp.bfloat16)
    ln2_out, ln2_vjp = jax.vjp(layer_norm, mid_loc.astype(jnp.float32), gain_mlp.astype(jnp.float32))
    mlp_in = lax.all_gather(ln2_out.astype(jnp.bfloat16), 'model', axis=1, tiled=True)
    pre_act = jnp.einsum('bsd,df->bsf', mlp_in, w_up, preferred_element_type=jnp.float32)
    act_f32, gelu_vjp = jax.vjp(gelu_tanh, pre_act)
    act_lo = act_f32.astype(jnp.bfloat16)
    mlp_part = jnp.einsum('bsf,fd->bsd', act_lo, w_down, preferred_element_type=jnp.float32).astype(jnp.bfloat16)
    mlp_sum = lax.psum_scatter(mlp_part, 'model', scatter_dimension=1, tiled=True)
    hidden_out = (mid_loc.astype(jnp.float32) + mlp_sum.astype(jnp.float32)).astype(jnp.bfloat16)
    grad_full = lax.all_gather(grad_out, 'model', axis=1, tiled=True)
    d_act = jnp.einsum('bsd,fd->bsf', grad_full, w_down, preferred_element_type=jnp.float32)
    d_pre = gelu_vjp(d_act)[0].astype(jnp.bfloat16)
    g_down = jnp.einsum('bsf,bsd->fd', act_lo, grad_full, preferred_element_type=jnp.float32).astype(jnp.bfloat16)
    d_mlp_part = jnp.einsum('bsf,df->bsd', d_pre, w_up, preferred_element_type=jnp.float32).astype(jnp.bfloat16)
    g_up = jnp.einsum('bsd,bsf->df', mlp_in, d_pre, preferred_element_type=jnp.float32).astype(jnp.bfloat16)
    d_mlp_in = lax.psum_scatter(d_mlp_part, 'model', scatter_dimension=1, tiled=True)
    d_mid_ln, d_gain_mlp = ln2_vjp(d_mlp_in.astype(jnp.float32))
    d_mid = (grad_out.astype(jnp.float32) + d_mid_ln).astype(jnp.bfloat16)
    d_mid_full = lax.all_gather(d_mid, 'model', axis=1, tiled=True)
    d_attn_out = jnp.einsum('bsd,hed->bshe', d_mid_full, w_out, preferred_element_type=jnp.float32).astype(jnp.bfloat16)
    g_out = jnp.einsum('bshe,bsd->hed', attn_out, d_mid_full, preferred_element_type=jnp.float32).astype(jnp.bfloat16)
    d_qkv = attention_bwd(qkv_vals, attn_out, d_attn_out, attn_prob, prob_lo, attn_scale)
    g_qkv = jnp.einsum('bsd,bshce->dhce', attn_in, d_qkv, preferred_element_type=jnp.float32).astype(jnp.bfloat16)
    d_attn_part = jnp.einsum('bshce,dhce->bsd', d_qkv, w_qkv, preferred_element_type=jnp.float32).astype(jnp.bfloat16)
    d_attn_in = lax.psum_scatter(d_attn_part, 'model', scatter_dimension=1, tiled=True)
    d_x_ln, d_gain_attn = ln1_vjp(d_attn_in.astype(jnp.float32))
    grad_in = (d_mid.astype(jnp.float32) + d_x_ln).astype(jnp.bfloat16)
    gain_sums = lax.psum(jnp.stack([d_gain_attn, d_gain_mlp]), 'model')
    return (hidden_out, grad_in, g_qkv, g_out, g_up, g_down, gain_sums[0].astype(jnp.bfloat16), gain_sums[1].astype(jnp.bfloat16))


def solution(mesh):
    act_spec = P('data', 'model', None)
    in_specs = (act_spec, P('data', None), P(), P(None, 'model', None, None), P('model', None, None), P(), P(None, 'model'), P('model', None), act_spec)
    out_specs = (act_spec, act_spec, P('data', 'model', None, None), P(('data', 'model'), None, None), P('data', 'model'), P(('data', 'model'), None), P('data'), P('data'))
    return jax.shard_map(local_layer, mesh=mesh, in_specs=in_specs, out_specs=out_specs, check_vma=False)
```

profile of v0, /device:TPU:81, one launch (start us, length us, event | category | flops | bytes accessed | tf_op | source)
XLA Modules:
  0.0 808.7 jit_solution(2339625192828433761)
XLA Ops:
  7.2 0.1 all-gather.5.cloned.1.call-start
  7.3 1.7 convert_reduce_fusion.1
  9.0 1.8 fusion.59
  10.8 0.6 copy-done.21
  11.4 0.7 convert_element_type.156
  12.1 0.6 copy-done.11
  12.7 2.8 fusion.56
  15.5 0.1 all-gather.5.cloned.1.call-update
  15.6 0.1 reduce-scatter.5.cloned.1.call-start
  15.7 5.4 fusion.6
  21.1 54.5 %all-gather.5.cloned.1.call-done = bf16[1,2048,2560]{2,1,0:T(8,128)(2,1)} async-done(((bf16[1,256,2560]{2,1,0:T(8,128)(2,1)}), bf16[1,2048,2560]{2,1,0:T(8,128)(2,1)}) %all-gather.5.cloned.1.call-update) | async-done | bytes 10485776 | tf_op jit(solution)/shard_map/all_gather | solution.py:51
  75.6 14.5 %fusion.26 = f32[2048,960]{0,1:S(1)} fusion(bf16[2560,960]{0,1:T(8,128)(2,1)} %bitcast.140, bf16[1,2048,2560]{2,1,0:T(8,128)(2,1)} %all-gather.5.cloned.1.call-done), kind=kOutput, calls=%fused_computation.39 | convolution fusion | flops 10066329600 | bytes 23265280
  90.1 2.5 convert_bitcast_fusion
  92.6 36.3 %fusion.79 = (f32[4,2048]{1,0:T(4,128)S(1)}, f32[4,2048,2048]{1,2,0:T(8,128)}) fusion(pred[2048,2048]{0,1:T(8,128)(4,1)} %fusion.6, bf16[1,2048,4,3,80]{1,4,3,2,0:T(8,128)(2,1)} %convert_bitcast_fusion), kind=kOutput, calls=%fused_computation.120 | convolution fusion | flops 2751465472 | bytes 73957376 | tf_op jit(solution)/shard_map/sub | solution.py:25
  129.0 33.2 %fusion.5 = bf16[4,2048,2048]{1,2,0:T(8,128)(2,1)} fusion(f32[4,2048,2048]{1,2,0:T(8,128)} %get-tuple-element.19, f32[4,2048]{1,0:T(4,128)S(1)} %get-tuple-element.18), kind=kLoop, calls=%fused_computation.9 | loop fusion | flops 33554432 | bytes 100696064 | tf_op jit(solution)/shard_map/convert_element_type | solution.py:26
  162.2 16.8 %convolution_convert_fusion.7 = bf16[4,80,2048]{2,1,0:T(8,128)(2,1)S(1)} fusion(bf16[4,2048,2048]{1,2,0:T(8,128)(2,1)} %fusion.5, bf16[1,2048,4,3,80]{1,4,3,2,0:T(8,128)(2,1)} %convert_bitcast_fusion), kind=kOutput, calls=%fused_computation.78 | convolution fusion | flops 2685009920 | bytes 36175872 | tf_op jit(solution)/shard_map/bhqk,bkhe->bqhe/dot_general | solution.py:27
  179.0 1.1 copy-done.6
  180.1 8.2 %fusion.33 = bf16[1,2048,2560]{2,1,0:T(8,128)(2,1)} fusion(bf16[4,80,2560]{2,1,0:T(8,128)(2,1)S(1)} %copy-done, bf16[4,80,2048]{2,1,0:T(8,128)(2,1)S(1)} %convolution_convert_fusion.7), kind=kOutput, calls=%fused_computation.45 | convolution fusion | flops 3360686080 | bytes 13434880 | tf_op jit(solution)/shard_map/bshe,hed->bsd/dot_general | solution.py:54
  188.3 0.1 reduce-scatter.5.cloned.1.call-update
  188.4 0.1 all-gather.7.cloned.1.call-start
  188.5 0.6 copy-done.23
  189.0 58.4 %reduce-scatter.5.cloned.1.call-done = bf16[1,256,2560]{2,1,0:T(8,128)(2,1)} async-done(((bf16[1,2048,2560]{2,1,0:T(8,128)(2,1)}), bf16[1,256,2560]{2,1,0:T(8,128)(2,1)}) %reduce-scatter.5.cloned.1.call-update) | async-done | bytes 1310736 | tf_op jit(solution)/shard_map/reduce_scatter | solution.py:55
  247.4 1.8 convert_reduce_fusion
  249.2 0.5 fusion.62
  249.7 0.5 copy-done.4
  250.2 1.5 fusion.55
  251.8 0.1 all-gather.9.cloned.1.call-start
  251.9 0.6 all-gather.9.cloned.1.call-update
  252.4 0.1 reduce-scatter.9.cloned.1.call-start
  252.5 55.3 %all-gather.7.cloned.1.call-done = bf16[1,2048,2560]{2,1,0:T(8,128)(2,1)} async-done(((bf16[1,256,2560]{2,1,0:T(8,128)(2,1)}), bf16[1,2048,2560]{2,1,0:T(8,128)(2,1)}) %all-gather.7.cloned.1.call-update) | async-done | bytes 10485776 | tf_op jit(solution)/shard_map/all_gather | solution.py:58
  307.8 19.5 %fusion.22 = f32[2048,1280]{1,0:T(8,128)} fusion(bf16[2560,1280]{1,0:T(8,128)(2,1)} %param.15, bf16[1,2048,2560]{2,1,0:T(8,128)(2,1)} %all-gather.7.cloned.1.call-done), kind=kOutput, calls=%fused_computation.35 | convolution fusion | flops 13421772800 | bytes 27525120 | tf_op jit(solution)/shard_map/bsd,df->bsf/dot_general | solution.py:59
  327.3 37.6 %all-gather.9.cloned.1.call-done = bf16[1,2048,2560]{2,1,0:T(8,128)(2,1)} async-done(((bf16[1,256,2560]{2,1,0:T(8,128)(2,1)}), bf16[1,2048,2560]{2,1,0:T(8,128)(2,1)}) %all-gather.9.cloned.1.call-update) | async-done | bytes 10485776 | tf_op jit(solution)/shard_map/all_gather | solution.py:65
  364.9 26.0 %fusion.13 = bf16[2048,1280]{1,0:T(8,128)(2,1)} fusion(f32[2048,1280]{1,0:T(8,128)} %fusion.22, bf16[1280,2560]{1,0:T(8,128)(2,1)} %param.16, bf16[1,2048,2560]{2,1,0:T(8,128)(2,1)} %all-gather.9.cloned.1.call-done), kind=kOutput, calls=%fused_computation.26 | convolution fusion | flops 13474201600 | bytes 32768000 | tf_op jit(solution)/shard_map/bsd,fd->bsf/dot_general | solution.py:66
  390.9 20.1 %fusion.31 = bf16[1,2048,2560]{2,1,0:T(8,128)(2,1)} fusion(bf16[2048,1280]{1,0:T(8,128)(2,1)} %fusion.13, bf16[2560,1280]{1,0:T(8,128)(2,1)} %param.15), kind=kOutput, calls=%fused_computation.43 | convolution fusion | flops 13427015680 | bytes 22282240 | tf_op jit(solution)/shard_map/bsf,df->bsd/dot_general | solution.py:69
  411.1 0.1 reduce-scatter.7.cloned.1.call-start
  411.1 21.2 %fusion.30 = bf16[1,2048,2560]{2,1,0:T(8,128)(2,1)} fusion(bf16[1280,2560]{1,0:T(8,128)(2,1)} %param.16, f32[2048,1280]{1,0:T(8,128)} %fusion.22), kind=kOutput, calls=%fused_computation.42 | convolution fusion | flops 13450608640 | bytes 27525120 | tf_op jit(solution)/shard_map/bsf,fd->bsd/dot_general | solution.py:62
  432.4 0.3 all-gather.11.cloned.1.call-start
  432.8 37.3 %reduce-scatter.9.cloned.1.call-done = bf16[1,256,2560]{2,1,0:T(8,128)(2,1)} async-done(((bf16[1,2048,2560]{2,1,0:T(8,128)(2,1)}), bf16[1,256,2560]{2,1,0:T(8,128)(2,1)}) %reduce-scatter.9.cloned.1.call-update) | async-done | bytes 1310736 | tf_op jit(solution)/shard_map/reduce_scatter | solution.py:71
  470.1 2.0 fusion.63
  472.0 3.2 fusion.57
  475.2 56.1 %reduce-scatter.7.cloned.1.call-done = bf16[1,256,2560]{2,1,0:T(8,128)(2,1)} async-done(((bf16[1,2048,2560]{2,1,0:T(8,128)(2,1)}), bf16[1,256,2560]{2,1,0:T(8,128)(2,1)}) %reduce-scatter.7.cloned.1.call-update) | async-done | bytes 1310736 | tf_op jit(solution)/shard_map/reduce_scatter | solution.py:63
  531.3 4.9 add_convert_fusion.1
  536.2 0.1 all-gather.11.cloned.1.call-update
  536.3 0.1 reduce-scatter.11.cloned.1.call-start
  536.4 55.9 %all-gather.11.cloned.1.call-done = bf16[1,2048,2560]{2,1,0:T(8,128)(2,1)} async-done(((bf16[1,256,2560]{2,1,0:T(8,128)(2,1)}), bf16[1,2048,2560]{2,1,0:T(8,128)(2,1)}) %all-gather.11.cloned.1.call-update) | async-done | bytes 10485776 | tf_op jit(solution)/shard_map/all_gather | solution.py:74
  592.3 7.9 fusion.65
  600.2 16.5 %fusion.68 = bf16[1,2048,4,1,80]{1,4,2,3,0:T(8,128)(2,1)} fusion(bf16[2048,4,80]{0,2,1:T(8,128)(2,1)S(1)} %get-tuple-element.21, bf16[4,2048,2048]{1,2,0:T(8,128)(2,1)} %fusion.5), kind=kOutput, calls=%fused_computation.96 | convolution fusion | flops 2685009920 | bytes 36175872 | tf_op jit(solution)/shard_map/bhqk,bqhe->bkhe/dot_general | solution.py:40
  616.7 34.7 %multiply_convert_fusion = bf16[4,2048,2048]{1,2,0:T(8,128)(2,1)} fusion(bf16[2048,4,80]{0,2,1:T(8,128)(2,1)S(1)} %get-tuple-element.21, f32[4,2048]{1,0:T(4,128)S(1)} %get-tuple-element.20, f32[4,2048,2048]{1,2,0:T(8,128)} %get-tuple-element.19, f32[4,2048]{1,0:T(4,128)S(1)} %copy-done.17, bf16[1,2048,4,3,80]{1,4,3,2,0:T(8,128)(2,1)} %convert_bitcast_fusion), kind=kOutput, calls=%fused_computation.1 | convolution fusion | flops 2768240640 | bytes 103350272 | tf_op jit(solution)/shard_map/bqhe,bkhe->bhqk/dot_general | solution.py:35
  651.4 16.8 %fusion.67 = bf16[1,2048,4,1,80]{1,4,2,3,0:T(8,128)(2,1)S(1)} fusion(bf16[4,2048,2048]{1,2,0:T(8,128)(2,1)} %multiply_convert_fusion, bf16[1,2048,4,3,80]{1,4,3,2,0:T(8,128)(2,1)} %convert_bitcast_fusion), kind=kOutput, calls=%fused_computation.95 | convolution fusion | flops 2685009920 | bytes 36175872 | tf_op jit(solution)/shard_map/bhqk,bqhe->bkhe/dot_general | solution.py:39
  668.2 16.9 %fusion.66 = bf16[1,2048,4,1,80]{1,4,2,3,0:T(8,128)(2,1)S(1)} fusion(bf16[4,2048,2048]{1,2,0:T(8,128)(2,1)} %multiply_convert_fusion, bf16[1,2048,4,3,80]{1,4,3,2,0:T(8,128)(2,1)} %convert_bitcast_fusion), kind=kOutput, calls=%fused_computation.94 | convolution fusion | flops 2685009920 | bytes 36175872 | tf_op jit(solution)/shard_map/bhqk,bkhe->bqhe/dot_general | solution.py:38
  685.1 1.1 copy-done.9
  686.2 15.9 %fusion.32 = bf16[1,2048,2560]{2,1,0:T(8,128)(2,1)} fusion(bf16[2560,4,3,80]{0,3,2,1:T(8,128)(2,1)} %param.12, bf16[1,2048,4,1,80]{1,4,2,3,0:T(8,128)(2,1)S(1)} %copy-done.8, bf16[1,2048,4,1,80]{1,4,2,3,0:T(8,128)(2,1)S(1)} %fusion.67, bf16[1,2048,4,1,80]{1,4,2,3,0:T(8,128)(2,1)S(1)} %fusion.66), kind=kOutput, calls=%fused_computation.44 | convolution fusion | flops 10075504640 | bytes 19333120 | tf_op jit(solution)/shard_map/bshce,dhce->bsd/dot_general | solution.py:79
  702.2 22.7 %convolution_convert_fusion.2 = bf16[1280,2560]{1,0:T(8,128)(2,1)} fusion(bf16[1,2048,2560]{2,1,0:T(8,128)(2,1)} %all-gather.9.cloned.1.call-done, f32[2048,1280]{1,0:T(8,128)} %fusion.22), kind=kOutput, calls=%fused_computation.18 | convolution fusion | flops 13448642560 | bytes 27525120 | tf_op jit(solution)/shard_map/bsf,bsd->fd/dot_general | solution.py:68
  724.8 20.2 %convolution_convert_fusion.3 = bf16[2560,1280]{1,0:T(8,128)(2,1)} fusion(bf16[2048,1280]{1,0:T(8,128)(2,1)} %fusion.13, bf16[1,2048,2560]{2,1,0:T(8,128)(2,1)} %all-gather.7.cloned.1.call-done), kind=kOutput, calls=%fused_computation.19 | convolution fusion | flops 13425049600 | bytes 22282240 | tf_op jit(solution)/shard_map/bsd,bsf->df/dot_general | solution.py:70
  745.1 0.5 maximum_bitcast_fusion
  745.5 0.5 copy.23
  746.1 13.3 %fusion.24 = f32[2560,960]{0,1:S(1)} fusion(bf16[2048,960]{0,1:T(8,128)(2,1)S(1)} %bitcast.138, bf16[1,2048,2560]{2,1,0:T(8,128)(2,1)} %all-gather.5.cloned.1.call-done), kind=kOutput, calls=%fused_computation.37 | convolution fusion | flops 10066329600 | bytes 24248320
  759.4 3.0 convert_element_type.198
  762.4 8.7 %fusion.37 = bf16[4,80,2560]{2,1,0:T(8,128)(2,1)} fusion(bf16[1,2048,2560]{2,1,0:T(8,128)(2,1)} %all-gather.11.cloned.1.call-done, bf16[4,80,2048]{2,1,0:T(8,128)(2,1)S(1)} %copy-done.7), kind=kOutput, calls=%fused_computation.48 | convolution fusion | flops 3356262400 | bytes 13434880 | tf_op jit(solution)/shard_map/bshe,bsd->hed/dot_general | solution.py:76
  771.1 2.0 fusion.60
  773.1 2.7 fusion.58
  775.9 21.0 %psum.7 = bf16[2,2560]{1,0:T(2,128)(2,1)S(1)} all-reduce(f32[2,2560]{1,0:T(2,128)S(1)} %pad_maximum_fusion), channel_id=1, replica_groups=mesh['data'=4,'model'=8] {'model'}, use_global_device_ids=true, to_apply=%region_16.17 | all-reduce | flops 5120 | bytes 30720 | tf_op jit(solution)/shard_map/psum | solution.py:83
  796.9 0.7 slice_reduce_fusion
  797.5 3.9 add_convert_fusion
  (59 shorter events, 0.4 us)
Async XLA Ops:
  7.2 172.9 %copy-start = (bf16[4,80,2560]{2,1,0:T(8,128)(2,1)S(1)}, bf16[4,80,2560]{2,1,0:T(8,128)(2,1)}, u32[]{:S(2)}) copy-start(bf16[4,80,2560]{2,1,0:T(8,128)(2,1)} %param.13) | copy-start | bytes 4915204
  7.2 8.5 %copy-start.18 = (s32[1,2048]{1,0:T(1,128)S(1)}, s32[1,2048]{1,0:T(1,128)}, u32[]{:S(2)}) copy-start(s32[1,2048]{1,0:T(1,128)} %param.10) | copy-start | bytes 24580
  7.2 68.4 %all-gather.5.cloned.1.call-start = ((), (), s32[]{:S(2)}) async-start(), calls=%async_computation.4 | async-start | bytes 11796480 | tf_op jit(solution)/shard_map/all_gather | solution.py:51
  9.0 3.1 copy-start.14
  10.8 0.6 copy-start.21
  11.4 0.7 copy-start.19
  12.1 0.6 copy-start.11
  15.6 231.8 %reduce-scatter.5.cloned.1.call-start = ((), (), s32[]{:S(2)}) async-start(), calls=%async_computation.5 | async-start | bytes 11796480 | tf_op jit(solution)/shard_map/reduce_scatter | solution.py:55
  128.9 33.2 %copy-start.16 = (f32[4,2048]{1,0:T(4,128)}, f32[4,2048]{1,0:T(4,128)S(1)}, u32[]{:S(2)}) copy-start(f32[4,2048]{1,0:T(4,128)S(1)} %get-tuple-element.18) | copy-start | bytes 98308
  179.0 1.1 copy-start.6
  188.3 0.7 copy-start.23
  188.3 59.1 %copy-start.2 = (bf16[1,256,2560]{2,1,0:T(8,128)(2,1)S(1)}, bf16[1,256,2560]{2,1,0:T(8,128)(2,1)}, u32[]{:S(2)}) copy-start(bf16[1,256,2560]{2,1,0:T(8,128)(2,1)} %param.9) | copy-start | bytes 3932164
  188.4 119.4 %all-gather.7.cloned.1.call-start = ((), (), s32[]{:S(2)}) async-start(), calls=%async_computation.6 | async-start | bytes 11796480 | tf_op jit(solution)/shard_map/all_gather | solution.py:58
  249.2 1.1 copy-start.4
  251.8 113.1 %all-gather.9.cloned.1.call-start = ((), (), s32[]{:S(2)}) async-start(), calls=%async_computation.8 | async-start | bytes 11796480 | tf_op jit(solution)/shard_map/all_gather | solution.py:65
  252.4 217.6 %reduce-scatter.9.cloned.1.call-start = ((), (), s32[]{:S(2)}) async-start(), calls=%async_computation.9 | async-start | bytes 11796480 | tf_op jit(solution)/shard_map/reduce_scatter | solution.py:71
  411.1 120.2 %reduce-scatter.7.cloned.1.call-start = ((), (), s32[]{:S(2)}) async-start(), calls=%async_computation.7 | async-start | bytes 11796480 | tf_op jit(solution)/shard_map/reduce_scatter | solution.py:63
  432.4 37.7 %copy-start.5 = (bf16[1,256,2560]{2,1,0:T(8,128)(2,1)S(1)}, bf16[1,256,2560]{2,1,0:T(8,128)(2,1)}, u32[]{:S(2)}) copy-start(bf16[1,256,2560]{2,1,0:T(8,128)(2,1)} %copy-done.4) | copy-start | bytes 3932164
  432.4 159.9 %all-gather.11.cloned.1.call-start = ((), (), s32[]{:S(2)}) async-start(), calls=%async_computation.10 | async-start | bytes 11796480 | tf_op jit(solution)/shard_map/all_gather | solution.py:74
  536.3 234.8 %reduce-scatter.11.cloned.1.call-start = ((), (), s32[]{:S(2)}) async-start(), calls=%async_computation.11 | async-start | bytes 11796480 | tf_op jit(solution)/shard_map/reduce_scatter | solution.py:80
  600.2 16.5 %copy-start.17 = (f32[4,2048]{1,0:T(4,128)S(1)}, f32[4,2048]{1,0:T(4,128)}, u32[]{:S(2)}) copy-start(f32[4,2048]{1,0:T(4,128)} %copy-done.16) | copy-start | bytes 98308
  668.2 18.0 %copy-start.8 = (bf16[1,2048,4,1,80]{1,4,2,3,0:T(8,128)(2,1)S(1)}, bf16[1,2048,4,1,80]{1,4,2,3,0:T(8,128)(2,1)}, u32[]{:S(2)}) copy-start(bf16[1,2048,4,1,80]{1,4,2,3,0:T(8,128)(2,1)} %fusion.68) | copy-start | bytes 3932164
  685.1 1.1 copy-start.9
  724.8 20.2 %copy-start.13 = (f32[2560]{0:T(1024)S(1)}, f32[2560]{0:T(1024)}, u32[]{:S(2)}) copy-start(f32[2560]{0:T(1024)} %get-tuple-element.10) | copy-start | bytes 30724
  724.8 20.2 %copy-start.10 = (bf16[1,2048,4,1,80]{1,4,2,3,0:T(8,128)(2,1)S(1)}, bf16[1,2048,4,1,80]{1,4,2,3,0:T(8,128)(2,1)}, u32[]{:S(2)}) copy-start(bf16[1,2048,4,1,80]{1,4,2,3,0:T(8,128)(2,1)} %copy-done.9) | copy-start | bytes 3932164
  759.4 3.0 copy-start.7
  762.3 8.8 %copy-start.3 = (bf16[1,256,2560]{2,1,0:T(8,128)(2,1)S(1)}, bf16[1,256,2560]{2,1,0:T(8,128)(2,1)}, u32[]{:S(2)}) copy-start(bf16[1,256,2560]{2,1,0:T(8,128)(2,1)} %param.9) | copy-start | bytes 3932164
  762.3 8.8 %copy-start.12 = (f32[2560]{0:T(1024)S(1)}, f32[2560]{0:T(1024)}, u32[]{:S(2)}) copy-start(f32[2560]{0:T(1024)} %copy-done.11) | copy-start | bytes 30724
  762.3 8.8 %copy-start.15 = (f32[256]{0:T(256)S(1)}, f32[256]{0:T(256)}, u32[]{:S(2)}) copy-start(f32[256]{0:T(256)} %copy-done.14) | copy-start | bytes 3076
  762.3 10.7 %copy-start.22 = (f32[256]{0:T(256)S(1)}, f32[256]{0:T(256)}, u32[]{:S(2)}) copy-start(f32[256]{0:T(256)} %copy-done.21) | copy-start | bytes 3076
  762.3 10.8 %copy-start.20 = (f32[256]{0:T(256)S(1)}, f32[256]{0:T(256)}, u32[]{:S(2)}) copy-start(f32[256]{0:T(256)} %copy-done.19) | copy-start | bytes 3076
  773.1 28.3 %copy-start.1 = (bf16[4,80,2560]{2,1,0:T(8,128)(2,1)S(1)}, bf16[4,80,2560]{2,1,0:T(8,128)(2,1)}, u32[]{:S(2)}) copy-start(bf16[4,80,2560]{2,1,0:T(8,128)(2,1)} %param.13) | copy-start | bytes 4915204
Sparse Core Ops, SparseCore 0:
  15.7 59.8 all-gather.4
  188.5 58.8 reduce-scatter.4
  251.9 55.8 all-gather.6
  309.2 55.6 all-gather.8
  411.2 58.8 reduce-scatter.8
  472.2 59.0 reduce-scatter.6
  536.4 55.8 all-gather.10
  702.3 58.8 reduce-scatter.10
where the time goes:
time: 820 us; the launch traced here: 809 us
  waiting for transfers between devices  356 us (43%)
  matrix products  336 us (41%)
  other arithmetic  74.1 us (9%)
  blocking collectives  21 us (3%)
  between operations  14.9 us (2%)
    reduce_scatter x1, waiting for transfers between devices, local_layer(): lax.psum_scatter(attn_part, 'model', scatter_dimension=1, tiled=True)  58.4 us
    reduce_scatter x1, waiting for transfers between devices, local_layer(): lax.psum_scatter(mlp_part, 'model', scatter_dimension=1, tiled=True)  56.1 us
    all_gather x1, waiting for transfers between devices, local_layer(): d_mid_full = lax.all_gather(d_mid, 'model', axis=1, tiled=True)  55.9 us
    all_gather x1, waiting for transfers between devices, local_layer(): lax.all_gather(ln2_out.astype(jnp.bfloat16), 'model', axis=1, tiled=True)  55.3 us
    all_gather x1, waiting for transfers between devices, local_layer(): lax.all_gather(ln1_out.astype(jnp.bfloat16), 'model', axis=1, tiled=True)  54.5 us
    all_gather x1, waiting for transfers between devices, local_layer(): grad_full = lax.all_gather(grad_out, 'model', axis=1, tiled=True)  37.6 us
    reduce_scatter x1, waiting for transfers between devices, local_layer(): lax.psum_scatter(d_mlp_part, 'model', scatter_dimension=1, tiled=True)  37.3 us
    sub x1, matrix products, attention_fwd(): jax.nn.softmax(jnp.where(attn_mask[:, None], scores, -1e+30), axis=-1)  36.3 us
  transfers between devices with their start and end apart: 8, of which 7 were waited for; matrix products, arithmetic and copies ran while one was open for 15% of the time, Pallas kernels for 0%

commit v1 on v0

v1 whole, which is shorter than its diff:
```python
import functools

import jax
import jax.numpy as jnp
from jax import lax
from jax.experimental import pallas as pl
from jax.experimental.pallas import tpu as pltpu
from jax.sharding import PartitionSpec as P

LN_EPS = 1e-5
BLK = 256
NT = (((1,), (1,)), ((), ()))


def layer_norm(x_f32, gain_f32):
    mean_val = jnp.mean(x_f32, axis=-1, keepdims=True)
    centered = x_f32 - mean_val
    variance = jnp.mean(centered * centered, axis=-1, keepdims=True)
    return centered * lax.rsqrt(variance + LN_EPS) * gain_f32


def gelu_tanh(pre_act):
    return jax.nn.gelu(pre_act, approximate=True)


def dot32(a, b):
    return jnp.dot(a, b, preferred_element_type=jnp.float32)


def visible(j, i, first_row):
    kpos = j * BLK + lax.broadcasted_iota(jnp.int32, (BLK, BLK), 0)
    qpos = i * BLK + lax.broadcasted_iota(jnp.int32, (BLK, BLK), 1)
    return (kpos <= qpos) & (kpos >= first_row)


def attn_fwd_kernel(heads, hd, lo_ref, qkv_ref, first_ref, o_ref, lse_ref, k_s, s_s, o_s):
    i = pl.program_id(0)
    scale = hd ** -0.5

    @pl.when(i == 0)
    def _():
        for h in range(heads):
            for j in range(k_s.shape[1] // BLK):
                kt = qkv_ref[(3 * h + 1) * hd:(3 * h + 2) * hd, j * BLK:(j + 1) * BLK]
                k_s[h, j * BLK:(j + 1) * BLK, :] = kt.T

    lo = lo_ref[i]
    cols = pl.ds(pl.multiple_of(i * BLK, BLK), BLK)
    first_row = first_ref[0:1, cols]
    neg = jnp.full((8, BLK), -jnp.inf, jnp.float32)

    def scores(j, m):
        rows = pl.ds(pl.multiple_of(j * BLK, BLK), BLK)
        mask = visible(j, i, first_row)
        out = []
        for h in range(heads):
            s = dot32(k_s[h, rows, :], qkv_ref[3 * h * hd:(3 * h + 1) * hd, cols]) * scale
            s = jnp.where(mask, s, -1e30)
            s_s[h, rows, :] = s
            out.append(jnp.maximum(m[h], jnp.max(s.reshape(BLK // 8, 8, BLK), axis=0)))
        return tuple(out)

    m = lax.fori_loop(lo, i + 1, scores, (neg,) * heads)
    m = [jnp.max(x, axis=0, keepdims=True) for x in m]

    def expo(j, l):
        rows = pl.ds(pl.multiple_of(j * BLK, BLK), BLK)
        out = []
        for h in range(heads):
            e = jnp.exp(s_s[h, rows, :] - m[h])
            s_s[h, rows, :] = e
            out.append(l[h] + jnp.sum(e.reshape(BLK // 8, 8, BLK), axis=0))
        return tuple(out)

    l = lax.fori_loop(lo, i + 1, expo, (jnp.zeros((8, BLK), jnp.float32),) * heads)
    l = [jnp.sum(x, axis=0, keepdims=True) for x in l]
    r = [1.0 / x for x in l]
    for h in range(heads):
        lse_ref[h:h + 1, :] = m[h] + jnp.log(l[h])
        o_s[h] = jnp.zeros((hd, BLK), jnp.float32)

    def values(j, c):
        rows = pl.ds(pl.multiple_of(j * BLK, BLK), BLK)
        for h in range(heads):
            pb = (s_s[h, rows, :] * r[h]).astype(jnp.bfloat16)
            o_s[h] += dot32(qkv_ref[(3 * h + 2) * hd:(3 * h + 3) * hd, rows], pb)
        return c

    lax.fori_loop(lo, i + 1, values, 0)
    for h in range(heads):
        o_ref[h * hd:(h + 1) * hd, :] = o_s[h].astype(jnp.bfloat16)


def attention_fwd(qkv_t, lo, first, heads, hd):
    seq = qkv_t.shape[1]
    nb = seq // BLK
    flops = 4 * heads * seq * seq * hd // 2
    return pl.pallas_call(
        functools.partial(attn_fwd_kernel, heads, hd),
        grid_spec=pltpu.PrefetchScalarGridSpec(
            num_scalar_prefetch=1, grid=(nb,),
            in_specs=[pl.BlockSpec(qkv_t.shape, lambda i, lo: (0, 0)),
                      pl.BlockSpec((1, seq), lambda i, lo: (0, 0))],
            out_specs=[pl.BlockSpec((heads * hd, BLK), lambda i, lo: (0, i)),
                       pl.BlockSpec((8, BLK), lambda i, lo: (0, i))],
            scratch_shapes=[pltpu.VMEM((heads, seq, hd), jnp.bfloat16),
                            pltpu.VMEM((heads, seq, BLK), jnp.float32),
                            pltpu.VMEM((heads, hd, BLK), jnp.float32)]),
        out_shape=[jax.ShapeDtypeStruct((heads * hd, seq), jnp.bfloat16),
                   jax.ShapeDtypeStruct((8, seq), jnp.float32)],
        compiler_params=pltpu.CompilerParams(vmem_limit_bytes=56 * 2 ** 20),
        cost_estimate=pl.CostEstimate(flops=8 * flops, bytes_accessed=2 * qkv_t.size, transcendentals=0),
        name="attn_fwd",
    )(lo, qkv_t, first)


def attn_bwd_kernel(heads, hd, lo_ref, qkv_ref, o_ref, do_ref, lse_ref, first_ref, d_ref,
                    k_s, v_s, dq_s, dk_s, dv_s):
    i = pl.program_id(0)
    seq = qkv_ref.shape[1]
    scale = hd ** -0.5

    @pl.when(i == 0)
    def _():
        dk_s[...] = jnp.zeros_like(dk_s)
        dv_s[...] = jnp.zeros_like(dv_s)
        for h in range(heads):
            for j in range(seq // BLK):
                c = slice(j * BLK, (j + 1) * BLK)
                k_s[h, c, :] = qkv_ref[(3 * h + 1) * hd:(3 * h + 2) * hd, c].T
                v_s[h, c, :] = qkv_ref[(3 * h + 2) * hd:(3 * h + 3) * hd, c].T

    lo = lo_ref[i]
    cols = pl.ds(pl.multiple_of(i * BLK, BLK), BLK)
    first_row = first_ref[0:1, cols]
    delta = []
    for h in range(heads):
        hs = slice(h * hd, (h + 1) * hd)
        delta.append(jnp.sum(do_ref[hs, :].astype(jnp.float32) * o_ref[hs, :].astype(jnp.float32), axis=0, keepdims=True))
        dq_s[h] = jnp.zeros((hd, BLK), jnp.float32)

    def step(j, c):
        rows = pl.ds(pl.multiple_of(j * BLK, BLK), BLK)
        mask = visible(j, i, first_row)
        for h in range(heads):
            q_t = qkv_ref[3 * h * hd:(3 * h + 1) * hd, cols]
            do_t = do_ref[h * hd:(h + 1) * hd, :]
            s = dot32(k_s[h, rows, :], q_t) * scale
            p = jnp.exp(jnp.where(mask, s, -1e30) - lse_ref[h:h + 1, :])
            dp = dot32(v_s[h, rows, :], do_t)
            ds = (p * (dp - delta[h]) * scale).astype(jnp.bfloat16)
            pb = p.astype(jnp.bfloat16)
            dq_s[h] += dot32(qkv_ref[(3 * h + 1) * hd:(3 * h + 2) * hd, rows], ds)
            dk_s[h, :, rows] += lax.dot_general(q_t, ds, NT, preferred_element_type=jnp.float32)
            dv_s[h, :, rows] += lax.dot_general(do_t, pb, NT, preferred_element_type=jnp.float32)
        return c

    lax.fori_loop(lo, i + 1, step, 0)
    for h in range(heads):
        d_ref[3 * h * hd:(3 * h + 1) * hd, cols] = dq_s[h].astype(jnp.bfloat16)

    @pl.when(i == pl.num_programs(0) - 1)
    def _():
        for h in range(heads):
            d_ref[(3 * h + 1) * hd:(3 * h + 2) * hd, :] = dk_s[h].astype(jnp.bfloat16)
            d_ref[(3 * h + 2) * hd:(3 * h + 3) * hd, :] = dv_s[h].astype(jnp.bfloat16)


def attention_bwd(qkv_t, o_t, do_t, lse, lo, first, heads, hd):
    seq = qkv_t.shape[1]
    nb = seq // BLK
    flops = 10 * heads * seq * seq * hd // 2
    blk = lambda rows: pl.BlockSpec((rows, BLK), lambda i, lo: (0, i))
    return pl.pallas_call(
        functools.partial(attn_bwd_kernel, heads, hd),
        grid_spec=pltpu.PrefetchScalarGridSpec(
            num_scalar_prefetch=1, grid=(nb,),
            in_specs=[pl.BlockSpec(qkv_t.shape, lambda i, lo: (0, 0)), blk(heads * hd), blk(heads * hd), blk(8),
                      pl.BlockSpec((1, seq), lambda i, lo: (0, 0))],
            out_specs=pl.BlockSpec(qkv_t.shape, lambda i, lo: (0, 0)),
            scratch_shapes=[pltpu.VMEM((heads, seq, hd), jnp.bfloat16),
                            pltpu.VMEM((heads, seq, hd), jnp.bfloat16),
                            pltpu.VMEM((heads, hd, BLK), jnp.float32),
                            pltpu.VMEM((heads, hd, seq), jnp.float32),
                            pltpu.VMEM((heads, hd, seq), jnp.float32)]),
        out_shape=jax.ShapeDtypeStruct(qkv_t.shape, jnp.bfloat16),
        compiler_params=pltpu.CompilerParams(vmem_limit_bytes=56 * 2 ** 20),
        cost_estimate=pl.CostEstimate(flops=8 * flops, bytes_accessed=4 * qkv_t.size, transcendentals=0),
        name="attn_bwd",
    )(lo, qkv_t, o_t, do_t, lse, first)


def group_sum(vals, n):
    total = vals
    for shift in range(1, n):
        total = total + lax.ppermute(vals, 'model', [(a, (a + shift) % n) for a in range(n)])
    return total


def local_layer(n, hidden_in, seg_ids, gain_attn, w_qkv, w_out, gain_mlp, w_up, w_down, grad_out):
    heads, hd, hidden = w_out.shape
    seq_len = seg_ids.shape[1]
    x_f32 = hidden_in[0].astype(jnp.float32)
    dy = grad_out[0]
    wq_t = jnp.transpose(w_qkv, (1, 2, 3, 0)).reshape(heads * 3 * hd, hidden)
    wo = w_out.reshape(heads * hd, hidden)
    first = jnp.sum(seg_ids[0][:, None] < seg_ids[0][None, :], axis=0, dtype=jnp.int32)
    lo = first[::BLK] // BLK
    first = first[None]
    ein = functools.partial(jnp.einsum, preferred_element_type=jnp.float32)
    gather = lambda a: lax.all_gather(a, 'model', axis=0, tiled=True)
    scatter = lambda a: lax.psum_scatter(a, 'model', scatter_dimension=0, tiled=True)

    ln1_out, ln1_vjp = jax.vjp(layer_norm, x_f32, gain_attn.astype(jnp.float32))
    attn_in = gather(ln1_out.astype(jnp.bfloat16))
    qkv_t = ein('nd,sd->ns', wq_t, attn_in).astype(jnp.bfloat16)
    o_t, lse = attention_fwd(qkv_t, lo, first, heads, hd)
    attn_sum = scatter(ein('es,ed->sd', o_t, wo).astype(jnp.bfloat16))
    mid_loc = (x_f32 + attn_sum.astype(jnp.float32)).astype(jnp.bfloat16)
    ln2_out, ln2_vjp = jax.vjp(layer_norm, mid_loc.astype(jnp.float32), gain_mlp.astype(jnp.float32))
    mlp_in = gather(ln2_out.astype(jnp.bfloat16))
    pre_act = ein('sd,df->sf', mlp_in, w_up)
    act_f32, gelu_vjp = jax.vjp(gelu_tanh, pre_act)
    act_lo = act_f32.astype(jnp.bfloat16)
    grad_full = gather(dy)
    d_act = ein('sd,fd->sf', grad_full, w_down)
    d_pre = gelu_vjp(d_act)[0].astype(jnp.bfloat16)
    d_mlp_in = scatter(ein('sf,df->sd', d_pre, w_up).astype(jnp.bfloat16))
    mlp_sum = scatter(ein('sf,fd->sd', act_lo, w_down).astype(jnp.bfloat16))
    hidden_out = (mid_loc.astype(jnp.float32) + mlp_sum.astype(jnp.float32)).astype(jnp.bfloat16)
    g_down = ein('sf,sd->fd', act_lo, grad_full).astype(jnp.bfloat16)
    g_up = ein('sd,sf->df', mlp_in, d_pre).astype(jnp.bfloat16)
    d_mid_ln, d_gain_mlp = ln2_vjp(d_mlp_in.astype(jnp.float32))
    d_mid = (dy.astype(jnp.float32) + d_mid_ln).astype(jnp.bfloat16)
    d_mid_full = gather(d_mid)
    do_t = ein('ed,sd->es', wo, d_mid_full).astype(jnp.bfloat16)
    g_out = ein('es,sd->ed', o_t, d_mid_full).astype(jnp.bfloat16)
    dqkv_t = attention_bwd(qkv_t, o_t, do_t, lse, lo, first, heads, hd)
    d_attn_in = scatter(ein('ns,nd->sd', dqkv_t, wq_t).astype(jnp.bfloat16))
    g_qkv = ein('ns,sd->nd', dqkv_t, attn_in).astype(jnp.bfloat16)
    d_x_ln, d_gain_attn = ln1_vjp(d_attn_in.astype(jnp.float32))
    grad_in = (d_mid.astype(jnp.float32) + d_x_ln).astype(jnp.bfloat16)
    gain_sums = group_sum(jnp.stack([d_gain_attn, d_gain_mlp]), n).astype(jnp.bfloat16)
    g_qkv = jnp.transpose(g_qkv.reshape(heads, 3, hd, hidden), (3, 0, 1, 2))
    return (hidden_out[None], grad_in[None], g_qkv, g_out.reshape(heads, hd, hidden), g_up, g_down,
            gain_sums[0], gain_sums[1])


def solution(mesh):
    act_spec = P('data', 'model', None)
    in_specs = (act_spec, P('data', None), P(), P(None, 'model', None, None), P('model', None, None), P(), P(None, 'model'), P('model', None), act_spec)
    out_specs = (act_spec, act_spec, P('data', 'model', None, None), P(('data', 'model'), None, None), P('data', 'model'), P(('data', 'model'), None), P('data'), P('data'))
    return jax.shard_map(functools.partial(local_layer, mesh.shape['model']), mesh=mesh, in_specs=in_specs, out_specs=out_specs, check_vma=False)
```

time: 820 us -> 685 us (0.84); the launches traced: 809 us -> 682 us
  matrix products: 336 us -> 196 us
  Pallas kernels: 0 us -> 73.2 us
  other arithmetic: 74.1 us -> 25.1 us
  blocking collectives: 21 us -> 0 us
  starting transfers between devices: 0.76 us -> 9.07 us
    dot_general x15 -> x12, matrix products: 272 us -> 196 us  [the longest x1 26.1 us: local_layer(): d_act = ein('sd,fd->sf', grad_full, w_down)]
    pallas_call x0 -> x2, Pallas kernels: none -> 73.2 us  [the longest x1 48.1 us: attention_bwd(): pl.pallas_call(functools.partial(attn_bwd_kernel, heads, hd), grid_spec=p...]
    convert_element_type x7 -> x4, other arithmetic: 51.8 us -> 8.06 us  [the longest x1 4.96 us: local_layer(): d_mid = (dy.astype(jnp.float32) + d_mid_ln).astype(jnp.bfloat16)]
    sub x1 -> x0, matrix products: 36.3 us -> none  [attention_fwd(): jax.nn.softmax(jnp.where(attn_mask[:, None], scores, -1e+30), axis=-1)]
    unnamed x2 -> x0, matrix products: 27.8 us -> none
    psum x1 -> x0, blocking collectives: 21 us -> none  [local_layer(): gain_sums = lax.psum(jnp.stack([d_gain_attn, d_gain_mlp]), 'model')]
  transfers between devices with their start and end apart: 8 -> 15, of which waited for: 7 -> 7; matrix products, arithmetic and copies ran while one was open for 15% -> 16% of each run, Pallas kernels for 0% -> 0%
where the time goes in v1:
time: 685 us; the launch traced here: 682 us
  waiting for transfers between devices  360 us (53%)
  matrix products  196 us (29%)
  Pallas kernels  73.2 us (11%)
  other arithmetic  25.1 us (4%)
  between operations  14.8 us (2%)
  starting transfers between devices  9.07 us (1%)
    all_gather x4, waiting for transfers between devices, local_layer(): gather = lambda a: lax.all_gather(a, 'model', axis=0, tiled=True)  206 us
    reduce_scatter x4, waiting for transfers between devices, local_layer(): lax.psum_scatter(a, 'model', scatter_dimension=0, tiled=True)  153 us
    pallas_call x1, Pallas kernels, attention_bwd(): pl.pallas_call(functools.partial(attn_bwd_kernel, heads, hd), grid_spec=p...  48.1 us
    dot_general x1, matrix products, local_layer(): d_act = ein('sd,fd->sf', grad_full, w_down)  26.1 us
    pallas_call x1, Pallas kernels, attention_fwd(): pl.pallas_call(functools.partial(attn_fwd_kernel, heads, hd), grid_spec=p...  25.1 us
    dot_general x1, matrix products, local_layer(): g_down = ein('sf,sd->fd', act_lo, grad_full).astype(jnp.bfloat16)  22.8 us
    dot_general x1, matrix products, local_layer(): mlp_sum = scatter(ein('sf,fd->sd', act_lo, w_down).astype(jnp.bfloat16))  21.2 us
    dot_general x1, matrix products, local_layer(): g_up = ein('sd,sf->df', mlp_in, d_pre).astype(jnp.bfloat16)  20.3 us
  transfers between devices with their start and end apart: 15, of which 7 were waited for; matrix products, arithmetic and copies ran while one was open for 16% of the time, Pallas kernels for 0%

profile of v1, /device:TPU:81, one launch (start us, length us, event | category | flops | bytes accessed | tf_op | source)
XLA Modules:
  0.0 682.0 jit_solution(13463157315245788607)
XLA Ops:
  7.2 0.1 all-gather.6.cloned.1.call-start
  7.3 1.7 convert_reduce_fusion.2
  9.0 1.8 fusion.28
  10.9 0.6 copy-done.15
  11.5 0.5 copy-done.13
  12.0 0.6 copy-done.9
  12.6 1.5 fusion.27
  14.1 0.1 all-gather.6.cloned.1.call-update
  14.2 0.1 reduce-scatter.5.cloned.1.call-start
  14.3 1.7 convert_reduce_fusion
  16.0 0.1 slice.9
  16.1 0.5 and_select_fusion.lo_ref
  16.6 57.6 %all-gather.6.cloned.1.call-done = bf16[2048,2560]{1,0:T(8,128)(2,1)} async-done(((bf16[256,2560]{1,0:T(8,128)(2,1)}), bf16[2048,2560]{1,0:T(8,128)(2,1)}) %all-gather.6.cloned.1.call-update) | async-done | bytes 10485776 | tf_op jit(solution)/shard_map/all_gather | solution.py:211
  74.2 15.8 %convert_bitcast_fusion.qkv_ref = bf16[960,2048]{1,0:T(8,128)(2,1)} fusion(bf16[2048,2560]{1,0:T(8,128)(2,1)} %all-gather.6.cloned.1.call-done, bf16[960,2560]{1,0:T(8,128)(2,1)} %bitcast.91), kind=kOutput, calls=%fused_computation.31 | convolution fusion | flops 10068295680 | bytes 19333120 | tf_op jit(solution)/shard_map/nd,sd->ns/dot_general | solution.py:216
  90.0 25.1 %attn_fwd.1 = (bf16[320,2048]{1,0:T(8,128)(2,1)}, f32[8,2048]{1,0:T(8,128)}) custom-call(s32[8]{0:T(128)} %and_select_fusion.lo_ref, bf16[960,2048]{1,0:T(8,128)(2,1)} %convert_bitcast_fusion.qkv_ref, s32[1,2048]{1,0:T(1,128)} %bitcast.98), custom_call_target="tpu_custom_call" | custom-call | flops 21474836480 | bytes 3932160 | tf_op jit(solution)/shard_map/attn_fwd/pallas_call | solution.py:98
  115.1 9.6 %convolution_convert_fusion.5 = bf16[2048,2560]{1,0:T(8,128)(2,1)} fusion(bf16[320,2048]{1,0:T(8,128)(2,1)} %get-tuple-element.10.o_ref, bf16[320,2560]{1,0:T(8,128)(2,1)S(1)} %bitcast.85), kind=kOutput, calls=%fused_computation.8 | convolution fusion | flops 3360686080 | bytes 13434880 | tf_op jit(solution)/shard_map/es,ed->sd/dot_general | solution.py:218
  124.7 0.1 reduce-scatter.5.cloned.1.call-update
  124.7 0.1 all-gather.8.cloned.1.call-start
  124.8 0.6 copy-done.18
  125.4 57.5 %reduce-scatter.5.cloned.1.call-done = bf16[256,2560]{1,0:T(8,128)(2,1)} async-done(((bf16[2048,2560]{1,0:T(8,128)(2,1)}), bf16[256,2560]{1,0:T(8,128)(2,1)}) %reduce-scatter.5.cloned.1.call-update) | async-done | bytes 1310736 | tf_op jit(solution)/shard_map/reduce_scatter | solution.py:212
  182.8 1.8 convert_reduce_fusion.1
  184.6 0.5 fusion.33
  185.1 0.5 copy-done.4
  185.7 1.5 fusion.26
  187.2 0.1 all-gather.8.cloned.1.call-update
  187.2 0.1 all-gather.12.cloned.1.call-start
  187.3 0.6 all-gather.12.cloned.1.call-update
  187.9 0.6 reduce-scatter.9.cloned.1.call-start
  188.5 54.7 %all-gather.8.cloned.1.call-done = bf16[2048,2560]{1,0:T(8,128)(2,1)} async-done(((bf16[256,2560]{1,0:T(8,128)(2,1)}), bf16[2048,2560]{1,0:T(8,128)(2,1)}) %all-gather.8.cloned.1.call-update) | async-done | bytes 10485776 | tf_op jit(solution)/shard_map/all_gather | solution.py:211
  243.2 19.4 %fusion.45 = f32[2048,1280]{1,0:T(8,128)} fusion(bf16[2048,2560]{1,0:T(8,128)(2,1)} %all-gather.8.cloned.1.call-done, bf16[2560,1280]{1,0:T(8,128)(2,1)} %param.15), kind=kOutput, calls=%fused_computation.85 | convolution fusion | flops 13421772800 | bytes 27525120 | tf_op jit(solution)/shard_map/sd,df->sf/dot_general | solution.py:222
  262.6 37.7 %all-gather.12.cloned.1.call-done = bf16[1,2048,2560]{2,1,0:T(8,128)(2,1)} async-done(((bf16[1,256,2560]{2,1,0:T(8,128)(2,1)}), bf16[1,2048,2560]{2,1,0:T(8,128)(2,1)}) %all-gather.12.cloned.1.call-update) | async-done | bytes 10485776 | tf_op jit(solution)/shard_map/all_gather | solution.py:211
  300.3 26.1 %fusion.6 = bf16[2048,1280]{1,0:T(8,128)(2,1)} fusion(f32[2048,1280]{1,0:T(8,128)} %fusion.45, bf16[1280,2560]{1,0:T(8,128)(2,1)} %param.16, bf16[1,2048,2560]{2,1,0:T(8,128)(2,1)} %all-gather.12.cloned.1.call-done), kind=kOutput, calls=%fused_computation.15 | convolution fusion | flops 13474201600 | bytes 32768000 | tf_op jit(solution)/shard_map/sd,fd->sf/dot_general | solution.py:226
  326.4 20.1 %convolution_convert_fusion.1 = bf16[2048,2560]{1,0:T(8,128)(2,1)} fusion(bf16[2048,1280]{1,0:T(8,128)(2,1)} %fusion.6, bf16[2560,1280]{1,0:T(8,128)(2,1)} %param.15), kind=kOutput, calls=%fused_computation.4 | convolution fusion | flops 13427015680 | bytes 22282240 | tf_op jit(solution)/shard_map/sf,df->sd/dot_general | solution.py:228
  346.5 0.1 reduce-scatter.7.cloned.1.call-start
  346.6 21.2 %convolution_convert_fusion.2 = bf16[2048,2560]{1,0:T(8,128)(2,1)} fusion(bf16[1280,2560]{1,0:T(8,128)(2,1)} %param.16, f32[2048,1280]{1,0:T(8,128)} %fusion.45), kind=kOutput, calls=%fused_computation.5 | convolution fusion | flops 13450608640 | bytes 27525120 | tf_op jit(solution)/shard_map/sf,fd->sd/dot_general | solution.py:229
  367.8 0.1 reduce-scatter.7.cloned.1.call-update
  367.9 0.1 all-gather.10.cloned.1.call-start
  367.9 37.6 %reduce-scatter.9.cloned.1.call-done = bf16[256,2560]{1,0:T(8,128)(2,1)} async-done(((bf16[2048,2560]{1,0:T(8,128)(2,1)}), bf16[256,2560]{1,0:T(8,128)(2,1)}) %reduce-scatter.9.cloned.1.call-update) | async-done | bytes 1310736 | tf_op jit(solution)/shard_map/reduce_scatter | solution.py:212
  405.5 2.1 fusion.34
  407.6 1.3 fusion.31
  408.9 57.9 %reduce-scatter.7.cloned.1.call-done = bf16[256,2560]{1,0:T(8,128)(2,1)} async-done(((bf16[2048,2560]{1,0:T(8,128)(2,1)}), bf16[256,2560]{1,0:T(8,128)(2,1)}) %reduce-scatter.7.cloned.1.call-update) | async-done | bytes 1310736 | tf_op jit(solution)/shard_map/reduce_scatter | solution.py:212
  466.8 5.0 fusion.36
  471.7 0.1 all-gather.10.cloned.1.call-update
  471.8 0.1 reduce-scatter.11.cloned.1.call-start
  471.9 55.9 %all-gather.10.cloned.1.call-done = bf16[2048,2560]{1,0:T(8,128)(2,1)} async-done(((bf16[256,2560]{1,0:T(8,128)(2,1)}), bf16[2048,2560]{1,0:T(8,128)(2,1)}) %all-gather.10.cloned.1.call-update) | async-done | bytes 10485776 | tf_op jit(solution)/shard_map/all_gather | solution.py:211
  527.8 8.8 %fusion.37.do_ref = bf16[320,2048]{1,0:T(8,128)(2,1)} fusion(bf16[2048,2560]{1,0:T(8,128)(2,1)} %all-gather.10.cloned.1.call-done, bf16[320,2560]{1,0:T(8,128)(2,1)S(1)} %bitcast.86), kind=kOutput, calls=%fused_computation.62 | convolution fusion | flops 3356098560 | bytes 13434880 | tf_op jit(solution)/shard_map/ed,sd->es/dot_general | solution.py:236
  536.5 48.1 %attn_bwd.1 = bf16[960,2048]{1,0:T(8,128)(2,1)} custom-call(s32[8]{0:T(128)} %and_select_fusion.lo_ref, bf16[960,2048]{1,0:T(8,128)(2,1)} %convert_bitcast_fusion.qkv_ref, bf16[320,2048]{1,0:T(8,128)(2,1)} %get-tuple-element.10.o_ref, bf16[320,2048]{1,0:T(8,128)(2,1)} %fusion.37.do_ref, f32[8,2048]{1,0:T(8,128)} %get-tuple-element.11.lse_ref, s32[1,2048]{1,0:T(1,128)} %bitcast.99), custom_call_target="tpu_custom_call" | custom-call | flops 53687091200 | bytes 7864320 | tf_op jit(solution)/shard_map/attn_bwd/pallas_call | solution.py:174
  584.6 15.5 %convolution_convert_fusion = bf16[2048,2560]{1,0:T(8,128)(2,1)} fusion(bf16[960,2048]{1,0:T(8,128)(2,1)} %attn_bwd.1, bf16[960,2560]{1,0:T(8,128)(2,1)S(1)} %bitcast.94), kind=kOutput, calls=%fused_computation.3 | convolution fusion | flops 10071572480 | bytes 19333120 | tf_op jit(solution)/shard_map/ns,nd->sd/dot_general | solution.py:239
  600.2 22.8 %convolution_convert_fusion.3 = bf16[1280,2560]{1,0:T(8,128)(2,1)} fusion(bf16[1,2048,2560]{2,1,0:T(8,128)(2,1)} %all-gather.12.cloned.1.call-done, f32[2048,1280]{1,0:T(8,128)} %fusion.45), kind=kOutput, calls=%fused_computation.6 | convolution fusion | flops 13448642560 | bytes 27525120 | tf_op jit(solution)/shard_map/sf,sd->fd/dot_general | solution.py:231
  623.1 20.3 %convolution_convert_fusion.4 = bf16[2560,1280]{1,0:T(8,128)(2,1)} fusion(bf16[2048,2560]{1,0:T(8,128)(2,1)} %all-gather.8.cloned.1.call-done, bf16[2048,1280]{1,0:T(8,128)(2,1)} %fusion.6), kind=kOutput, calls=%fused_computation.7 | convolution fusion | flops 13425049600 | bytes 22282240 | tf_op jit(solution)/shard_map/sd,sf->df/dot_general | solution.py:232
  643.4 4.7 convolution_convert_fusion.7
  648.2 12.1 %convolution_convert_fusion.6 = bf16[960,2560]{1,0:T(8,128)(2,1)} fusion(bf16[960,2048]{1,0:T(8,128)(2,1)S(1)} %copy-done.22, bf16[2048,2560]{1,0:T(8,128)(2,1)S(1)} %bitcast.88), kind=kOutput, calls=%fused_computation.20 | convolution fusion | flops 10068787200 | bytes 19333120 | tf_op jit(solution)/shard_map/ns,sd->nd/dot_general | solution.py:240
  660.4 2.1 fusion.29
  662.5 1.3 fusion.32
  663.8 0.7 collective-permute-start.5
  664.6 1.9 collective-permute-start.4
  666.4 1.2 collective-permute-start.3
  667.6 2.2 collective-permute-start.2
  669.8 0.3 collective-permute-start.1
  670.1 0.1 collective-permute-start.6
  670.2 1.7 collective-permute-start
  671.9 2.2 fusion.40
  674.2 0.1 add_convert_fusion.1
  674.2 0.7 slice_reduce_fusion
  (83 shorter events, 0.4 us)
Async XLA Ops:
  7.2 107.9 %copy-start = (bf16[4,80,2560]{2,1,0:T(8,128)(2,1)S(1)}, bf16[4,80,2560]{2,1,0:T(8,128)(2,1)}, u32[]{:S(2)}) copy-start(bf16[4,80,2560]{2,1,0:T(8,128)(2,1)} %param.13) | copy-start | bytes 4915204
  7.2 5.4 copy-start.2
  7.2 4.2 copy-start.17
  7.2 67.0 %all-gather.6.cloned.1.call-start = ((), (), s32[]{:S(2)}) async-start(), calls=%async_computation.4 | async-start | bytes 11796480 | tf_op jit(solution)/shard_map/all_gather | solution.py:211
  9.0 2.4 copy-start.11
  9.0 5.2 copy-start.19
  10.8 0.6 copy-start.15
  11.4 0.6 copy-start.13
  12.0 0.6 copy-start.9
  14.2 168.6 %reduce-scatter.5.cloned.1.call-start = ((), (), s32[]{:S(2)}) async-start(), calls=%async_computation.5 | async-start | bytes 11796480 | tf_op jit(solution)/shard_map/reduce_scatter | solution.py:212
  16.0 74.0 %copy-start.20 = (s32[2048]{0:T(1024)}, s32[2048]{0:T(1024)S(1)}, u32[]{:S(2)}) copy-start(s32[2048]{0:T(1024)S(1)} %convert_reduce_fusion) | copy-start | bytes 24580
  124.7 0.7 copy-start.18
  124.7 118.5 %all-gather.8.cloned.1.call-start = ((), (), s32[]{:S(2)}) async-start(), calls=%async_computation.6 | async-start | bytes 11796480 | tf_op jit(solution)/shard_map/all_gather | solution.py:211
  184.6 1.1 copy-start.4
  187.2 113.1 %all-gather.12.cloned.1.call-start = ((), (), s32[]{:S(2)}) async-start(), calls=%async_computation.11 | async-start | bytes 11796480 | tf_op jit(solution)/shard_map/all_gather | solution.py:211
  187.9 217.6 %reduce-scatter.9.cloned.1.call-start = ((), (), s32[]{:S(2)}) async-start(), calls=%async_computation.8 | async-start | bytes 11796480 | tf_op jit(solution)/shard_map/reduce_scatter | solution.py:212
  346.5 120.2 %reduce-scatter.7.cloned.1.call-start = ((), (), s32[]{:S(2)}) async-start(), calls=%async_computation.7 | async-start | bytes 11796480 | tf_op jit(solution)/shard_map/reduce_scatter | solution.py:212
  367.8 37.7 %copy-start.5 = (bf16[256,2560]{1,0:T(8,128)(2,1)S(1)}, bf16[256,2560]{1,0:T(8,128)(2,1)}, u32[]{:S(2)}) copy-start(bf16[256,2560]{1,0:T(8,128)(2,1)} %copy-done.4) | copy-start | bytes 3932164
  367.9 159.9 %all-gather.10.cloned.1.call-start = ((), (), s32[]{:S(2)}) async-start(), calls=%async_computation.9 | async-start | bytes 11796480 | tf_op jit(solution)/shard_map/all_gather | solution.py:211
  405.5 2.1 copy-start.8
  471.8 188.5 %reduce-scatter.11.cloned.1.call-start = ((), (), s32[]{:S(2)}) async-start(), calls=%async_computation.10 | async-start | bytes 11796480 | tf_op jit(solution)/shard_map/reduce_scatter | solution.py:212
  527.8 56.8 %slice-start.6 = ((s8[4915200]{0:T(1024)(128)(4,1)}), s8[4194304]{0:T(1024)(128)(4,1)S(1)}, s32[]{:S(2)}) async-start(s8[4915200]{0:T(1024)(128)(4,1)} %bitcast.92), calls=%async_computation.18 | async-start | bytes 8388608
  536.5 48.1 %slice-start.7 = ((s8[4915200]{0:T(1024)(128)(4,1)}), s8[720896]{0:T(1024)(128)(4,1)S(1)}, s32[]{:S(2)}) async-start(s8[4915200]{0:T(1024)(128)(4,1)} %bitcast.92), calls=%async_computation.19 | async-start | bytes 1441792
  600.2 43.2 %slice-start.3 = ((s8[10485760]{0:T(1024)(128)(4,1)}), s8[4194304]{0:T(1024)(128)(4,1)S(1)}, s32[]{:S(2)}) async-start(s8[10485760]{0:T(1024)(128)(4,1)} %bitcast.89), calls=%async_computation.15 | async-start | bytes 8388608
  600.2 43.2 %slice-start.4 = ((s8[10485760]{0:T(1024)(128)(4,1)}), s8[4194304]{0:T(1024)(128)(4,1)S(1)}, s32[]{:S(2)}) async-start(s8[10485760]{0:T(1024)(128)(4,1)} %bitcast.89), calls=%async_computation.16 | async-start | bytes 8388608
  600.2 47.9 %slice-start = ((s8[10485760]{0:T(1024)(128)(4,1)}), s8[2097152]{0:T(1024)(128)(4,1)S(1)}, s32[]{:S(2)}) async-start(s8[10485760]{0:T(1024)(128)(4,1)} %bitcast.87), calls=%async_computation.12 | async-start | bytes 4194304
  623.1 20.3 %slice-start.5 = ((s8[10485760]{0:T(1024)(128)(4,1)}), s8[2097152]{0:T(1024)(128)(4,1)S(1)}, s32[]{:S(2)}) async-start(s8[10485760]{0:T(1024)(128)(4,1)} %bitcast.89), calls=%async_computation.17 | async-start | bytes 4194304
  623.1 20.3 %copy-start.21 = (bf16[320,2048]{1,0:T(8,128)(2,1)S(1)}, bf16[320,2048]{1,0:T(8,128)(2,1)}, u32[]{:S(2)}) copy-start(bf16[320,2048]{1,0:T(8,128)(2,1)} %get-tuple-element.10.o_ref) | copy-start | bytes 3932164
  623.1 25.1 %slice-start.1 = ((s8[10485760]{0:T(1024)(128)(4,1)}), s8[4194304]{0:T(1024)(128)(4,1)S(1)}, s32[]{:S(2)}) async-start(s8[10485760]{0:T(1024)(128)(4,1)} %bitcast.87), calls=%async_computation.13 | async-start | bytes 8388608
  623.1 25.1 %slice-start.2 = ((s8[10485760]{0:T(1024)(128)(4,1)}), s8[4194304]{0:T(1024)(128)(4,1)S(1)}, s32[]{:S(2)}) async-start(s8[10485760]{0:T(1024)(128)(4,1)} %bitcast.87), calls=%async_computation.14 | async-start | bytes 8388608
  643.4 4.7 copy-start.22
  648.1 12.2 %copy-start.3 = (bf16[1,256,2560]{2,1,0:T(8,128)(2,1)S(1)}, bf16[1,256,2560]{2,1,0:T(8,128)(2,1)}, u32[]{:S(2)}) copy-start(bf16[1,256,2560]{2,1,0:T(8,128)(2,1)} %param.9) | copy-start | bytes 3932164
  648.2 12.2 %copy-start.10 = (f32[2560]{0:T(1024)S(1)}, f32[2560]{0:T(1024)}, u32[]{:S(2)}) copy-start(f32[2560]{0:T(1024)} %copy-done.9) | copy-start | bytes 30724
  648.2 12.2 %copy-start.12 = (f32[256]{0:T(256)S(1)}, f32[256]{0:T(256)}, u32[]{:S(2)}) copy-start(f32[256]{0:T(256)} %copy-done.11) | copy-start | bytes 3076
  660.3 2.2 copy-start.16
  660.3 2.2 copy-start.14
  660.4 2.2 copy-start.6
  660.4 11.6 %copy-start.7 = (bf16[256,2560]{1,0:T(8,128)(2,1)S(1)}, bf16[256,2560]{1,0:T(8,128)(2,1)}, u32[]{:S(2)}) copy-start(bf16[256,2560]{1,0:T(8,128)(2,1)} %get-tuple-element.20) | copy-start | bytes 3932164
  663.8 6.3 collective-permute-start.5
  664.6 5.6 collective-permute-start.4
  666.4 7.7 %collective-permute-start.3 = (f32[2,2560]{1,0:T(2,128)S(1)}, f32[2,2560]{1,0:T(2,128)S(1)}, u32[]{:S(2)}, u32[]{:S(2)}) collective-permute-start(f32[2,2560]{1,0:T(2,128)S(1)} %pad_maximum_fusion), channel_id=1, source_target_pairs={{0,4},{1,5},{2,6},{3,7},{4,0},{5,1},{6,2},{7,3},{8,12},{9,13},{10,... | collective-permute-start | bytes 61448 | tf_op jit(solution)/shard_map/ppermute | solution.py:196
  667.6 6.5 collective-permute-start.2
  669.8 4.3 collective-permute-start.1
  670.1 4.8 copy-start.1
  670.1 4.0 collective-permute-start.6
  670.2 3.9 collective-permute-start
Sparse Core Ops, SparseCore 0:
  14.3 59.8 all-gather.5
  124.8 57.9 reduce-scatter.4
  187.4 55.8 all-gather.7
  244.7 55.6 all-gather.11
  346.7 58.8 reduce-scatter.8
  407.7 59.0 reduce-scatter.6
  471.9 55.8 all-gather.9
  600.3 57.8 reduce-scatter.10

commit v2 on v1

--- a/solution.py
+++ b/solution.py
@@ -10,6 +10,7 @@
 LN_EPS = 1e-5
 BLK = 256
 NT = (((1,), (1,)), ((), ()))
+MESH = pl.DeviceIdType.MESH
 
 
 def layer_norm(x_f32, gain_f32):
@@ -190,6 +191,423 @@
     )(lo, qkv_t, o_t, do_t, lse, first)
 
 
+def dot_nt(a, b):
+    return lax.dot_general(a, b, NT, preferred_element_type=jnp.float32)
+
+
+class Ring:
+    def __init__(self, n):
+        self.n = n
+        self.me = lax.axis_index('model')
+        self.core = lax.rem(self.me, 2)
+        self.chip = self.me // 2
+        self.partner = self.me + 1 - 2 * self.core
+        self.next = lax.rem(self.me + 2, n)
+        self.prev = lax.rem(self.me + n - 2, n)
+        self.opp = lax.rem(self.me + n // 2, n)
+
+    def barrier(self):
+        sem = pltpu.get_barrier_semaphore()
+        for dev in (self.partner, self.next, self.prev):
+            pl.semaphore_signal(sem, inc=1, device_id={'model': dev}, device_id_type=MESH)
+        pl.semaphore_wait(sem, 3)
+
+    def ahead(self, d):
+        return lax.rem(self.chip + d, self.n // 2)
+
+
+def rows_at(start, size, unit=None):
+    return pl.ds(pl.multiple_of(start, unit or size), size)
+
+
+class Gather:
+    def __init__(self, ring, buf, send, recv):
+        self.ring, self.buf, self.send, self.recv = ring, buf, send, recv
+        self.rows = buf.shape[0] // ring.n
+        self.half = self.rows // 2
+        r = ring
+        self.table = {0: (r.me, None, r.partner),
+                      1: (r.me, 0, r.next), 2: (r.me, 1, r.next), 3: (r.prev, 0, r.next),
+                      4: (r.me, 1, r.prev), 5: (r.me, 0, r.prev), 6: (r.next, 1, r.prev),
+                      7: (r.prev, 0, r.partner), 8: (r.prev, 1, r.partner),
+                      9: (r.next, 1, r.partner), 10: (r.next, 0, r.partner),
+                      11: (r.opp, 0, r.partner), 12: (r.opp, 1, r.partner)}
+
+    def copy(self, k):
+        owner, part, dev = self.table[k]
+        if part is None:
+            ref = self.buf.at[rows_at(owner * self.rows, self.rows)]
+        else:
+            ref = self.buf.at[rows_at(owner * self.rows + part * self.half, self.half)]
+        return pltpu.make_async_remote_copy(src_ref=ref, dst_ref=ref, send_sem=self.send.at[k], recv_sem=self.recv.at[k],
+                                            device_id={'model': dev}, device_id_type=MESH)
+
+    def start(self, *ks):
+        for k in ks:
+            self.copy(k).start()
+
+    def arrived(self, *ks):
+        for k in ks:
+            self.copy(k).wait_recv()
+
+    def run(self, compute):
+        self.start(1, 4, 0, 2, 5)
+        self.arrived(0)
+        compute(self.ring.chip)
+        self.arrived(1)
+        self.start(3, 7)
+        self.arrived(4)
+        self.start(6, 9)
+        self.arrived(2)
+        self.start(8)
+        self.arrived(5)
+        self.start(10)
+        self.arrived(7, 8)
+        compute(self.ring.ahead(self.ring.n // 2 - 1))
+        self.arrived(9, 10)
+        compute(self.ring.ahead(1))
+        self.arrived(3)
+        self.start(11)
+        self.arrived(6)
+        self.start(12)
+        self.arrived(11, 12)
+        compute(self.ring.ahead(self.ring.n // 4))
+        for k in self.table:
+            self.copy(k).wait_send()
+
+
+def gather_t_kernel(n, tile, x_ref, w_ref, full_ref, out_ref, buf, w_s, stage, send, recv, load, store, put):
+    ring = Ring(n)
+    rows = x_ref.shape[0]
+    mine = pltpu.make_async_copy(x_ref, buf.at[rows_at(ring.me * rows, rows)], load.at[0])
+    mine.start()
+    weights = pltpu.make_async_copy(w_ref, w_s, load.at[1])
+    weights.start()
+    ring.barrier()
+    mine.wait()
+    g = Gather(ring, buf, send, recv)
+    pending = []
+
+    def compute(chip):
+        s = len(pending)
+        if s == 0:
+            weights.wait()
+        at = rows_at(chip * (2 * rows), 2 * rows)
+        keep = pltpu.make_async_copy(buf.at[at], full_ref.at[at], store.at[s])
+        keep.start()
+
+        def body(t, c):
+            w_rows = rows_at(t * tile, tile)
+            stage[s, w_rows, :] = dot_nt(w_s[w_rows, :], buf[at, :]).astype(jnp.bfloat16)
+            return c
+
+        lax.fori_loop(0, w_s.shape[0] // tile, body, 0)
+        out = pltpu.make_async_copy(stage.at[s], out_ref.at[:, at], put.at[s])
+        out.start()
+        pending.append((keep, out))
+
+    g.run(compute)
+    for pair in pending:
+        for cp in pair:
+            cp.wait()
+
+
+def gather_t(n, cid, x, w, tile):
+    rows, hidden = x.shape
+    seq, m, chips = rows * n, w.shape[0], n // 2
+    dma = pltpu.SemaphoreType.DMA
+    return pl.pallas_call(
+        functools.partial(gather_t_kernel, n, tile),
+        in_specs=[pl.BlockSpec(memory_space=pl.ANY)] * 2,
+        out_specs=[pl.BlockSpec(memory_space=pl.ANY)] * 2,
+        out_shape=[jax.ShapeDtypeStruct((seq, hidden), x.dtype), jax.ShapeDtypeStruct((m, seq), x.dtype)],
+        scratch_shapes=[pltpu.VMEM((seq, hidden), x.dtype), pltpu.VMEM(w.shape, w.dtype),
+                        pltpu.VMEM((chips, m, 2 * rows), x.dtype),
+                        dma((13,)), dma((13,)), dma((2,)), dma((chips,)), dma((chips,))],
+        compiler_params=pltpu.CompilerParams(collective_id=cid, has_side_effects=True, vmem_limit_bytes=60 * 2 ** 20),
+        cost_estimate=pl.CostEstimate(flops=40 * 10 ** 9, bytes_accessed=3 * seq * hidden, transcendentals=0),
+        name="gather_t",
+    )(x, w)
+
+
+def mlp_kernel(n, tile, x_ref, dy_ref, up_ref, down_ref, full_ref, g_ref, dz_ref,
+               buf, dy_s, up_s, down_s, g_s, dz_s, send, recv, load, store, put, put2, dy_sem):
+    ring = Ring(n)
+    rows = x_ref.shape[0]
+    mine = pltpu.make_async_copy(x_ref, buf.at[rows_at(ring.me * rows, rows)], load.at[0])
+    mine.start()
+    w_up = pltpu.make_async_copy(up_ref, up_s, load.at[1])
+    w_up.start()
+    w_down = pltpu.make_async_copy(down_ref, down_s, load.at[2])
+    w_down.start()
+    order = [ring.chip, ring.ahead(n // 2 - 1), ring.ahead(1), ring.ahead(n // 4)]
+
+    def dy_copy(s):
+        return pltpu.make_async_copy(dy_ref.at[rows_at(order[s] * (2 * rows), 2 * rows)], dy_s.at[s % 2], dy_sem.at[s])
+
+    dy_copy(0).start()
+    dy_copy(1).start()
+    ring.barrier()
+    mine.wait()
+    g = Gather(ring, buf, send, recv)
+    pending = []
+    root = (2.0 / jnp.pi) ** 0.5
+
+    def compute(chip):
+        s = len(pending)
+        if s == 0:
+            w_up.wait()
+            w_down.wait()
+        at = rows_at(chip * (2 * rows), 2 * rows)
+        keep = pltpu.make_async_copy(buf.at[at], full_ref.at[at], store.at[s])
+        keep.start()
+        dy_copy(s).wait()
+        if s >= 2:
+            for cp in pending[s - 2][1:]:
+                cp.wait()
+
+        def body(t, c):
+            cols = rows_at(t * tile, tile)
+            z = dot32(buf[at, :], up_s[:, cols])
+            da = dot_nt(dy_s[s % 2], down_s[cols, :])
+            z2 = z * z
+            th = jnp.tanh(root * (z + 0.044715 * (z2 * z)))
+            cdf = 0.5 * (1.0 + th)
+            g_s[s % 2, :, cols] = (z * cdf).astype(jnp.bfloat16)
+            slope = cdf + (0.5 * z) * (1.0 - th * th) * (root * (1.0 + (3 * 0.044715) * z2))
+            dz_s[s % 2, :, cols] = (slope * da).astype(jnp.bfloat16)
+            return c
+
+        lax.fori_loop(0, up_s.shape[1] // tile, body, 0)
+        if s + 2 < n // 2:
+            dy_copy(s + 2).start()
+        og = pltpu.make_async_copy(g_s.at[s % 2], g_ref.at[at], put.at[s])
+        od = pltpu.make_async_copy(dz_s.at[s % 2], dz_ref.at[at], put2.at[s])
+        og.start()
+        od.start()
+        pending.append((keep, og, od))
+
+    g.run(compute)
+    for s, cps in enumerate(pending):
+        for cp in (cps if s >= n // 2 - 2 else cps[:1]):
+            cp.wait()
+
+
+def mlp(n, cid, x, dy, up, down, tile=256):
+    rows, hidden = x.shape
+    seq, ffn, chips = rows * n, up.shape[1], n // 2
+    dma = pltpu.SemaphoreType.DMA
+    return pl.pallas_call(
+        functools.partial(mlp_kernel, n, tile),
+        in_specs=[pl.BlockSpec(memory_space=pl.ANY)] * 4,
+        out_specs=[pl.BlockSpec(memory_space=pl.ANY)] * 3,
+        out_shape=[jax.ShapeDtypeStruct((seq, hidden), x.dtype)] + [jax.ShapeDtypeStruct((seq, ffn), x.dtype)] * 2,
+        scratch_shapes=[pltpu.VMEM((seq, hidden), x.dtype), pltpu.VMEM((2, 2 * rows, hidden), x.dtype),
+                        pltpu.VMEM(up.shape, x.dtype), pltpu.VMEM(down.shape, x.dtype),
+                        pltpu.VMEM((2, 2 * rows, ffn), x.dtype), pltpu.VMEM((2, 2 * rows, ffn), x.dtype),
+                        dma((13,)), dma((13,)), dma((3,)), dma((chips,)), dma((chips,)), dma((chips,)), dma((chips,))],
+        compiler_params=pltpu.CompilerParams(collective_id=cid, has_side_effects=True, vmem_limit_bytes=60 * 2 ** 20),
+        cost_estimate=pl.CostEstimate(flops=40 * 10 ** 9, bytes_accessed=3 * seq * hidden, transcendentals=0),
+        name="gather_mlp",
+    )(x, dy, up, down)
+
+
+def add_rows(dst, start, count, *terms):
+    step = 32
+
+    def body(i, c):
+        at = rows_at(start + i * step, step)
+        total = dst[at, :].astype(jnp.float32)
+        for ref, first in terms:
+            total = total + ref[rows_at(first + i * step, step), :].astype(jnp.float32)
+        dst[at, :] = total.astype(jnp.bfloat16)
+        return c
+
+    lax.fori_loop(0, count // step, body, 0)
+
+
+class Scatter:
+    def __init__(self, ring, part, pin, mid, fin, send, recv):
+        self.ring, self.part, self.pin, self.mid, self.fin, self.send, self.recv = ring, part, pin, mid, fin, send, recv
+        self.rows = part.shape[1] // 2
+        self.half = self.rows // 2
+        self.own = ring.core * self.rows
+
+    def copy(self, k):
+        r, h = self.ring, self.half
+        if k < 4:
+            src, dst, dev = self.part.at[k, rows_at((1 - r.core) * self.rows, self.rows)], self.pin.at[k], r.partner
+        else:
+            d, half, dst, dev = {4: (2, 0, self.mid.at[0], r.next), 5: (2, 1, self.mid.at[1], r.prev),
+                                 6: (1, 1, self.fin.at[0, h:], r.next), 7: (1, 0, self.fin.at[0, :h], r.next),
+                                 8: (3, 0, self.fin.at[1, :h], r.prev), 9: (3, 1, self.fin.at[1, h:], r.prev)}[k]
+            src = self.part.at[d, rows_at(self.own + half * h, h)]
+        return pltpu.make_async_remote_copy(src_ref=src, dst_ref=dst, send_sem=self.send.at[k], recv_sem=self.recv.at[k],
+                                            device_id={'model': dev}, device_id_type=MESH)
+
+    def start(self, k):
+        self.copy(k).start()
+
+    def arrived(self, k):
+        self.copy(k).wait_recv()
+
+    def join(self, d):
+        self.arrived(d)
+        add_rows(self.part.at[d], self.own, self.rows, (self.pin.at[d], 0))
+
+    def run(self, product, filler, out_ref):
+        h = self.half
+        product(2)
+        self.start(2)
+        product(1)
+        self.start(1)
+        self.join(2)
+        self.start(4)
+        self.start(5)
+        product(3)
+        self.start(3)
+        self.join(1)
+        self.start(6)
+        self.join(3)
+        self.start(8)
+        product(0)
+        self.start(0)
+        self.join(0)
+        self.arrived(4)
+        add_rows(self.part.at[1], self.own, h, (self.mid.at[0], 0))
+        self.start(7)
+        self.arrived(5)
+        add_rows(self.part.at[3], self.own + h, h, (self.mid.at[1], 0))
+        self.start(9)
+        filler()
+        for k in (6, 7, 8, 9):
+            self.arrived(k)
+        step = 32
+
+        def body(i, c):
+            at = rows_at(i * step, step)
+            total = self.part[0, rows_at(self.own + i * step, step), :].astype(jnp.float32)
+            total = total + self.fin[0, at, :].astype(jnp.float32) + self.fin[1, at, :].astype(jnp.float32)
+            out_ref[at, :] = total.astype(jnp.bfloat16)
+            return c
+
+        lax.fori_loop(0, self.rows // step, body, 0)
+        for k in range(10):
+            self.copy(k).wait_send()
+
+
+def scatter_scratch(rows, hidden, dtype):
+    dma = pltpu.SemaphoreType.DMA
+    return [pltpu.VMEM((4, 2 * rows, hidden), dtype), pltpu.VMEM((4, rows, hidden), dtype),
+            pltpu.VMEM((2, rows // 2, hidden), dtype), pltpu.VMEM((2, rows, hidden), dtype), dma((10,)), dma((10,))]
+
+
+def scatter_t_kernel(n, tile, x_ref, w_ref, out_ref, x_s, w_s, lhs, part, pin, mid, fin, send, recv, load):
+    ring = Ring(n)
+    cx = pltpu.make_async_copy(x_ref, x_s, load.at[0])
+    cx.start()
+    cw = pltpu.make_async_copy(w_ref, w_s, load.at[1])
+    cw.start()
+    ring.barrier()
+    cx.wait()
+    cw.wait()
+    sc = Scatter(ring, part, pin, mid, fin, send, recv)
+    wide = part.shape[1]
+
+    def product(d):
+        at = rows_at(ring.ahead(d) * wide, wide)
+        lhs[...] = x_s[:, at].T
+
+        def body(t, c):
+            cols = rows_at(t * tile, tile)
+            part[d, :, cols] = dot32(lhs[...], w_s[:, cols]).astype(jnp.bfloat16)
+            return c
+
+        lax.fori_loop(0, w_s.shape[1] // tile, body, 0)
+
+    sc.run(product, lambda: None, out_ref)
+
+
+def scatter_t(n, cid, x, w, tile=512):
+    (m, seq), hidden = x.shape, w.shape[1]
+    rows = seq // n
+    dma = pltpu.SemaphoreType.DMA
+    return pl.pallas_call(
+        functools.partial(scatter_t_kernel, n, tile),
+        in_specs=[pl.BlockSpec(memory_space=pl.ANY)] * 2,
+        out_specs=pl.BlockSpec(memory_space=pltpu.VMEM),
+        out_shape=jax.ShapeDtypeStruct((rows, hidden), x.dtype),
+        scratch_shapes=[pltpu.VMEM(x.shape, x.dtype), pltpu.VMEM(w.shape, x.dtype), pltpu.VMEM((2 * rows, m), x.dtype)]
+        + scatter_scratch(rows, hidden, x.dtype) + [dma((2,))],
+        compiler_params=pltpu.CompilerParams(collective_id=cid, has_side_effects=True, vmem_limit_bytes=60 * 2 ** 20),
+        cost_estimate=pl.CostEstimate(flops=40 * 10 ** 9, bytes_accessed=3 * seq * hidden, transcendentals=0),
+        name="scatter_t",
+    )(x, w)
+
+
+def scatter_mlp_kernel(n, tile, dz_ref, up_ref, g_ref, down_ref, out_ref, y_ref,
+                       dz_s, w_s, g_s, down_s, part, pin, mid, fin, send, recv, load, ystage, put):
+    ring = Ring(n)
+    loads = [pltpu.make_async_copy(a, b, load.at[i]) for i, (a, b) in
+             enumerate(((dz_ref, dz_s), (up_ref, w_s), (g_ref, g_s), (down_ref, down_s)))]
+    for cp in loads:
+        cp.start()
+    ring.barrier()
+    loads[0].wait()
+    loads[1].wait()
+    sc = Scatter(ring, part, pin, mid, fin, send, recv)
+    wide = part.shape[1]
+    hidden = part.shape[2]
+
+    def product(d):
+        at = rows_at(ring.ahead(d) * wide, wide)
+
+        def body(t, c):
+            cols = rows_at(t * tile, tile)
+            part[d, :, cols] = dot_nt(dz_s[at, :], w_s[cols, :]).astype(jnp.bfloat16)
+            return c
+
+        lax.fori_loop(0, hidden // tile, body, 0)
+
+    def filler():
+        loads[2].wait()
+        loads[3].wait()
+        puts = []
+        for q in range(n // 2):
+            if q >= 2:
+                puts[q - 2].wait()
+
+            def body(t, c):
+                cols = rows_at(t * tile, tile)
+                ystage[q % 2, :, cols] = dot32(g_s[q * wide:(q + 1) * wide, :], down_s[:, cols]).astype(jnp.bfloat16)
+                return c
+
+            lax.fori_loop(0, hidden // tile, body, 0)
+            puts.append(pltpu.make_async_copy(ystage.at[q % 2], y_ref.at[q * wide:(q + 1) * wide], put.at[q]))
+            puts[q].start()
+        for cp in puts[-2:]:
+            cp.wait()
+
+    sc.run(product, filler, out_ref)
+
+
+def scatter_mlp(n, cid, dz, up, g, down, tile=512):
+    (seq, ffn), hidden = dz.shape, down.shape[1]
+    rows = seq // n
+    dma = pltpu.SemaphoreType.DMA
+    return pl.pallas_call(
+        functools.partial(scatter_mlp_kernel, n, tile),
+        in_specs=[pl.BlockSpec(memory_space=pl.ANY)] * 4,
+        out_specs=[pl.BlockSpec(memory_space=pltpu.VMEM), pl.BlockSpec(memory_space=pl.ANY)],
+        out_shape=[jax.ShapeDtypeStruct((rows, hidden), dz.dtype), jax.ShapeDtypeStruct((seq, hidden), dz.dtype)],
+        scratch_shapes=[pltpu.VMEM(a.shape, a.dtype) for a in (dz, up, g, down)]
+        + scatter_scratch(rows, hidden, dz.dtype) + [dma((4,)), pltpu.VMEM((2, 2 * rows, hidden), dz.dtype), dma((n // 2,))],
+        compiler_params=pltpu.CompilerParams(collective_id=cid, has_side_effects=True, vmem_limit_bytes=63 * 2 ** 20),
+        cost_estimate=pl.CostEstimate(flops=60 * 10 ** 9, bytes_accessed=3 * seq * hidden, transcendentals=0),
+        name="scatter_mlp",
+    )(dz, up, g, down)
+
+
 def group_sum(vals, n):
     total = vals
     for shift in range(1, n):
@@ -212,31 +630,26 @@
     scatter = lambda a: lax.psum_scatter(a, 'model', scatter_dimension=0, tiled=True)
 
     ln1_out, ln1_vjp = jax.vjp(layer_norm, x_f32, gain_attn.astype(jnp.float32))
-    attn_in = gather(ln1_out.astype(jnp.bfloat16))
-    qkv_t = ein('nd,sd->ns', wq_t, attn_in).astype(jnp.bfloat16)
+    attn_in, qkv_t = gather_t(n, 0, ln1_out.astype(jnp.bfloat16), wq_t, 320)
+    dy_late, qkv_t = lax.optimization_barrier((dy, qkv_t))
+    grad_full = gather(dy_late)
     o_t, lse = attention_fwd(qkv_t, lo, first, heads, hd)
-    attn_sum = scatter(ein('es,ed->sd', o_t, wo).astype(jnp.bfloat16))
+    attn_sum = scatter_t(n, 1, o_t, wo)
     mid_loc = (x_f32 + attn_sum.astype(jnp.float32)).astype(jnp.bfloat16)
     ln2_out, ln2_vjp = jax.vjp(layer_norm, mid_loc.astype(jnp.float32), gain_mlp.astype(jnp.float32))
-    mlp_in = gather(ln2_out.astype(jnp.bfloat16))
-    pre_act = ein('sd,df->sf', mlp_in, w_up)
-    act_f32, gelu_vjp = jax.vjp(gelu_tanh, pre_act)
-    act_lo = act_f32.astype(jnp.bfloat16)
-    grad_full = gather(dy)
-    d_act = ein('sd,fd->sf', grad_full, w_down)
-    d_pre = gelu_vjp(d_act)[0].astype(jnp.bfloat16)
-    d_mlp_in = scatter(ein('sf,df->sd', d_pre, w_up).astype(jnp.bfloat16))
-    mlp_sum = scatter(ein('sf,fd->sd', act_lo, w_down).astype(jnp.bfloat16))
+    mlp_in, act_lo, d_pre = mlp(n, 2, ln2_out.astype(jnp.bfloat16), grad_full, w_up, w_down)
+    d_mlp_in, mlp_part = scatter_mlp(n, 3, d_pre, w_up, act_lo, w_down)
+    d_mid_ln, d_gain_mlp = ln2_vjp(d_mlp_in.astype(jnp.float32))
+    d_mid = (dy.astype(jnp.float32) + d_mid_ln).astype(jnp.bfloat16)
+    d_mid_full, do_t = gather_t(n, 4, d_mid, wo, heads * hd)
+    mlp_part, do_t = lax.optimization_barrier((mlp_part, do_t))
+    mlp_sum = scatter(mlp_part)
     hidden_out = (mid_loc.astype(jnp.float32) + mlp_sum.astype(jnp.float32)).astype(jnp.bfloat16)
+    dqkv_t = attention_bwd(qkv_t, o_t, do_t, lse, lo, first, heads, hd)
+    d_attn_in = scatter_t(n, 5, dqkv_t, wq_t)
     g_down = ein('sf,sd->fd', act_lo, grad_full).astype(jnp.bfloat16)
     g_up = ein('sd,sf->df', mlp_in, d_pre).astype(jnp.bfloat16)
-    d_mid_ln, d_gain_mlp = ln2_vjp(d_mlp_in.astype(jnp.float32))
-    d_mid = (dy.astype(jnp.float32) + d_mid_ln).astype(jnp.bfloat16)
-    d_mid_full = gather(d_mid)
-    do_t = ein('ed,sd->es', wo, d_mid_full).astype(jnp.bfloat16)
     g_out = ein('es,sd->ed', o_t, d_mid_full).astype(jnp.bfloat16)
-    dqkv_t = attention_bwd(qkv_t, o_t, do_t, lse, lo, first, heads, hd)
-    d_attn_in = scatter(ein('ns,nd->sd', dqkv_t, wq_t).astype(jnp.bfloat16))
     g_qkv = ein('ns,sd->nd', dqkv_t, attn_in).astype(jnp.bfloat16)
     d_x_ln, d_gain_attn = ln1_vjp(d_attn_in.astype(jnp.float32))
     grad_in = (d_mid.astype(jnp.float32) + d_x_ln).astype(jnp.bfloat16)

time: 685 us -> 544 us (0.79)
  waiting for transfers between devices: 360 us -> 0.13 us
  Pallas kernels: 73.2 us -> 426 us
  matrix products: 196 us -> 59.2 us
    pallas_call x0 -> x6, Pallas kernels: none -> 369 us  [the longest x2 139 us: scatter_t(): pl.pallas_call(functools.partial(scatter_t_kernel, n, tile), in_specs=[pl...]
    all_gather x4 -> x1, waiting for transfers between devices: 206 us -> 0.01 us  [local_layer(): gather = lambda a: lax.all_gather(a, 'model', axis=0, tiled=True)]
    reduce_scatter x4 -> x1, waiting for transfers between devices: 153 us -> 0.01 us  [local_layer(): lax.psum_scatter(a, 'model', scatter_dimension=0, tiled=True)]
    dot_general x8 -> x0, matrix products: 136 us -> none  [the longest x1 26.1 us: local_layer(): d_act = ein('sd,fd->sf', grad_full, w_down)]
    pallas_call x1, Pallas kernels: 48.1 us -> 36.8 us  [attention_bwd(): pl.pallas_call(functools.partial(attn_bwd_kernel, heads, hd), grid_spec=p...]
  transfers between devices with their start and end apart: 15 -> 9, of which waited for: 7 -> 0; matrix products, arithmetic and copies ran while one was open for 16% -> 13% of each run, Pallas kernels for 0% -> 37%
where the time goes in v2:
time: 544 us; the launch traced here: 536 us
  Pallas kernels  426 us (78%)
  matrix products  59.2 us (11%)
  other arithmetic  25.4 us (5%)
  between operations  14.7 us (3%)
  starting transfers between devices  8.09 us (1%)
    pallas_call x2, Pallas kernels, scatter_t(): pl.pallas_call(functools.partial(scatter_t_kernel, n, tile), in_specs=[pl...  139 us
    pallas_call x2, Pallas kernels, gather_t(): pl.pallas_call(functools.partial(gather_t_kernel, n, tile), in_specs=[pl....  108 us
    pallas_call x1, Pallas kernels, mlp(): pl.pallas_call(functools.partial(mlp_kernel, n, tile), in_specs=[pl.Block...  63.7 us
    pallas_call x1, Pallas kernels, scatter_mlp(): pl.pallas_call(functools.partial(scatter_mlp_kernel, n, tile), in_specs=[...  57.9 us
    pallas_call x1, Pallas kernels, attention_bwd(): pl.pallas_call(functools.partial(attn_bwd_kernel, heads, hd), grid_spec=p...  36.8 us
    dot_general x1, matrix products, local_layer(): g_up = ein('sd,sf->df', mlp_in, d_pre).astype(jnp.bfloat16)  20 us
    pallas_call x1, Pallas kernels, attention_fwd(): pl.pallas_call(functools.partial(attn_fwd_kernel, heads, hd), grid_spec=p...  19.9 us
    dot_general x1, matrix products, local_layer(): g_down = ein('sf,sd->fd', act_lo, grad_full).astype(jnp.bfloat16)  18.4 us
  transfers between devices with their start and end apart: 9, of which 0 were waited for; matrix products, arithmetic and copies ran while one was open for 13% of the time, Pallas kernels for 37%

profile of v2, /device:TPU:81, one launch (start us, length us, event | category | flops | bytes accessed | tf_op | source)
XLA Modules:
  0.0 536.1 jit_solution(18133723437778515451)
XLA Ops:
  7.2 0.0 copy-start.3
  7.2 0.0 copy-start.17
  7.2 0.1 all-gather.2.cloned.1.call-start
  7.3 1.7 convert_reduce_fusion.2
  8.9 0.0 copy-start.11
  8.9 1.8 fusion.16
  10.8 0.5 copy-done.15
  11.3 0.0 copy-start.9
  11.3 0.6 copy-done.9
  11.9 1.5 fusion.15.x_ref
  13.5 55.8 %gather_t.2 = (bf16[2048,2560]{1,0:T(8,128)(2,1)}, bf16[960,2048]{1,0:T(8,128)(2,1)}) custom-call(bf16[256,2560]{1,0:T(8,128)(2,1)} %fusion.15.x_ref, bf16[960,2560]{1,0:T(8,128)(2,1)} %bitcast.64), custom_call_target="tpu_custom_call" | custom-call | flops 40000000000 | bytes 15728640 | tf_op jit(solution)/shard_map/gather_t/pallas_call | solution.py:319
  69.3 0.1 all-gather.2.cloned.1.call-update
  69.3 0.1 reduce-scatter.2.cloned.1.call-start
  69.4 1.7 convert_reduce_fusion
  71.1 0.0 copy-start.20
  71.1 0.1 slice.9
  71.2 0.5 and_select_fusion.lo_ref
  71.8 19.9 %attn_fwd.1 = (bf16[320,2048]{1,0:T(8,128)(2,1)}, f32[8,2048]{1,0:T(8,128)}) custom-call(s32[8]{0:T(128)} %and_select_fusion.lo_ref, bf16[960,2048]{1,0:T(8,128)(2,1)} %get-tuple-element.24.qkv_ref, s32[1,2048]{1,0:T(1,128)} %bitcast.71), custom_call_target="tpu_custom_call" | custom-call | flops 21474836480 | bytes 3932160 | tf_op jit(solution)/shard_map/attn_fwd/pallas_call | solution.py:99
  91.7 75.7 %scatter_t.2 = bf16[256,2560]{1,0:T(8,128)(2,1)} custom-call(bf16[320,2048]{1,0:T(8,128)(2,1)} %get-tuple-element.25.x_ref.o_ref, bf16[320,2560]{1,0:T(8,128)(2,1)} %bitcast.66), custom_call_target="tpu_custom_call" | custom-call | flops 40000000000 | bytes 15728640 | tf_op jit(solution)/shard_map/scatter_t/pallas_call | solution.py:535
  167.4 1.8 convert_reduce_fusion.1
  169.2 0.5 fusion.21
  169.7 0.5 copy-done
  170.2 1.5 fusion.14.x_ref
  171.7 63.7 %gather_mlp.1 = (bf16[2048,2560]{1,0:T(8,128)(2,1)}, bf16[2048,1280]{1,0:T(8,128)(2,1)}, bf16[2048,1280]{1,0:T(8,128)(2,1)}) custom-call(bf16[256,2560]{1,0:T(8,128)(2,1)} %fusion.14.x_ref, bf16[2048,2560]{1,0:T(8,128)(2,1)} %all-gather.2.cloned.1.call-done.dy_ref, bf16[2560,1280]{1,0:T(8,128)(2,1)} %up_ref.3, bf16[1280,2560]{1,0:T(8,128)(2,1)} %down_ref.3), custom_call_target="tpu_custom_call" | custom-call | flops 40000000000 | bytes 15728640 | tf_op jit(solution)/shard_map/gather_mlp/pallas_call | solution.py:400
  235.5 57.9 %scatter_mlp.1 = (bf16[256,2560]{1,0:T(8,128)(2,1)}, bf16[2048,2560]{1,0:T(8,128)(2,1)}) custom-call(bf16[2048,1280]{1,0:T(8,128)(2,1)} %get-tuple-element.27.dz_ref, bf16[2560,1280]{1,0:T(8,128)(2,1)} %up_ref.3, bf16[2048,1280]{1,0:T(8,128)(2,1)} %get-tuple-element.28.g_ref, bf16[1280,2560]{1,0:T(8,128)(2,1)} %down_ref.3), custom_call_target="tpu_custom_call" | custom-call | flops 60000002048 | bytes 15728640 | tf_op jit(solution)/shard_map/scatter_mlp/pallas_call | solution.py:598
  293.4 0.0 copy-start.8
  293.4 2.5 fusion.22
  296.0 1.3 fusion.19
  297.3 2.2 add_convert_fusion.1.x_ref
  299.5 52.6 %gather_t.3 = (bf16[2048,2560]{1,0:T(8,128)(2,1)}, bf16[320,2048]{1,0:T(8,128)(2,1)}) custom-call(bf16[256,2560]{1,0:T(8,128)(2,1)} %add_convert_fusion.1.x_ref, bf16[320,2560]{1,0:T(8,128)(2,1)} %bitcast.67), custom_call_target="tpu_custom_call" | custom-call | flops 40000000000 | bytes 15728640 | tf_op jit(solution)/shard_map/gather_t/pallas_call | solution.py:319
  352.1 0.1 reduce-scatter.2.cloned.1.call-update
  352.1 36.8 %attn_bwd.1.x_ref = bf16[960,2048]{1,0:T(8,128)(2,1)} custom-call(s32[8]{0:T(128)} %and_select_fusion.lo_ref, bf16[960,2048]{1,0:T(8,128)(2,1)} %get-tuple-element.24.qkv_ref, bf16[320,2048]{1,0:T(8,128)(2,1)} %get-tuple-element.25.x_ref.o_ref, bf16[320,2048]{1,0:T(8,128)(2,1)} %get-tuple-element.33.do_ref, f32[8,2048]{1,0:T(8,128)} %get-tuple-element.34.lse_ref, ...), custom_call_target="tpu_custom_call" | custom-call | flops 53687091200 | bytes 7864320 | tf_op jit(solution)/shard_map/attn_bwd/pallas_call | solution.py:175
  389.0 0.0 copy-start.21
  389.0 63.6 %scatter_t.3 = bf16[256,2560]{1,0:T(8,128)(2,1)} custom-call(bf16[960,2048]{1,0:T(8,128)(2,1)} %attn_bwd.1.x_ref, bf16[960,2560]{1,0:T(8,128)(2,1)} %bitcast.65), custom_call_target="tpu_custom_call" | custom-call | flops 40000000000 | bytes 15728640 | tf_op jit(solution)/shard_map/scatter_t/pallas_call | solution.py:535
  452.7 0.0 copy-start.14
  452.7 0.0 slice-start.3
  452.7 2.1 fusion.17
  454.8 0.0 copy-done.16
  454.8 1.3 fusion.20
  456.1 0.7 collective-permute-start.5
  456.8 2.0 collective-permute-start.4
  458.8 1.3 collective-permute-start.3
  460.1 2.0 collective-permute-start.2
  462.1 0.3 collective-permute-start.1
  462.4 8.8 %convolution_convert_fusion.3 = bf16[320,2560]{1,0:T(8,128)(2,1)} fusion(bf16[320,2048]{1,0:T(8,128)(2,1)S(1)} %copy-done.21, bf16[2048,2560]{1,0:T(8,128)(2,1)} %get-tuple-element.36), kind=kOutput, calls=%fused_computation.4 | convolution fusion | flops 3356262400 | bytes 13434880 | tf_op jit(solution)/shard_map/es,sd->ed/dot_general | solution.py:652
  471.2 0.0 slice-start
  471.2 0.0 slice-start.1
  471.2 12.0 %convolution_convert_fusion.2 = bf16[960,2560]{1,0:T(8,128)(2,1)} fusion(bf16[960,2048]{1,0:T(8,128)(2,1)S(1)} %copy-done.22, bf16[2048,2560]{1,0:T(8,128)(2,1)S(1)} %bitcast.74), kind=kOutput, calls=%fused_computation.3 | convolution fusion | flops 10068787200 | bytes 19333120 | tf_op jit(solution)/shard_map/ns,sd->nd/dot_general | solution.py:653
  483.3 20.0 %convolution_convert_fusion.1 = bf16[2560,1280]{1,0:T(8,128)(2,1)} fusion(bf16[2048,2560]{1,0:T(8,128)(2,1)} %get-tuple-element.37, bf16[2048,1280]{1,0:T(8,128)(2,1)} %get-tuple-element.27.dz_ref), kind=kOutput, calls=%fused_computation.2 | convolution fusion | flops 13425049600 | bytes 22282240 | tf_op jit(solution)/shard_map/sd,sf->df/dot_general | solution.py:651
  503.3 0.0 copy-start.7
  503.3 18.4 %convolution_convert_fusion = bf16[1280,2560]{1,0:T(8,128)(2,1)} fusion(bf16[2048,1280]{1,0:T(8,128)(2,1)} %get-tuple-element.28.g_ref, bf16[2048,2560]{1,0:T(8,128)(2,1)S(1)} %bitcast.63), kind=kOutput, calls=%fused_computation.1 | convolution fusion | flops 13425049600 | bytes 22282240 | tf_op jit(solution)/shard_map/sf,sd->fd/dot_general | solution.py:650
  521.7 0.0 collective-permute-done.5
  521.7 0.1 collective-permute-start.6
  521.7 0.0 collective-permute-done.4
  521.7 1.7 collective-permute-start
  523.5 2.2 fusion.26
  525.6 0.0 collective-permute-done.3
  525.6 0.0 collective-permute-done.2
  525.6 0.0 collective-permute-done.1
  525.6 0.0 collective-permute-done.6
  525.6 0.0 collective-permute-done
  525.7 0.1 add_convert_fusion.2
  525.7 0.7 slice_reduce_fusion
  526.4 2.7 fusion.27
  (59 shorter events, 0.2 us)
Async XLA Ops:
  7.2 4.7 copy-start.3
  7.2 4.1 copy-start.17
  7.2 164.5 %all-gather.2.cloned.1.call-start = ((), (), s32[]{:S(2)}) async-start(), calls=%async_computation.1 | async-start | bytes 11796480 | tf_op jit(solution)/shard_map/all_gather | solution.py:629
  8.9 4.5 copy-start.11
  10.7 0.5 copy-start.15
  11.3 2.1 copy-start.13
  11.3 0.6 copy-start.9
  13.4 56.0 %copy-start.19 = (s32[1,2048]{1,0:T(1,128)S(1)}, s32[1,2048]{1,0:T(1,128)}, u32[]{:S(2)}) copy-start(s32[1,2048]{1,0:T(1,128)} %param.10) | copy-start | bytes 24580
  13.4 57.8 %copy-start.18 = (bf16[2560]{0:T(1024)(128)(2,1)S(1)}, bf16[2560]{0:T(1024)(128)(2,1)}, u32[]{:S(2)}) copy-start(bf16[2560]{0:T(1024)(128)(2,1)} %param.14) | copy-start | bytes 15364
  69.3 457.0 %reduce-scatter.2.cloned.1.call-start = ((), (), s32[]{:S(2)}) async-start(), calls=%async_computation.2 | async-start | bytes 11796480 | tf_op jit(solution)/shard_map/reduce_scatter | solution.py:630
  71.1 0.6 copy-start.20
  169.2 1.1 copy-start
  293.4 2.6 copy-start.1
  293.4 2.6 copy-start.6
  293.4 3.9 copy-start.8
  389.0 63.6 %copy-start.4 = (bf16[1,256,2560]{2,1,0:T(8,128)(2,1)S(1)}, bf16[1,256,2560]{2,1,0:T(8,128)(2,1)}, u32[]{:S(2)}) copy-start(bf16[1,256,2560]{2,1,0:T(8,128)(2,1)} %param.9) | copy-start | bytes 3932164
  389.0 63.6 %copy-start.10 = (f32[2560]{0:T(1024)S(1)}, f32[2560]{0:T(1024)}, u32[]{:S(2)}) copy-start(f32[2560]{0:T(1024)} %copy-done.9) | copy-start | bytes 30724
  389.0 63.7 %copy-start.12 = (f32[256]{0:T(256)S(1)}, f32[256]{0:T(256)}, u32[]{:S(2)}) copy-start(f32[256]{0:T(256)} %copy-done.11) | copy-start | bytes 3076
  389.0 73.4 %copy-start.21 = (bf16[320,2048]{1,0:T(8,128)(2,1)S(1)}, bf16[320,2048]{1,0:T(8,128)(2,1)}, u32[]{:S(2)}) copy-start(bf16[320,2048]{1,0:T(8,128)(2,1)} %get-tuple-element.25.x_ref.o_ref) | copy-start | bytes 3932164
  452.6 2.2 copy-start.16
  452.7 2.2 copy-start.5
  452.7 2.2 copy-start.14
  452.7 18.5 %slice-start.3 = ((s8[10485760]{0:T(1024)(128)(4,1)}), s8[4194304]{0:T(1024)(128)(4,1)S(1)}, s32[]{:S(2)}) async-start(s8[10485760]{0:T(1024)(128)(4,1)} %bitcast.73), calls=%async_computation.6 | async-start | bytes 8388608
  456.1 65.5 %collective-permute-start.5 = (f32[2,2560]{1,0:T(2,128)S(1)}, f32[2,2560]{1,0:T(2,128)S(1)}, u32[]{:S(2)}, u32[]{:S(2)}) collective-permute-start(f32[2,2560]{1,0:T(2,128)S(1)} %pad_maximum_fusion), channel_id=1, source_target_pairs={{0,6},{1,7},{2,0},{3,1},{4,2},{5,3},{6,4},{7,5},{8,14},{9,15},{10,... | collective-permute-start | bytes 61448 | tf_op jit(solution)/shard_map/ppermute | solution.py:614
  456.8 64.9 %collective-permute-start.4 = (f32[2,2560]{1,0:T(2,128)S(1)}, f32[2,2560]{1,0:T(2,128)S(1)}, u32[]{:S(2)}, u32[]{:S(2)}) collective-permute-start(f32[2,2560]{1,0:T(2,128)S(1)} %pad_maximum_fusion), channel_id=1, source_target_pairs={{0,5},{1,6},{2,7},{3,0},{4,1},{5,2},{6,3},{7,4},{8,13},{9,14},{10,... | collective-permute-start | bytes 61448 | tf_op jit(solution)/shard_map/ppermute | solution.py:614
  458.8 66.8 %collective-permute-start.3 = (f32[2,2560]{1,0:T(2,128)S(1)}, f32[2,2560]{1,0:T(2,128)S(1)}, u32[]{:S(2)}, u32[]{:S(2)}) collective-permute-start(f32[2,2560]{1,0:T(2,128)S(1)} %pad_maximum_fusion), channel_id=1, source_target_pairs={{0,4},{1,5},{2,6},{3,7},{4,0},{5,1},{6,2},{7,3},{8,12},{9,13},{10,... | collective-permute-start | bytes 61448 | tf_op jit(solution)/shard_map/ppermute | solution.py:614
  460.1 65.6 %collective-permute-start.2 = (f32[2,2560]{1,0:T(2,128)S(1)}, f32[2,2560]{1,0:T(2,128)S(1)}, u32[]{:S(2)}, u32[]{:S(2)}) collective-permute-start(f32[2,2560]{1,0:T(2,128)S(1)} %pad_maximum_fusion), channel_id=1, source_target_pairs={{0,3},{1,4},{2,5},{3,6},{4,7},{5,0},{6,1},{7,2},{8,11},{9,12},{10,... | collective-permute-start | bytes 61448 | tf_op jit(solution)/shard_map/ppermute | solution.py:614
  462.1 63.6 %collective-permute-start.1 = (f32[2,2560]{1,0:T(2,128)S(1)}, f32[2,2560]{1,0:T(2,128)S(1)}, u32[]{:S(2)}, u32[]{:S(2)}) collective-permute-start(f32[2,2560]{1,0:T(2,128)S(1)} %pad_maximum_fusion), channel_id=1, source_target_pairs={{0,2},{1,3},{2,4},{3,5},{4,6},{5,7},{6,0},{7,1},{8,10},{9,11},{10,... | collective-permute-start | bytes 61448 | tf_op jit(solution)/shard_map/ppermute | solution.py:614
  462.3 8.9 %slice-start.4 = ((s8[10485760]{0:T(1024)(128)(4,1)}), s8[4194304]{0:T(1024)(128)(4,1)S(1)}, s32[]{:S(2)}) async-start(s8[10485760]{0:T(1024)(128)(4,1)} %bitcast.73), calls=%async_computation.7 | async-start | bytes 8388608
  462.3 8.9 %slice-start.5 = ((s8[10485760]{0:T(1024)(128)(4,1)}), s8[2097152]{0:T(1024)(128)(4,1)S(1)}, s32[]{:S(2)}) async-start(s8[10485760]{0:T(1024)(128)(4,1)} %bitcast.73), calls=%async_computation.8 | async-start | bytes 4194304
  462.3 8.9 %copy-start.22 = (bf16[960,2048]{1,0:T(8,128)(2,1)S(1)}, bf16[960,2048]{1,0:T(8,128)(2,1)}, u32[]{:S(2)}) copy-start(bf16[960,2048]{1,0:T(8,128)(2,1)} %attn_bwd.1.x_ref) | copy-start | bytes 11796484
  471.2 32.0 %slice-start = ((s8[10485760]{0:T(1024)(128)(4,1)}), s8[4194304]{0:T(1024)(128)(4,1)S(1)}, s32[]{:S(2)}) async-start(s8[10485760]{0:T(1024)(128)(4,1)} %bitcast.62), calls=%async_computation.3 | async-start | bytes 8388608
  471.2 32.0 %slice-start.1 = ((s8[10485760]{0:T(1024)(128)(4,1)}), s8[4194304]{0:T(1024)(128)(4,1)S(1)}, s32[]{:S(2)}) async-start(s8[10485760]{0:T(1024)(128)(4,1)} %bitcast.62), calls=%async_computation.4 | async-start | bytes 8388608
  483.3 20.0 %slice-start.2 = ((s8[10485760]{0:T(1024)(128)(4,1)}), s8[2097152]{0:T(1024)(128)(4,1)S(1)}, s32[]{:S(2)}) async-start(s8[10485760]{0:T(1024)(128)(4,1)} %bitcast.62), calls=%async_computation.5 | async-start | bytes 4194304
  503.3 20.2 %copy-start.7 = (bf16[256,2560]{1,0:T(8,128)(2,1)S(1)}, bf16[256,2560]{1,0:T(8,128)(2,1)}, u32[]{:S(2)}) copy-start(bf16[256,2560]{1,0:T(8,128)(2,1)} %add_convert_fusion.1.x_ref) | copy-start | bytes 3932164
  521.7 4.7 copy-start.2
  521.7 4.0 collective-permute-start.6
  521.7 3.9 collective-permute-start
Sparse Core Ops, SparseCore 0:
  69.5 79.0 all-gather.1
  352.3 70.7 reduce-scatter.1

commit v3 on v2

--- a/solution.py
+++ b/solution.py
@@ -250,14 +250,16 @@
         for k in ks:
             self.copy(k).wait_recv()
 
-    def run(self, compute):
+    def run(self, compute, fill=lambda k: None):
         self.start(1, 4, 0, 2, 5)
         self.arrived(0)
         compute(self.ring.chip)
+        fill(0)
         self.arrived(1)
         self.start(3, 7)
         self.arrived(4)
         self.start(6, 9)
+        fill(1)
         self.arrived(2)
         self.start(8)
         self.arrived(5)
@@ -266,6 +268,7 @@
         compute(self.ring.ahead(self.ring.n // 2 - 1))
         self.arrived(9, 10)
         compute(self.ring.ahead(1))
+        fill(2)
         self.arrived(3)
         self.start(11)
         self.arrived(6)
@@ -331,7 +334,7 @@
 
 
 def mlp_kernel(n, tile, x_ref, dy_ref, up_ref, down_ref, full_ref, g_ref, dz_ref,
-               buf, dy_s, up_s, down_s, g_s, dz_s, send, recv, load, store, put, put2, dy_sem):
+               buf, dy_s, up_s, down_s, g_s, dz_s, da_s, send, recv, load, store, put, put2, dy_sem):
     ring = Ring(n)
     rows = x_ref.shape[0]
     mine = pltpu.make_async_copy(x_ref, buf.at[rows_at(ring.me * rows, rows)], load.at[0])
@@ -361,15 +364,19 @@
         at = rows_at(chip * (2 * rows), 2 * rows)
         keep = pltpu.make_async_copy(buf.at[at], full_ref.at[at], store.at[s])
         keep.start()
-        dy_copy(s).wait()
         if s >= 2:
             for cp in pending[s - 2][1:]:
                 cp.wait()
+        if s == 0:
+            dy_copy(0).wait()
 
         def body(t, c):
             cols = rows_at(t * tile, tile)
             z = dot32(buf[at, :], up_s[:, cols])
-            da = dot_nt(dy_s[s % 2], down_s[cols, :])
+            if s == 0:
+                da = dot_nt(dy_s[0], down_s[cols, :])
+            else:
+                da = da_s[s - 1, :, cols]
             z2 = z * z
             th = jnp.tanh(root * (z + 0.044715 * (z2 * z)))
             cdf = 0.5 * (1.0 + th)
@@ -379,15 +386,29 @@
             return c
 
         lax.fori_loop(0, up_s.shape[1] // tile, body, 0)
-        if s + 2 < n // 2:
-            dy_copy(s + 2).start()
+        if s == 0:
+            dy_copy(2).start()
         og = pltpu.make_async_copy(g_s.at[s % 2], g_ref.at[at], put.at[s])
         od = pltpu.make_async_copy(dz_s.at[s % 2], dz_ref.at[at], put2.at[s])
         og.start()
         od.start()
         pending.append((keep, og, od))
 
-    g.run(compute)
+    def fill(k):
+        if k == 1:
+            for s in range(1, n // 2):
+                dy_copy(s).wait()
+
+                def body(t, c):
+                    cols = rows_at(t * tile, tile)
+                    da_s[s - 1, :, cols] = dot_nt(dy_s[s % 2], down_s[cols, :])
+                    return c
+
+                lax.fori_loop(0, up_s.shape[1] // tile, body, 0)
+                if s + 2 < n // 2:
+                    dy_copy(s + 2).start()
+
+    g.run(compute, fill)
     for s, cps in enumerate(pending):
         for cp in (cps if s >= n // 2 - 2 else cps[:1]):
             cp.wait()
@@ -405,11 +426,140 @@
         scratch_shapes=[pltpu.VMEM((seq, hidden), x.dtype), pltpu.VMEM((2, 2 * rows, hidden), x.dtype),
                         pltpu.VMEM(up.shape, x.dtype), pltpu.VMEM(down.shape, x.dtype),
                         pltpu.VMEM((2, 2 * rows, ffn), x.dtype), pltpu.VMEM((2, 2 * rows, ffn), x.dtype),
+                        pltpu.VMEM((chips - 1, 2 * rows, ffn), jnp.float32),
                         dma((13,)), dma((13,)), dma((3,)), dma((chips,)), dma((chips,)), dma((chips,)), dma((chips,))],
         compiler_params=pltpu.CompilerParams(collective_id=cid, has_side_effects=True, vmem_limit_bytes=60 * 2 ** 20),
         cost_estimate=pl.CostEstimate(flops=40 * 10 ** 9, bytes_accessed=3 * seq * hidden, transcendentals=0),
         name="gather_mlp",
     )(x, dy, up, down)
+
+
+class Product:
+    def __init__(self, x, fixed, out, slots, stage, load, store, rows, lhs=None):
+        self.x, self.fixed, self.out, self.slots, self.stage = x, fixed, out, slots, stage
+        self.load, self.store, self.rows, self.lhs = load, store, rows, lhs
+        self.unit = slots.shape[2]
+        self.total = x.shape[1] // self.unit
+
+    def get(self, u):
+        slot = lax.rem(u, 2)
+        return pltpu.make_async_copy(self.x.at[:, rows_at(u * self.unit, self.unit)], self.slots.at[slot], self.load.at[slot])
+
+    def put(self, u):
+        slot = lax.rem(u, 2)
+        at = rows_at(u * self.unit, self.unit)
+        dst = self.out.at[at] if self.rows else self.out.at[:, at]
+        return pltpu.make_async_copy(self.stage.at[slot], dst, self.store.at[slot])
+
+    def run(self, first, last):
+        def body(u, c):
+            slot = lax.rem(u, 2)
+            self.get(u).wait()
+
+            @pl.when(u + 1 < self.total)
+            def _():
+                self.get(u + 1).start()
+
+            @pl.when(u >= 2)
+            def _():
+                self.put(u - 2).wait()
+
+            if self.rows:
+                self.lhs[...] = self.slots[slot].T
+                width = self.fixed.shape[1]
+                for w in range(0, width, 1280):
+                    at = slice(w, min(w + 1280, width))
+                    self.stage[slot, :, at] = dot32(self.lhs[...], self.fixed[:, at]).astype(jnp.bfloat16)
+            else:
+                step = 320
+
+                def part(t, c):
+                    at = rows_at(t * step, step)
+                    self.stage[slot, at, :] = dot32(self.fixed[at, :], self.slots[slot]).astype(jnp.bfloat16)
+                    return c
+
+                lax.fori_loop(0, self.fixed.shape[0] // step, part, 0)
+            self.put(u).start()
+            return c
+
+        lax.fori_loop(first, last, body, 0)
+
+    def finish(self):
+        self.put(self.total - 2).wait()
+        self.put(self.total - 1).wait()
+
+
+def gather_grads_kernel(n, x_ref, w_ref, b_ref, dz_ref, g_ref, dy_ref, full_ref, out_ref, up_ref, down_ref,
+                        buf, w_s, stage, dz_s, dy_s, b_s, g_s, lhs, up_st, down_st,
+                        send, recv, load, store, put, up_l, up_p, down_l, down_p):
+    ring = Ring(n)
+    rows = x_ref.shape[0]
+    loads = [pltpu.make_async_copy(a, b, load.at[i]) for i, (a, b) in
+             enumerate(((x_ref, buf.at[rows_at(ring.me * rows, rows)]), (w_ref, w_s), (dz_ref, dz_s), (dy_ref, dy_s)))]
+    up = Product(b_ref, dz_s, up_ref, b_s, up_st, up_l, up_p, True, lhs)
+    down = Product(g_ref, dy_s, down_ref, g_s, down_st, down_l, down_p, True, lhs)
+    loads[0].start()
+    loads[1].start()
+    up.get(0).start()
+    loads[2].start()
+    down.get(0).start()
+    loads[3].start()
+    ring.barrier()
+    loads[0].wait()
+    g = Gather(ring, buf, send, recv)
+    pending = []
+
+    def compute(chip):
+        s = len(pending)
+        if s == 0:
+            loads[1].wait()
+        at = rows_at(chip * (2 * rows), 2 * rows)
+        keep = pltpu.make_async_copy(buf.at[at], full_ref.at[at], store.at[s])
+        keep.start()
+        stage[s] = dot_nt(w_s[...], buf[at, :]).astype(jnp.bfloat16)
+        out = pltpu.make_async_copy(stage.at[s], out_ref.at[:, at], put.at[s])
+        out.start()
+        pending.append((keep, out))
+
+    def fill(k):
+        mid = up.total // 2
+        if k == 0:
+            loads[2].wait()
+            up.run(0, mid)
+        elif k == 1:
+            up.run(mid, up.total)
+            loads[3].wait()
+            down.run(0, down.total // 2)
+        else:
+            down.run(down.total // 2, down.total)
+
+    g.run(compute, fill)
+    up.finish()
+    down.finish()
+    for pair in pending:
+        for cp in pair:
+            cp.wait()
+
+
+def gather_grads(n, cid, x, w, b1, dz, g, dy, unit=256):
+    rows, hidden = x.shape
+    seq, m, chips, ffn = rows * n, w.shape[0], n // 2, dz.shape[1]
+    dma = pltpu.SemaphoreType.DMA
+    shape = lambda *d: jax.ShapeDtypeStruct(d, x.dtype)
+    vmem = lambda *d: pltpu.VMEM(d, x.dtype)
+    return pl.pallas_call(
+        functools.partial(gather_grads_kernel, n),
+        in_specs=[pl.BlockSpec(memory_space=pl.ANY)] * 6,
+        out_specs=[pl.BlockSpec(memory_space=pl.ANY)] * 4,
+        out_shape=[shape(seq, hidden), shape(m, seq), shape(hidden, ffn), shape(ffn, hidden)],
+        scratch_shapes=[vmem(seq, hidden), vmem(*w.shape), vmem(chips, m, 2 * rows), vmem(seq, ffn), vmem(seq, hidden),
+                        vmem(2, seq, unit), vmem(2, seq, unit), vmem(unit, seq), vmem(2, unit, ffn), vmem(2, unit, hidden),
+                        dma((13,)), dma((13,)), dma((4,)), dma((chips,)), dma((chips,)),
+                        dma((2,)), dma((2,)), dma((2,)), dma((2,))],
+        compiler_params=pltpu.CompilerParams(collective_id=cid, has_side_effects=True, vmem_limit_bytes=60 * 2 ** 20),
+        cost_estimate=pl.CostEstimate(flops=60 * 10 ** 9, bytes_accessed=6 * seq * hidden, transcendentals=0),
+        name="gather_grads",
+    )(x, w, b1, dz, g, dy)
 
 
 def add_rows(dst, start, count, *terms):
@@ -545,6 +695,64 @@
     )(x, w)
 
 
+def scatter_grads_kernel(n, tile, x_ref, w_ref, a_ref, o_ref, d_ref, out_ref, gq_ref, go_ref,
+                         x_s, w_s, lhs, o_s, a_s, d_s, gq_st, go_st, part, pin, mid, fin, send, recv, load, a_l, a_p, d_l, d_p):
+    ring = Ring(n)
+    loads = [pltpu.make_async_copy(a, b, load.at[i]) for i, (a, b) in enumerate(((x_ref, x_s), (w_ref, w_s), (o_ref, o_s)))]
+    for cp in loads:
+        cp.start()
+    wq = Product(a_ref, x_s, gq_ref, a_s, gq_st, a_l, a_p, False)
+    wo = Product(d_ref, o_s, go_ref, d_s, go_st, d_l, d_p, False)
+    wq.get(0).start()
+    wo.get(0).start()
+    ring.barrier()
+    loads[0].wait()
+    loads[1].wait()
+    sc = Scatter(ring, part, pin, mid, fin, send, recv)
+    wide = part.shape[1]
+
+    def product(d):
+        at = rows_at(ring.ahead(d) * wide, wide)
+        lhs[...] = x_s[:, at].T
+
+        def body(t, c):
+            cols = rows_at(t * tile, tile)
+            part[d, :, cols] = dot32(lhs[...], w_s[:, cols]).astype(jnp.bfloat16)
+            return c
+
+        lax.fori_loop(0, w_s.shape[1] // tile, body, 0)
+
+    def filler():
+        loads[2].wait()
+        wq.run(0, wq.total)
+        wo.run(0, wo.total)
+
+    sc.run(product, filler, out_ref)
+    wq.finish()
+    wo.finish()
+
+
+def scatter_grads(n, cid, x, w, a, o, d, tile=512):
+    (m, seq), hidden = x.shape, w.shape[1]
+    rows = seq // n
+    dma = pltpu.SemaphoreType.DMA
+    vmem = lambda *s: pltpu.VMEM(s, x.dtype)
+    any_spec = pl.BlockSpec(memory_space=pl.ANY)
+    return pl.pallas_call(
+        functools.partial(scatter_grads_kernel, n, tile),
+        in_specs=[any_spec] * 5,
+        out_specs=[pl.BlockSpec(memory_space=pltpu.VMEM), any_spec, any_spec],
+        out_shape=[jax.ShapeDtypeStruct((rows, hidden), x.dtype), jax.ShapeDtypeStruct(w.shape, x.dtype),
+                   jax.ShapeDtypeStruct((o.shape[0], hidden), x.dtype)],
+        scratch_shapes=[vmem(*x.shape), vmem(*w.shape), vmem(2 * rows, m), vmem(*o.shape), vmem(2, seq, tile), vmem(2, seq, tile),
+                        vmem(2, m, tile), vmem(2, o.shape[0], tile)]
+        + scatter_scratch(rows, hidden, x.dtype) + [dma((3,)), dma((2,)), dma((2,)), dma((2,)), dma((2,))],
+        compiler_params=pltpu.CompilerParams(collective_id=cid, has_side_effects=True, vmem_limit_bytes=60 * 2 ** 20),
+        cost_estimate=pl.CostEstimate(flops=60 * 10 ** 9, bytes_accessed=6 * seq * hidden, transcendentals=0),
+        name="scatter_grads",
+    )(x, w, a, o, d)
+
+
 def scatter_mlp_kernel(n, tile, dz_ref, up_ref, g_ref, down_ref, out_ref, y_ref,
                        dz_s, w_s, g_s, down_s, part, pin, mid, fin, send, recv, load, ystage, put):
     ring = Ring(n)
@@ -608,11 +816,38 @@
     )(dz, up, g, down)
 
 
-def group_sum(vals, n):
-    total = vals
-    for shift in range(1, n):
-        total = total + lax.ppermute(vals, 'model', [(a, (a + shift) % n) for a in range(n)])
-    return total
+def group_sum_kernel(n, x_ref, out_ref, slots, send, recv):
+    me = lax.axis_index('model')
+    sem = pltpu.get_barrier_semaphore()
+    peers = [lax.rem(me + k, n) for k in range(1, n)]
+    for dev in peers:
+        pl.semaphore_signal(sem, inc=1, device_id={'model': dev}, device_id_type=MESH)
+    pl.semaphore_wait(sem, n - 1)
+    copies = [pltpu.make_async_remote_copy(src_ref=x_ref, dst_ref=slots.at[me], send_sem=send.at[k], recv_sem=recv.at[k],
+                                           device_id={'model': dev}, device_id_type=MESH) for k, dev in enumerate(peers)]
+    for cp in copies:
+        cp.start()
+    slots[me] = x_ref[...]
+    for cp in copies:
+        cp.wait()
+    total = slots[0]
+    for k in range(1, n):
+        total = total + slots[k]
+    out_ref[...] = total.astype(out_ref.dtype)
+
+
+def group_sum(vals, n, cid):
+    dma = pltpu.SemaphoreType.DMA
+    return pl.pallas_call(
+        functools.partial(group_sum_kernel, n),
+        in_specs=[pl.BlockSpec(memory_space=pltpu.VMEM)],
+        out_specs=pl.BlockSpec(memory_space=pltpu.VMEM),
+        out_shape=jax.ShapeDtypeStruct(vals.shape, jnp.bfloat16),
+        scratch_shapes=[pltpu.VMEM((n,) + vals.shape, vals.dtype), dma((n - 1,)), dma((n - 1,))],
+        compiler_params=pltpu.CompilerParams(collective_id=cid, has_side_effects=True),
+        cost_estimate=pl.CostEstimate(flops=10 ** 9, bytes_accessed=vals.size * 4, transcendentals=0),
+        name="group_sum",
+    )(vals)
 
 
 def local_layer(n, hidden_in, seg_ids, gain_attn, w_qkv, w_out, gain_mlp, w_up, w_down, grad_out):
@@ -625,7 +860,6 @@
     first = jnp.sum(seg_ids[0][:, None] < seg_ids[0][None, :], axis=0, dtype=jnp.int32)
     lo = first[::BLK] // BLK
     first = first[None]
-    ein = functools.partial(jnp.einsum, preferred_element_type=jnp.float32)
     gather = lambda a: lax.all_gather(a, 'model', axis=0, tiled=True)
     scatter = lambda a: lax.psum_scatter(a, 'model', scatter_dimension=0, tiled=True)
 
@@ -641,19 +875,15 @@
     d_mlp_in, mlp_part = scatter_mlp(n, 3, d_pre, w_up, act_lo, w_down)
     d_mid_ln, d_gain_mlp = ln2_vjp(d_mlp_in.astype(jnp.float32))
     d_mid = (dy.astype(jnp.float32) + d_mid_ln).astype(jnp.bfloat16)
-    d_mid_full, do_t = gather_t(n, 4, d_mid, wo, heads * hd)
+    d_mid_full, do_t, g_up, g_down = gather_grads(n, 4, d_mid, wo, mlp_in, d_pre, act_lo, grad_full)
     mlp_part, do_t = lax.optimization_barrier((mlp_part, do_t))
     mlp_sum = scatter(mlp_part)
     hidden_out = (mid_loc.astype(jnp.float32) + mlp_sum.astype(jnp.float32)).astype(jnp.bfloat16)
     dqkv_t = attention_bwd(qkv_t, o_t, do_t, lse, lo, first, heads, hd)
-    d_attn_in = scatter_t(n, 5, dqkv_t, wq_t)
-    g_down = ein('sf,sd->fd', act_lo, grad_full).astype(jnp.bfloat16)
-    g_up = ein('sd,sf->df', mlp_in, d_pre).astype(jnp.bfloat16)
-    g_out = ein('es,sd->ed', o_t, d_mid_full).astype(jnp.bfloat16)
-    g_qkv = ein('ns,sd->nd', dqkv_t, attn_in).astype(jnp.bfloat16)
+    d_attn_in, g_qkv, g_out = scatter_grads(n, 5, dqkv_t, wq_t, attn_in, o_t, d_mid_full)
     d_x_ln, d_gain_attn = ln1_vjp(d_attn_in.astype(jnp.float32))
     grad_in = (d_mid.astype(jnp.float32) + d_x_ln).astype(jnp.bfloat16)
-    gain_sums = group_sum(jnp.stack([d_gain_attn, d_gain_mlp]), n).astype(jnp.bfloat16)
+    gain_sums = group_sum(jnp.stack([d_gain_attn, d_gain_mlp]), n, 6)
     g_qkv = jnp.transpose(g_qkv.reshape(heads, 3, hd, hidden), (3, 0, 1, 2))
     return (hidden_out[None], grad_in[None], g_qkv, g_out.reshape(heads, hd, hidden), g_up, g_down,
             gain_sums[0], gain_sums[1])

time: 544 us -> 495 us (0.910)
  matrix products: 59.2 us -> 0 us
  local copies, waits for them, and re-layouts: 2.55 us -> 18.7 us
  starting transfers between devices: 8.09 us -> 0.13 us
    pallas_call x0 -> x3, Pallas kernels: none -> 129 us  [the longest x1 69.3 us: scatter_grads(): pl.pallas_call(functools.partial(scatter_grads_kernel, n, tile), in_specs...]
    pallas_call x2 -> x1, Pallas kernels: 139 us -> 78.4 us  [scatter_t(): pl.pallas_call(functools.partial(scatter_t_kernel, n, tile), in_specs=[pl...]
    dot_general x4 -> x0, matrix products: 59.2 us -> none  [the longest x1 20 us: local_layer(): g_up = ein('sd,sf->df', mlp_in, d_pre).astype(jnp.bfloat16)]
    pallas_call x2 -> x1, Pallas kernels: 108 us -> 55.8 us  [gather_t(): pl.pallas_call(functools.partial(gather_t_kernel, n, tile), in_specs=[pl....]
    unnamed x58 -> x50, local copies, waits for them, and re-layouts: 1.79 us -> 17.1 us
    ppermute x7 -> x0, starting transfers between devices: 7.97 us -> none  [group_sum(): lax.ppermute(vals, 'model', [(a, (a + shift) % n) for a in range(n)])]
    pallas_call x1, Pallas kernels: 63.7 us -> 56.3 us  [mlp(): pl.pallas_call(functools.partial(mlp_kernel, n, tile), in_specs=[pl.Block...]
  transfers between devices with their start and end apart: 9 -> 2, of which waited for: 0 -> 0; matrix products, arithmetic and copies ran while one was open for 13% -> 3% of each run, Pallas kernels for 37% -> 42%
where the time goes in v3:
time: 495 us; the launch traced here: 489 us
  Pallas kernels  428 us (86%)
  other arithmetic  27.7 us (6%)
  local copies, waits for them, and re-layouts  18.7 us (4%)
  between operations  14.6 us (3%)
    pallas_call x1, Pallas kernels, scatter_t(): pl.pallas_call(functools.partial(scatter_t_kernel, n, tile), in_specs=[pl...  78.4 us
    pallas_call x1, Pallas kernels, scatter_grads(): pl.pallas_call(functools.partial(scatter_grads_kernel, n, tile), in_specs...  69.3 us
    pallas_call x1, Pallas kernels, scatter_mlp(): pl.pallas_call(functools.partial(scatter_mlp_kernel, n, tile), in_specs=[...  59.4 us
    pallas_call x1, Pallas kernels, mlp(): pl.pallas_call(functools.partial(mlp_kernel, n, tile), in_specs=[pl.Block...  56.3 us
    pallas_call x1, Pallas kernels, gather_t(): pl.pallas_call(functools.partial(gather_t_kernel, n, tile), in_specs=[pl....  55.8 us
    pallas_call x1, Pallas kernels, gather_grads(): pl.pallas_call(functools.partial(gather_grads_kernel, n), in_specs=[pl.Bl...  51.8 us
    pallas_call x1, Pallas kernels, attention_bwd(): pl.pallas_call(functools.partial(attn_bwd_kernel, heads, hd), grid_spec=p...  31.5 us
    pallas_call x1, Pallas kernels, attention_fwd(): pl.pallas_call(functools.partial(attn_fwd_kernel, heads, hd), grid_spec=p...  17.1 us
  transfers between devices with their start and end apart: 2, of which 0 were waited for; matrix products, arithmetic and copies ran while one was open for 3% of the time, Pallas kernels for 42%

profile of v3, /device:TPU:81, one launch (start us, length us, event | category | flops | bytes accessed | tf_op | source)
XLA Modules:
  0.0 488.7 jit_solution(15924478395501342742)
XLA Ops:
  7.2 0.0 copy-start.3
  7.2 0.0 copy-start.17
  7.2 0.1 all-gather.2.cloned.1.call-start
  7.3 1.7 convert_reduce_fusion.2
  8.9 0.0 copy-start.11
  8.9 1.8 fusion.16
  10.7 0.0 copy-start.15
  10.8 0.6 copy-done.15
  11.3 0.0 copy-done.17
  11.4 0.0 copy-start.9
  11.4 0.6 copy-done.9
  12.0 0.0 copy-done.3
  12.0 1.5 fusion.15.x_ref
  13.5 0.0 copy-done.11
  13.5 0.0 copy-done.13
  13.5 55.8 %gather_t.1 = (bf16[2048,2560]{1,0:T(8,128)(2,1)}, bf16[960,2048]{1,0:T(8,128)(2,1)}) custom-call(bf16[256,2560]{1,0:T(8,128)(2,1)} %fusion.15.x_ref, bf16[960,2560]{1,0:T(8,128)(2,1)} %bitcast.58), custom_call_target="tpu_custom_call" | custom-call | flops 40000000000 | bytes 15728640 | tf_op jit(solution)/shard_map/gather_t/pallas_call | solution.py:322
  69.3 0.1 all-gather.2.cloned.1.call-update
  69.4 0.1 reduce-scatter.2.cloned.1.call-start
  69.5 0.0 copy-done.19
  69.5 1.7 convert_reduce_fusion
  71.2 0.0 copy-start.20
  71.2 0.1 slice.9
  71.3 0.0 copy-done.18
  71.3 0.5 and_select_fusion.lo_ref
  71.8 0.0 copy-done.20
  71.8 17.1 %attn_fwd.1 = (bf16[320,2048]{1,0:T(8,128)(2,1)}, f32[8,2048]{1,0:T(8,128)}) custom-call(s32[8]{0:T(128)} %and_select_fusion.lo_ref, bf16[960,2048]{1,0:T(8,128)(2,1)} %get-tuple-element.29.qkv_ref, s32[1,2048]{1,0:T(1,128)} %bitcast.63), custom_call_target="tpu_custom_call" | custom-call | flops 21474836480 | bytes 3932160 | tf_op jit(solution)/shard_map/attn_fwd/pallas_call | solution.py:99
  89.0 78.4 %scatter_t.1 = bf16[256,2560]{1,0:T(8,128)(2,1)} custom-call(bf16[320,2048]{1,0:T(8,128)(2,1)} %get-tuple-element.30.x_ref.o_ref, bf16[320,2560]{1,0:T(8,128)(2,1)} %bitcast.60), custom_call_target="tpu_custom_call" | custom-call | flops 40000000000 | bytes 15728640 | tf_op jit(solution)/shard_map/scatter_t/pallas_call | solution.py:685
  167.4 1.8 convert_reduce_fusion.1
  169.2 0.5 fusion.21
  169.7 0.5 copy-done
  170.2 1.5 fusion.14.x_ref
  171.8 56.3 %gather_mlp.1 = (bf16[2048,2560]{1,0:T(8,128)(2,1)}, bf16[2048,1280]{1,0:T(8,128)(2,1)}, bf16[2048,1280]{1,0:T(8,128)(2,1)}) custom-call(bf16[256,2560]{1,0:T(8,128)(2,1)} %fusion.14.x_ref, bf16[2048,2560]{1,0:T(8,128)(2,1)} %all-gather.2.cloned.1.call-done.dy_ref, bf16[2560,1280]{1,0:T(8,128)(2,1)} %up_ref.3, bf16[1280,2560]{1,0:T(8,128)(2,1)} %down_ref.3), custom_call_target="tpu_custom_call" | custom-call | flops 40000000000 | bytes 15728640 | tf_op jit(solution)/shard_map/gather_mlp/pallas_call | solution.py:421
  228.0 59.4 %scatter_mlp.1 = (bf16[256,2560]{1,0:T(8,128)(2,1)}, bf16[2048,2560]{1,0:T(8,128)(2,1)}) custom-call(bf16[2048,1280]{1,0:T(8,128)(2,1)} %get-tuple-element.32.dz_ref, bf16[2560,1280]{1,0:T(8,128)(2,1)} %up_ref.3, bf16[2048,1280]{1,0:T(8,128)(2,1)} %get-tuple-element.33.g_ref, bf16[1280,2560]{1,0:T(8,128)(2,1)} %down_ref.3), custom_call_target="tpu_custom_call" | custom-call | flops 60000002048 | bytes 15728640 | tf_op jit(solution)/shard_map/scatter_mlp/pallas_call | solution.py:806
  287.4 0.0 copy-start.1
  287.4 0.0 copy-start.6
  287.4 0.0 copy-start.7
  287.4 2.5 fusion.22
  290.0 0.0 copy-done.1
  290.0 0.0 copy-done.6
  290.0 1.3 fusion.19
  291.3 0.0 copy-done.7
  291.3 2.2 add_convert_fusion.1.x_ref
  293.5 51.8 %gather_grads.1 = (bf16[2048,2560]{1,0:T(8,128)(2,1)}, bf16[320,2048]{1,0:T(8,128)(2,1)}, bf16[2560,1280]{1,0:T(8,128)(2,1)}, bf16[1280,2560]{1,0:T(8,128)(2,1)}) custom-call(bf16[256,2560]{1,0:T(8,128)(2,1)} %add_convert_fusion.1.x_ref, bf16[320,2560]{1,0:T(8,128)(2,1)} %bitcast.61, bf16[2048,2560]{1,0:T(8,128)(2,1)} %get-tuple-element.36.b_ref, ...), custom_call_target="tpu_custom_call" | custom-call | flops 60000002048 | bytes 31457280 | tf_op jit(solution)/shard_map/gather_grads/pallas_call | solution.py:550
  345.3 0.1 reduce-scatter.2.cloned.1.call-update
  345.4 31.5 %attn_bwd.1.x_ref = bf16[960,2048]{1,0:T(8,128)(2,1)} custom-call(s32[8]{0:T(128)} %and_select_fusion.lo_ref, bf16[960,2048]{1,0:T(8,128)(2,1)} %get-tuple-element.29.qkv_ref, bf16[320,2048]{1,0:T(8,128)(2,1)} %get-tuple-element.30.x_ref.o_ref, bf16[320,2048]{1,0:T(8,128)(2,1)} %get-tuple-element.39.do_ref, f32[8,2048]{1,0:T(8,128)} %get-tuple-element.40.lse_ref, ...), custom_call_target="tpu_custom_call" | custom-call | flops 53687091200 | bytes 7864320 | tf_op jit(solution)/shard_map/attn_bwd/pallas_call | solution.py:175
  376.9 69.3 %scatter_grads.1 = (bf16[256,2560]{1,0:T(8,128)(2,1)}, bf16[960,2560]{1,0:T(8,128)(2,1)}, bf16[320,2560]{1,0:T(8,128)(2,1)}) custom-call(bf16[960,2048]{1,0:T(8,128)(2,1)} %attn_bwd.1.x_ref, bf16[960,2560]{1,0:T(8,128)(2,1)} %bitcast.59, bf16[2048,2560]{1,0:T(8,128)(2,1)} %get-tuple-element.41.a_ref, bf16[320,2048]{1,0:T(8,128)(2,1)} %get-tuple-element.30.x_ref.o_ref, ...), custom_call_target="tpu_custom_call" | custom-call | flops 60000002048 | bytes 31457280 | tf_op jit(solution)/shard_map/scatter_grads/pallas_call | solution.py:741
  446.2 0.0 copy-start.16
  446.2 0.0 copy-start.5
  446.2 0.0 copy-start.14
  446.2 0.0 copy-done.4
  446.2 0.0 copy-done.10
  446.2 0.0 copy-done.12
  446.3 2.1 fusion.17
  448.4 1.3 fusion.20
  449.6 0.6 pad_maximum_fusion.x_ref
  450.3 8.0 %group_sum.1 = bf16[2,2560]{1,0:T(2,128)(2,1)} custom-call(f32[2,2560]{1,0:T(2,128)} %pad_maximum_fusion.x_ref), custom_call_target="tpu_custom_call" | custom-call | flops 1000000000 | bytes 20480 | tf_op jit(solution)/shard_map/group_sum/pallas_call | solution.py:841
  458.2 1.4 slice_reduce_fusion
  459.7 4.0 fusion.26
  463.6 2.7 fusion.27
  466.3 5.1 %copy.21 = bf16[2560,4,3,80]{0,3,2,1:T(8,128)(2,1)} copy(bf16[2560,4,3,80]{0,3,2,1:T(8,128)(2,1)} %bitcast.56) | data formatting | bytes 9830400
  471.5 1.2 copy.22
  472.6 6.2 %copy.23 = bf16[2560,1280]{1,0:T(8,128)(2,1)} copy(bf16[2560,1280]{1,0:T(8,128)(2,1)} %get-tuple-element.68) | data formatting | bytes 13107200
  478.8 0.0 slice-done
  478.9 2.8 copy.24
  (32 shorter events, 0.1 us)
Async XLA Ops:
  7.2 4.8 copy-start.3
  7.2 4.2 copy-start.17
  7.2 164.6 %all-gather.2.cloned.1.call-start = ((), (), s32[]{:S(2)}) async-start(), calls=%async_computation.1 | async-start | bytes 11796480 | tf_op jit(solution)/shard_map/all_gather | solution.py:863
  8.9 4.6 copy-start.11
  10.7 0.6 copy-start.15
  11.4 2.1 copy-start.13
  11.4 0.6 copy-start.9
  13.5 56.0 %copy-start.19 = (s32[1,2048]{1,0:T(1,128)S(1)}, s32[1,2048]{1,0:T(1,128)}, u32[]{:S(2)}) copy-start(s32[1,2048]{1,0:T(1,128)} %param.10) | copy-start | bytes 24580
  13.5 57.8 %copy-start.18 = (bf16[2560]{0:T(1024)(128)(2,1)S(1)}, bf16[2560]{0:T(1024)(128)(2,1)}, u32[]{:S(2)}) copy-start(bf16[2560]{0:T(1024)(128)(2,1)} %param.14) | copy-start | bytes 15364
  69.4 394.2 %reduce-scatter.2.cloned.1.call-start = ((), (), s32[]{:S(2)}) async-start(), calls=%async_computation.2 | async-start | bytes 11796480 | tf_op jit(solution)/shard_map/reduce_scatter | solution.py:864
  71.2 0.6 copy-start.20
  169.2 1.1 copy-start
  287.4 2.6 copy-start.1
  287.4 2.6 copy-start.6
  287.4 3.8 copy-start.7
  376.9 69.3 %copy-start.4 = (bf16[1,256,2560]{2,1,0:T(8,128)(2,1)S(1)}, bf16[1,256,2560]{2,1,0:T(8,128)(2,1)}, u32[]{:S(2)}) copy-start(bf16[1,256,2560]{2,1,0:T(8,128)(2,1)} %param.9) | copy-start | bytes 3932164
  376.9 69.3 %copy-start.10 = (f32[2560]{0:T(1024)S(1)}, f32[2560]{0:T(1024)}, u32[]{:S(2)}) copy-start(f32[2560]{0:T(1024)} %copy-done.9) | copy-start | bytes 30724
  376.9 69.3 %copy-start.12 = (f32[256]{0:T(256)S(1)}, f32[256]{0:T(256)}, u32[]{:S(2)}) copy-start(f32[256]{0:T(256)} %copy-done.11) | copy-start | bytes 3076
  446.2 2.1 copy-start.16
  446.2 2.1 copy-start.5
  446.2 2.1 copy-start.14
  459.7 4.0 copy-start.2
  466.3 5.1 %copy-start.8 = (bf16[320,2560]{1,0:T(8,128)(2,1)S(1)}, bf16[320,2560]{1,0:T(8,128)(2,1)}, u32[]{:S(2)}) copy-start(bf16[320,2560]{1,0:T(8,128)(2,1)} %get-tuple-element.45) | copy-start | bytes 4915204
  466.3 12.5 %slice-start = ((s8[6553600]{0:T(1024)(128)(4,1)}), s8[4194304]{0:T(1024)(128)(4,1)S(1)}, s32[]{:S(2)}) async-start(s8[6553600]{0:T(1024)(128)(4,1)} %bitcast.53), calls=%async_computation.3 | async-start | bytes 8388608
  472.6 6.2 %slice-start.1 = ((s8[6553600]{0:T(1024)(128)(4,1)}), s8[2359296]{0:T(1024)(128)(4,1)S(1)}, s32[]{:S(2)}) async-start(s8[6553600]{0:T(1024)(128)(4,1)} %bitcast.53), calls=%async_computation.4 | async-start | bytes 4718592
Sparse Core Ops, SparseCore 0:
  69.5 81.8 all-gather.1
  345.5 80.7 reduce-scatter.1

commit v4 on v3

--- a/solution.py
+++ b/solution.py
@@ -115,7 +115,7 @@
     )(lo, qkv_t, first)
 
 
-def attn_bwd_kernel(heads, hd, lo_ref, qkv_ref, o_ref, do_ref, lse_ref, first_ref, d_ref,
+def attn_bwd_kernel(heads, hd, lo_ref, qkv_ref, o_ref, do_ref, lse_ref, first_ref, up_ref, down_ref, d_ref, up_out, down_out,
                     k_s, v_s, dq_s, dk_s, dv_s):
     i = pl.program_id(0)
     seq = qkv_ref.shape[1]
@@ -131,6 +131,8 @@
                 k_s[h, c, :] = qkv_ref[(3 * h + 1) * hd:(3 * h + 2) * hd, c].T
                 v_s[h, c, :] = qkv_ref[(3 * h + 2) * hd:(3 * h + 3) * hd, c].T
 
+    up_out[...] = up_ref[...]
+    down_out[...] = down_ref[...]
     lo = lo_ref[i]
     cols = pl.ds(pl.multiple_of(i * BLK, BLK), BLK)
     first_row = first_ref[0:1, cols]
@@ -167,28 +169,29 @@
             d_ref[(3 * h + 2) * hd:(3 * h + 3) * hd, :] = dv_s[h].astype(jnp.bfloat16)
 
 
-def attention_bwd(qkv_t, o_t, do_t, lse, lo, first, heads, hd):
+def attention_bwd(qkv_t, o_t, do_t, lse, lo, first, g_up, g_down, heads, hd):
     seq = qkv_t.shape[1]
     nb = seq // BLK
     flops = 10 * heads * seq * seq * hd // 2
     blk = lambda rows: pl.BlockSpec((rows, BLK), lambda i, lo: (0, i))
+    through = [pl.BlockSpec((a.shape[0] // nb, a.shape[1]), lambda i, lo: (i, 0)) for a in (g_up, g_down)]
     return pl.pallas_call(
         functools.partial(attn_bwd_kernel, heads, hd),
         grid_spec=pltpu.PrefetchScalarGridSpec(
             num_scalar_prefetch=1, grid=(nb,),
             in_specs=[pl.BlockSpec(qkv_t.shape, lambda i, lo: (0, 0)), blk(heads * hd), blk(heads * hd), blk(8),
-                      pl.BlockSpec((1, seq), lambda i, lo: (0, 0))],
-            out_specs=pl.BlockSpec(qkv_t.shape, lambda i, lo: (0, 0)),
+                      pl.BlockSpec((1, seq), lambda i, lo: (0, 0))] + through,
+            out_specs=[pl.BlockSpec(qkv_t.shape, lambda i, lo: (0, 0))] + through,
             scratch_shapes=[pltpu.VMEM((heads, seq, hd), jnp.bfloat16),
                             pltpu.VMEM((heads, seq, hd), jnp.bfloat16),
                             pltpu.VMEM((heads, hd, BLK), jnp.float32),
                             pltpu.VMEM((heads, hd, seq), jnp.float32),
                             pltpu.VMEM((heads, hd, seq), jnp.float32)]),
-        out_shape=jax.ShapeDtypeStruct(qkv_t.shape, jnp.bfloat16),
+        out_shape=[jax.ShapeDtypeStruct(a.shape, jnp.bfloat16) for a in (qkv_t, g_up, g_down)],
         compiler_params=pltpu.CompilerParams(vmem_limit_bytes=56 * 2 ** 20),
         cost_estimate=pl.CostEstimate(flops=8 * flops, bytes_accessed=4 * qkv_t.size, transcendentals=0),
         name="attn_bwd",
-    )(lo, qkv_t, o_t, do_t, lse, first)
+    )(lo, qkv_t, o_t, do_t, lse, first, g_up, g_down)
 
 
 def dot_nt(a, b):
@@ -206,11 +209,12 @@
         self.prev = lax.rem(self.me + n - 2, n)
         self.opp = lax.rem(self.me + n // 2, n)
 
-    def barrier(self):
+    def barrier(self, peers=None):
         sem = pltpu.get_barrier_semaphore()
-        for dev in (self.partner, self.next, self.prev):
+        peers = peers or (self.partner, self.next, self.prev)
+        for dev in peers:
             pl.semaphore_signal(sem, inc=1, device_id={'model': dev}, device_id_type=MESH)
-        pl.semaphore_wait(sem, 3)
+        pl.semaphore_wait(sem, len(peers))
 
     def ahead(self, d):
         return lax.rem(self.chip + d, self.n // 2)
@@ -605,45 +609,97 @@
         self.arrived(d)
         add_rows(self.part.at[d], self.own, self.rows, (self.pin.at[d], 0))
 
-    def run(self, product, filler, out_ref):
+    def run(self, product, filler, emit):
         h = self.half
-        product(2)
+        product(2, self.rows - self.own, self.rows, True)
         self.start(2)
-        product(1)
-        self.start(1)
+        product(2, self.own, self.rows, False)
         self.join(2)
         self.start(4)
         self.start(5)
-        product(3)
-        self.start(3)
+        for d in (1, 3):
+            product(d, 0, 2 * self.rows, False)
+            self.start(d)
         self.join(1)
         self.start(6)
         self.join(3)
         self.start(8)
-        product(0)
+        product(0, 0, 2 * self.rows, False)
         self.start(0)
-        self.join(0)
         self.arrived(4)
         add_rows(self.part.at[1], self.own, h, (self.mid.at[0], 0))
         self.start(7)
         self.arrived(5)
         add_rows(self.part.at[3], self.own + h, h, (self.mid.at[1], 0))
         self.start(9)
+        self.join(0)
         filler()
         for k in (6, 7, 8, 9):
             self.arrived(k)
-        step = 32
+        step = 16
 
         def body(i, c):
             at = rows_at(i * step, step)
             total = self.part[0, rows_at(self.own + i * step, step), :].astype(jnp.float32)
             total = total + self.fin[0, at, :].astype(jnp.float32) + self.fin[1, at, :].astype(jnp.float32)
-            out_ref[at, :] = total.astype(jnp.bfloat16)
+            emit(at, total.astype(jnp.bfloat16))
             return c
 
         lax.fori_loop(0, self.rows // step, body, 0)
         for k in range(10):
             self.copy(k).wait_send()
+
+
+def normalized(x):
+    mean = jnp.mean(x, axis=-1, keepdims=True)
+    cen = x - mean
+    rstd = lax.rsqrt(jnp.mean(cen * cen, axis=-1, keepdims=True) + LN_EPS)
+    return cen * rstd, rstd
+
+
+def norm_backward(hat, rstd, gain, d):
+    dh = d * gain
+    return rstd * (dh - jnp.mean(dh, axis=-1, keepdims=True) - hat * jnp.mean(dh * hat, axis=-1, keepdims=True))
+
+
+def fold_rows(v):
+    return v[:8, :] + v[8:, :]
+
+
+class Weights:
+    def __init__(self, src, dst, sem, tile, rows):
+        self.src, self.dst, self.sem, self.tile, self.rows = src, dst, sem, tile, rows
+        self.count = src.shape[0 if rows else 1] // tile
+
+    def copy(self, t):
+        at = rows_at(t * self.tile, self.tile)
+        if self.rows:
+            return pltpu.make_async_copy(self.src.at[at], self.dst.at[at], self.sem.at[t])
+        return pltpu.make_async_copy(self.src.at[:, at], self.dst.at[:, at], self.sem.at[t])
+
+    def start(self):
+        for t in range(self.count):
+            self.copy(t).start()
+
+
+def product_t(ring, tile, x_s, weights, lhs, part):
+    wide = part.shape[1]
+
+    def product(d, row0, count, first):
+        if first or d != 2:
+            lhs[...] = x_s[:, rows_at(ring.ahead(d) * wide, wide)].T
+        at = rows_at(row0, count)
+
+        def body(t, c):
+            cols = rows_at(t * tile, tile)
+            if first:
+                weights.copy(t).wait()
+            part[d, at, cols] = dot32(lhs[at, :], weights.dst[:, cols]).astype(jnp.bfloat16)
+            return c
+
+        lax.fori_loop(0, weights.count, body, 0)
+
+    return product
 
 
 def scatter_scratch(rows, hidden, dtype):
@@ -652,134 +708,182 @@
             pltpu.VMEM((2, rows // 2, hidden), dtype), pltpu.VMEM((2, rows, hidden), dtype), dma((10,)), dma((10,))]
 
 
-def scatter_t_kernel(n, tile, x_ref, w_ref, out_ref, x_s, w_s, lhs, part, pin, mid, fin, send, recv, load):
+def scatter_norm_kernel(n, tile, x_ref, w_ref, res_ref, gain_ref, mid_ref, norm_ref,
+                        x_s, w_s, lhs, res_s, part, pin, mid, fin, send, recv, load, wl):
     ring = Ring(n)
-    cx = pltpu.make_async_copy(x_ref, x_s, load.at[0])
-    cx.start()
-    cw = pltpu.make_async_copy(w_ref, w_s, load.at[1])
-    cw.start()
+    loads = [pltpu.make_async_copy(a, b, load.at[i]) for i, (a, b) in enumerate(((x_ref, x_s), (res_ref, res_s)))]
+    weights = Weights(w_ref, w_s, wl, tile, False)
+    loads[0].start()
+    weights.start()
+    loads[1].start()
     ring.barrier()
-    cx.wait()
-    cw.wait()
+    loads[0].wait()
     sc = Scatter(ring, part, pin, mid, fin, send, recv)
-    wide = part.shape[1]
-
-    def product(d):
-        at = rows_at(ring.ahead(d) * wide, wide)
-        lhs[...] = x_s[:, at].T
-
-        def body(t, c):
-            cols = rows_at(t * tile, tile)
-            part[d, :, cols] = dot32(lhs[...], w_s[:, cols]).astype(jnp.bfloat16)
-            return c
-
-        lax.fori_loop(0, w_s.shape[1] // tile, body, 0)
-
-    sc.run(product, lambda: None, out_ref)
-
-
-def scatter_t(n, cid, x, w, tile=512):
+
+    def emit(at, total):
+        x1 = (res_s[at, :].astype(jnp.float32) + total.astype(jnp.float32)).astype(jnp.bfloat16)
+        mid_ref[at, :] = x1
+        norm_ref[at, :] = (normalized(x1.astype(jnp.float32))[0] * gain_ref[...]).astype(jnp.bfloat16)
+
+    sc.run(product_t(ring, tile, x_s, weights, lhs, part), lambda: loads[1].wait(), emit)
+
+
+def scatter_norm(n, cid, x, w, res, gain, tile=512):
     (m, seq), hidden = x.shape, w.shape[1]
     rows = seq // n
     dma = pltpu.SemaphoreType.DMA
+    vmem = lambda *d: pltpu.VMEM(d, x.dtype)
+    any_spec, vm = pl.BlockSpec(memory_space=pl.ANY), pl.BlockSpec(memory_space=pltpu.VMEM)
     return pl.pallas_call(
-        functools.partial(scatter_t_kernel, n, tile),
-        in_specs=[pl.BlockSpec(memory_space=pl.ANY)] * 2,
-        out_specs=pl.BlockSpec(memory_space=pltpu.VMEM),
-        out_shape=jax.ShapeDtypeStruct((rows, hidden), x.dtype),
-        scratch_shapes=[pltpu.VMEM(x.shape, x.dtype), pltpu.VMEM(w.shape, x.dtype), pltpu.VMEM((2 * rows, m), x.dtype)]
-        + scatter_scratch(rows, hidden, x.dtype) + [dma((2,))],
+        functools.partial(scatter_norm_kernel, n, tile),
+        in_specs=[any_spec] * 3 + [vm],
+        out_specs=[vm] * 2,
+        out_shape=[jax.ShapeDtypeStruct((rows, hidden), x.dtype)] * 2,
+        scratch_shapes=[vmem(*x.shape), vmem(*w.shape), vmem(2 * rows, m), vmem(rows, hidden)]
+        + scatter_scratch(rows, hidden, x.dtype) + [dma((2,)), dma((hidden // tile,))],
         compiler_params=pltpu.CompilerParams(collective_id=cid, has_side_effects=True, vmem_limit_bytes=60 * 2 ** 20),
         cost_estimate=pl.CostEstimate(flops=40 * 10 ** 9, bytes_accessed=3 * seq * hidden, transcendentals=0),
-        name="scatter_t",
-    )(x, w)
-
-
-def scatter_grads_kernel(n, tile, x_ref, w_ref, a_ref, o_ref, d_ref, out_ref, gq_ref, go_ref,
-                         x_s, w_s, lhs, o_s, a_s, d_s, gq_st, go_st, part, pin, mid, fin, send, recv, load, a_l, a_p, d_l, d_p):
+        name="scatter_norm",
+    )(x, w, res, gain)
+
+
+def scatter_grads_kernel(n, tile, x_ref, w_ref, a_ref, o_ref, d_ref, res_ref, dmid_ref, gain_ref, dg2_ref,
+                         out_ref, gq_ref, go_ref, sums_ref,
+                         x_s, w_s, lhs, o_s, a_s, d_s, gq_st, go_st, res_s, dmid_s, acc, mine, slots,
+                         part, pin, mid, fin, send, recv, load, wl, a_l, a_p, d_l, d_p, gsend, grecv):
     ring = Ring(n)
-    loads = [pltpu.make_async_copy(a, b, load.at[i]) for i, (a, b) in enumerate(((x_ref, x_s), (w_ref, w_s), (o_ref, o_s)))]
-    for cp in loads:
-        cp.start()
+    peers = [lax.rem(ring.me + k, n) for k in range(1, n)]
+    loads = [pltpu.make_async_copy(a, b, load.at[i]) for i, (a, b) in
+             enumerate(((x_ref, x_s), (o_ref, o_s), (res_ref, res_s), (dmid_ref, dmid_s)))]
+    weights = Weights(w_ref, w_s, wl, tile, False)
+    loads[0].start()
+    weights.start()
     wq = Product(a_ref, x_s, gq_ref, a_s, gq_st, a_l, a_p, False)
     wo = Product(d_ref, o_s, go_ref, d_s, go_st, d_l, d_p, False)
+    ring.barrier(peers)
+    for cp in loads[1:]:
+        cp.start()
     wq.get(0).start()
     wo.get(0).start()
-    ring.barrier()
     loads[0].wait()
-    loads[1].wait()
     sc = Scatter(ring, part, pin, mid, fin, send, recv)
-    wide = part.shape[1]
-
-    def product(d):
-        at = rows_at(ring.ahead(d) * wide, wide)
-        lhs[...] = x_s[:, at].T
-
-        def body(t, c):
-            cols = rows_at(t * tile, tile)
-            part[d, :, cols] = dot32(lhs[...], w_s[:, cols]).astype(jnp.bfloat16)
-            return c
-
-        lax.fori_loop(0, w_s.shape[1] // tile, body, 0)
+    acc[...] = jnp.zeros_like(acc)
 
     def filler():
-        loads[2].wait()
+        loads[1].wait()
         wq.run(0, wq.total)
         wo.run(0, wo.total)
-
-    sc.run(product, filler, out_ref)
+        loads[2].wait()
+        loads[3].wait()
+
+    def emit(at, total):
+        hat, _ = normalized(res_s[at, :].astype(jnp.float32))
+        out_ref[at, :] = total
+        acc[...] += fold_rows(total.astype(jnp.float32) * hat)
+
+    sc.run(product_t(ring, tile, x_s, weights, lhs, part), filler, emit)
+    mine[0:1, :] = jnp.sum(acc[...], axis=0, keepdims=True)
+    mine[1:2, :] = dg2_ref[...]
+    step = 16
+
+    def body(i, c):
+        at = rows_at(i * step, step)
+        hat, rstd = normalized(res_s[at, :].astype(jnp.float32))
+        dx = norm_backward(hat, rstd, gain_ref[...], out_ref[at, :].astype(jnp.float32))
+        out_ref[at, :] = (dmid_s[at, :].astype(jnp.float32) + dx).astype(jnp.bfloat16)
+        return c
+
+    steps = out_ref.shape[0] // step
+    lax.fori_loop(0, steps // 4, body, 0)
+    copies = [pltpu.make_async_remote_copy(src_ref=mine, dst_ref=slots.at[ring.me], send_sem=gsend.at[k], recv_sem=grecv.at[k],
+                                           device_id={'model': dev}, device_id_type=MESH) for k, dev in enumerate(peers)]
+    for cp in copies:
+        cp.start()
+    slots[ring.me] = mine[...]
+    lax.fori_loop(steps // 4, steps, body, 0)
     wq.finish()
     wo.finish()
-
-
-def scatter_grads(n, cid, x, w, a, o, d, tile=512):
+    for cp in copies:
+        cp.wait()
+    total = slots[0]
+    for k in range(1, n):
+        total = total + slots[k]
+    sums_ref[...] = total.astype(jnp.bfloat16)
+
+
+def scatter_grads(n, cid, x, w, a, o, d, res, d_mid, gain, dg2, tile=512):
     (m, seq), hidden = x.shape, w.shape[1]
     rows = seq // n
     dma = pltpu.SemaphoreType.DMA
     vmem = lambda *s: pltpu.VMEM(s, x.dtype)
-    any_spec = pl.BlockSpec(memory_space=pl.ANY)
+    any_spec, vm = pl.BlockSpec(memory_space=pl.ANY), pl.BlockSpec(memory_space=pltpu.VMEM)
     return pl.pallas_call(
         functools.partial(scatter_grads_kernel, n, tile),
-        in_specs=[any_spec] * 5,
-        out_specs=[pl.BlockSpec(memory_space=pltpu.VMEM), any_spec, any_spec],
+        in_specs=[any_spec] * 7 + [vm] * 2,
+        out_specs=[vm, any_spec, any_spec, vm],
         out_shape=[jax.ShapeDtypeStruct((rows, hidden), x.dtype), jax.ShapeDtypeStruct(w.shape, x.dtype),
-                   jax.ShapeDtypeStruct((o.shape[0], hidden), x.dtype)],
+                   jax.ShapeDtypeStruct((o.shape[0], hidden), x.dtype), jax.ShapeDtypeStruct((2, hidden), x.dtype)],
         scratch_shapes=[vmem(*x.shape), vmem(*w.shape), vmem(2 * rows, m), vmem(*o.shape), vmem(2, seq, tile), vmem(2, seq, tile),
-                        vmem(2, m, tile), vmem(2, o.shape[0], tile)]
-        + scatter_scratch(rows, hidden, x.dtype) + [dma((3,)), dma((2,)), dma((2,)), dma((2,)), dma((2,))],
-        compiler_params=pltpu.CompilerParams(collective_id=cid, has_side_effects=True, vmem_limit_bytes=60 * 2 ** 20),
+                        vmem(2, m, tile), vmem(2, o.shape[0], tile), vmem(rows, hidden), vmem(rows, hidden),
+                        pltpu.VMEM((8, hidden), jnp.float32), pltpu.VMEM((2, hidden), jnp.float32),
+                        pltpu.VMEM((n, 2, hidden), jnp.float32)]
+        + scatter_scratch(rows, hidden, x.dtype)
+        + [dma((4,)), dma((hidden // tile,)), dma((2,)), dma((2,)), dma((2,)), dma((2,)), dma((n - 1,)), dma((n - 1,))],
+        compiler_params=pltpu.CompilerParams(collective_id=cid, has_side_effects=True, vmem_limit_bytes=63 * 2 ** 20),
         cost_estimate=pl.CostEstimate(flops=60 * 10 ** 9, bytes_accessed=6 * seq * hidden, transcendentals=0),
         name="scatter_grads",
-    )(x, w, a, o, d)
-
-
-def scatter_mlp_kernel(n, tile, dz_ref, up_ref, g_ref, down_ref, out_ref, y_ref,
-                       dz_s, w_s, g_s, down_s, part, pin, mid, fin, send, recv, load, ystage, put):
+    )(x, w, a, o, d, res, d_mid, gain, dg2)
+
+
+def scatter_mlp_kernel(n, tile, dz_ref, up_ref, g_ref, down_ref, res_ref, dy_ref, gain_ref, out_ref, y_ref, dg_ref,
+                       dz_s, w_s, g_s, down_s, res_s, dy_s, acc, part, pin, mid, fin, send, recv, load, wl, zl, ystage, put):
     ring = Ring(n)
     loads = [pltpu.make_async_copy(a, b, load.at[i]) for i, (a, b) in
-             enumerate(((dz_ref, dz_s), (up_ref, w_s), (g_ref, g_s), (down_ref, down_s)))]
-    for cp in loads:
-        cp.start()
-    ring.barrier()
-    loads[0].wait()
-    loads[1].wait()
-    sc = Scatter(ring, part, pin, mid, fin, send, recv)
+             enumerate(((res_ref, res_s), (dy_ref, dy_s), (g_ref, g_s), (down_ref, down_s)))]
     wide = part.shape[1]
     hidden = part.shape[2]
 
-    def product(d):
-        at = rows_at(ring.ahead(d) * wide, wide)
+    def dz_at(d):
+        return rows_at(ring.ahead(d) * wide, wide)
+
+    dz_loads = [pltpu.make_async_copy(dz_ref.at[dz_at(d)], dz_s.at[dz_at(d)], zl.at[d]) for d in range(4)]
+    weights = Weights(up_ref, w_s, wl, tile, True)
+    dz_loads[2].start()
+    weights.start()
+    ring.barrier()
+    for d in (1, 3, 0):
+        dz_loads[d].start()
+    sc = Scatter(ring, part, pin, mid, fin, send, recv)
+    acc[...] = jnp.zeros_like(acc)
+
+    def product(d, row0, count, first):
+        if first or d != 2:
+            dz_loads[d].wait()
+        if d == 3:
+            for cp in loads:
+                cp.start()
+        src = rows_at(ring.ahead(d) * wide + row0, count, 256)
+        at = rows_at(row0, count, 256)
 
         def body(t, c):
             cols = rows_at(t * tile, tile)
-            part[d, :, cols] = dot_nt(dz_s[at, :], w_s[cols, :]).astype(jnp.bfloat16)
+            if first:
+                weights.copy(t).wait()
+            part[d, at, cols] = dot_nt(dz_s[src, :], w_s[cols, :]).astype(jnp.bfloat16)
             return c
 
         lax.fori_loop(0, hidden // tile, body, 0)
 
+    def emit(at, total):
+        d = total.astype(jnp.float32)
+        hat, rstd = normalized(res_s[at, :].astype(jnp.float32))
+        dx = norm_backward(hat, rstd, gain_ref[...], d)
+        out_ref[at, :] = (dy_s[at, :].astype(jnp.float32) + dx).astype(jnp.bfloat16)
+        acc[...] += fold_rows(d * hat)
+
     def filler():
-        loads[2].wait()
-        loads[3].wait()
+        for cp in loads:
+            cp.wait()
         puts = []
         for q in range(n // 2):
             if q >= 2:
@@ -796,58 +900,28 @@
         for cp in puts[-2:]:
             cp.wait()
 
-    sc.run(product, filler, out_ref)
-
-
-def scatter_mlp(n, cid, dz, up, g, down, tile=512):
+    sc.run(product, filler, emit)
+    dg_ref[...] = jnp.sum(acc[...], axis=0, keepdims=True)
+
+
+def scatter_mlp(n, cid, dz, up, g, down, res, dy, gain, tile=512):
     (seq, ffn), hidden = dz.shape, down.shape[1]
     rows = seq // n
     dma = pltpu.SemaphoreType.DMA
+    any_spec, vm = pl.BlockSpec(memory_space=pl.ANY), pl.BlockSpec(memory_space=pltpu.VMEM)
     return pl.pallas_call(
         functools.partial(scatter_mlp_kernel, n, tile),
-        in_specs=[pl.BlockSpec(memory_space=pl.ANY)] * 4,
-        out_specs=[pl.BlockSpec(memory_space=pltpu.VMEM), pl.BlockSpec(memory_space=pl.ANY)],
-        out_shape=[jax.ShapeDtypeStruct((rows, hidden), dz.dtype), jax.ShapeDtypeStruct((seq, hidden), dz.dtype)],
-        scratch_shapes=[pltpu.VMEM(a.shape, a.dtype) for a in (dz, up, g, down)]
-        + scatter_scratch(rows, hidden, dz.dtype) + [dma((4,)), pltpu.VMEM((2, 2 * rows, hidden), dz.dtype), dma((n // 2,))],
+        in_specs=[any_spec] * 6 + [vm],
+        out_specs=[vm, any_spec, vm],
+        out_shape=[jax.ShapeDtypeStruct((rows, hidden), dz.dtype), jax.ShapeDtypeStruct((seq, hidden), dz.dtype),
+                   jax.ShapeDtypeStruct((1, hidden), jnp.float32)],
+        scratch_shapes=[pltpu.VMEM(a.shape, a.dtype) for a in (dz, up, g, down, res, dy)]
+        + [pltpu.VMEM((8, hidden), jnp.float32)] + scatter_scratch(rows, hidden, dz.dtype)
+        + [dma((4,)), dma((hidden // tile,)), dma((4,)), pltpu.VMEM((2, 2 * rows, hidden), dz.dtype), dma((n // 2,))],
         compiler_params=pltpu.CompilerParams(collective_id=cid, has_side_effects=True, vmem_limit_bytes=63 * 2 ** 20),
         cost_estimate=pl.CostEstimate(flops=60 * 10 ** 9, bytes_accessed=3 * seq * hidden, transcendentals=0),
         name="scatter_mlp",
-    )(dz, up, g, down)
-
-
-def group_sum_kernel(n, x_ref, out_ref, slots, send, recv):
-    me = lax.axis_index('model')
-    sem = pltpu.get_barrier_semaphore()
-    peers = [lax.rem(me + k, n) for k in range(1, n)]
-    for dev in peers:
-        pl.semaphore_signal(sem, inc=1, device_id={'model': dev}, device_id_type=MESH)
-    pl.semaphore_wait(sem, n - 1)
-    copies = [pltpu.make_async_remote_copy(src_ref=x_ref, dst_ref=slots.at[me], send_sem=send.at[k], recv_sem=recv.at[k],
-                                           device_id={'model': dev}, device_id_type=MESH) for k, dev in enumerate(peers)]
-    for cp in copies:
-        cp.start()
-    slots[me] = x_ref[...]
-    for cp in copies:
-        cp.wait()
-    total = slots[0]
-    for k in range(1, n):
-        total = total + slots[k]
-    out_ref[...] = total.astype(out_ref.dtype)
-
-
-def group_sum(vals, n, cid):
-    dma = pltpu.SemaphoreType.DMA
-    return pl.pallas_call(
-        functools.partial(group_sum_kernel, n),
-        in_specs=[pl.BlockSpec(memory_space=pltpu.VMEM)],
-        out_specs=pl.BlockSpec(memory_space=pltpu.VMEM),
-        out_shape=jax.ShapeDtypeStruct(vals.shape, jnp.bfloat16),
-        scratch_shapes=[pltpu.VMEM((n,) + vals.shape, vals.dtype), dma((n - 1,)), dma((n - 1,))],
-        compiler_params=pltpu.CompilerParams(collective_id=cid, has_side_effects=True),
-        cost_estimate=pl.CostEstimate(flops=10 ** 9, bytes_accessed=vals.size * 4, transcendentals=0),
-        name="group_sum",
-    )(vals)
+    )(dz, up, g, down, res, dy, gain)
 
 
 def local_layer(n, hidden_in, seg_ids, gain_attn, w_qkv, w_out, gain_mlp, w_up, w_down, grad_out):
@@ -863,27 +937,22 @@
     gather = lambda a: lax.all_gather(a, 'model', axis=0, tiled=True)
     scatter = lambda a: lax.psum_scatter(a, 'model', scatter_dimension=0, tiled=True)
 
-    ln1_out, ln1_vjp = jax.vjp(layer_norm, x_f32, gain_attn.astype(jnp.float32))
-    attn_in, qkv_t = gather_t(n, 0, ln1_out.astype(jnp.bfloat16), wq_t, 320)
+    gain1 = gain_attn.astype(jnp.float32)
+    gain2 = gain_mlp.astype(jnp.float32)[None]
+    attn_in, qkv_t = gather_t(n, 0, layer_norm(x_f32, gain1).astype(jnp.bfloat16), wq_t, 320)
     dy_late, qkv_t = lax.optimization_barrier((dy, qkv_t))
     grad_full = gather(dy_late)
     o_t, lse = attention_fwd(qkv_t, lo, first, heads, hd)
-    attn_sum = scatter_t(n, 1, o_t, wo)
-    mid_loc = (x_f32 + attn_sum.astype(jnp.float32)).astype(jnp.bfloat16)
-    ln2_out, ln2_vjp = jax.vjp(layer_norm, mid_loc.astype(jnp.float32), gain_mlp.astype(jnp.float32))
-    mlp_in, act_lo, d_pre = mlp(n, 2, ln2_out.astype(jnp.bfloat16), grad_full, w_up, w_down)
-    d_mlp_in, mlp_part = scatter_mlp(n, 3, d_pre, w_up, act_lo, w_down)
-    d_mid_ln, d_gain_mlp = ln2_vjp(d_mlp_in.astype(jnp.float32))
-    d_mid = (dy.astype(jnp.float32) + d_mid_ln).astype(jnp.bfloat16)
+    mid_loc, norm2 = scatter_norm(n, 1, o_t, wo, hidden_in[0], gain2)
+    mlp_in, act_lo, d_pre = mlp(n, 2, norm2, grad_full, w_up, w_down)
+    d_mid, mlp_part, d_gain_mlp = scatter_mlp(n, 3, d_pre, w_up, act_lo, w_down, mid_loc, dy, gain2)
     d_mid_full, do_t, g_up, g_down = gather_grads(n, 4, d_mid, wo, mlp_in, d_pre, act_lo, grad_full)
     mlp_part, do_t = lax.optimization_barrier((mlp_part, do_t))
     mlp_sum = scatter(mlp_part)
     hidden_out = (mid_loc.astype(jnp.float32) + mlp_sum.astype(jnp.float32)).astype(jnp.bfloat16)
-    dqkv_t = attention_bwd(qkv_t, o_t, do_t, lse, lo, first, heads, hd)
-    d_attn_in, g_qkv, g_out = scatter_grads(n, 5, dqkv_t, wq_t, attn_in, o_t, d_mid_full)
-    d_x_ln, d_gain_attn = ln1_vjp(d_attn_in.astype(jnp.float32))
-    grad_in = (d_mid.astype(jnp.float32) + d_x_ln).astype(jnp.bfloat16)
-    gain_sums = group_sum(jnp.stack([d_gain_attn, d_gain_mlp]), n, 6)
+    dqkv_t, g_up, g_down = attention_bwd(qkv_t, o_t, do_t, lse, lo, first, g_up, g_down, heads, hd)
+    grad_in, g_qkv, g_out, gain_sums = scatter_grads(n, 5, dqkv_t, wq_t, attn_in, o_t, d_mid_full, hidden_in[0], d_mid,
+                                                     gain1[None], d_gain_mlp)
     g_qkv = jnp.transpose(g_qkv.reshape(heads, 3, hd, hidden), (3, 0, 1, 2))
     return (hidden_out[None], grad_in[None], g_qkv, g_out.reshape(heads, hd, hidden), g_up, g_down,
             gain_sums[0], gain_sums[1])

time: 495 us -> 471 us (0.952)
  other arithmetic: 27.7 us -> 10.4 us
  local copies, waits for them, and re-layouts: 18.7 us -> 8.28 us
    unnamed x50 -> x21, local copies, waits for them, and re-layouts: 17.1 us -> 5.49 us
    reduce_sum x4 -> x0, other arithmetic: 7.13 us -> none  [layer_norm(): return centered * lax.rsqrt(variance + LN_EPS) * gain_f32]
    pallas_call x1, Pallas kernels: 69.3 us -> 75.3 us  [scatter_grads(): pl.pallas_call(functools.partial(scatter_grads_kernel, n, tile), in_specs...]
    pallas_call x2 -> x1, Pallas kernels: 86.4 us -> 81.7 us  [scatter_norm(): pl.pallas_call(functools.partial(scatter_norm_kernel, n, tile), in_specs=...]
  transfers between devices with their start and end apart: 2 -> 2, of which waited for: 0 -> 0; matrix products, arithmetic and copies ran while one was open for 3% -> 1% of each run, Pallas kernels for 42% -> 45%
where the time goes in v4:
time: 471 us; the launch traced here: 466 us
  Pallas kernels  432 us (92%)
  between operations  14.7 us (3%)
  other arithmetic  10.4 us (2%)
  local copies, waits for them, and re-layouts  8.28 us (2%)
    pallas_call x1, Pallas kernels, scatter_norm(): pl.pallas_call(functools.partial(scatter_norm_kernel, n, tile), in_specs=...  81.7 us
    pallas_call x1, Pallas kernels, scatter_grads(): pl.pallas_call(functools.partial(scatter_grads_kernel, n, tile), in_specs...  75.3 us
    pallas_call x1, Pallas kernels, scatter_mlp(): pl.pallas_call(functools.partial(scatter_mlp_kernel, n, tile), in_specs=[...  59.9 us
    pallas_call x1, Pallas kernels, mlp(): pl.pallas_call(functools.partial(mlp_kernel, n, tile), in_specs=[pl.Block...  56.4 us
    pallas_call x1, Pallas kernels, gather_t(): pl.pallas_call(functools.partial(gather_t_kernel, n, tile), in_specs=[pl....  55.8 us
    pallas_call x1, Pallas kernels, gather_grads(): pl.pallas_call(functools.partial(gather_grads_kernel, n), in_specs=[pl.Bl...  51.6 us
    pallas_call x1, Pallas kernels, attention_bwd(): pl.pallas_call(functools.partial(attn_bwd_kernel, heads, hd), grid_spec=p...  34 us
    pallas_call x1, Pallas kernels, attention_fwd(): pl.pallas_call(functools.partial(attn_fwd_kernel, heads, hd), grid_spec=p...  17.1 us
  transfers between devices with their start and end apart: 2, of which 0 were waited for; matrix products, arithmetic and copies ran while one was open for 1% of the time, Pallas kernels for 45%

profile of v4, /device:TPU:81, one launch (start us, length us, event | category | flops | bytes accessed | tf_op | source)
XLA Modules:
  0.0 465.5 jit_solution(16212638070531125070)
XLA Ops:
  7.2 0.0 copy-start
  7.2 0.0 copy-start.4
  7.2 0.1 all-gather.2.cloned.1.call-start
  7.3 1.7 convert_reduce_fusion.1
  8.9 1.8 fusion.2
  10.8 0.0 copy-done.4
  10.8 0.0 copy-done
  10.8 1.5 fusion.4.x_ref
  12.3 0.0 copy-start.7
  12.3 0.0 copy-start.6
  12.3 55.8 %gather_t.1 = (bf16[2048,2560]{1,0:T(8,128)(2,1)}, bf16[960,2048]{1,0:T(8,128)(2,1)}) custom-call(bf16[256,2560]{1,0:T(8,128)(2,1)} %fusion.4.x_ref, bf16[960,2560]{1,0:T(8,128)(2,1)} %bitcast.25), custom_call_target="tpu_custom_call" | custom-call | flops 40000000000 | bytes 15728640 | tf_op jit(solution)/shard_map/gather_t/pallas_call | solution.py:326
  68.1 0.1 all-gather.2.cloned.1.call-update
  68.2 0.1 reduce-scatter.2.cloned.1.call-start
  68.3 0.0 copy-done.7
  68.3 1.7 convert_reduce_fusion
  70.0 0.0 copy-start.8
  70.0 0.1 slice.9
  70.1 0.0 copy-done.6
  70.1 0.6 reshape.46.gain_ref
  70.7 0.5 and_select_fusion.lo_ref
  71.2 0.0 copy-done.8
  71.2 17.1 %attn_fwd.1 = (bf16[320,2048]{1,0:T(8,128)(2,1)}, f32[8,2048]{1,0:T(8,128)}) custom-call(s32[8]{0:T(128)} %and_select_fusion.lo_ref, bf16[960,2048]{1,0:T(8,128)(2,1)} %get-tuple-element.36.qkv_ref, s32[1,2048]{1,0:T(1,128)} %bitcast.30), custom_call_target="tpu_custom_call" | custom-call | flops 21474836480 | bytes 3932160 | tf_op jit(solution)/shard_map/attn_fwd/pallas_call | solution.py:99
  88.4 81.7 %scatter_norm.1 = (bf16[256,2560]{1,0:T(8,128)(2,1)}, bf16[256,2560]{1,0:T(8,128)(2,1)}) custom-call(bf16[320,2048]{1,0:T(8,128)(2,1)} %get-tuple-element.37.x_ref.o_ref, bf16[320,2560]{1,0:T(8,128)(2,1)} %bitcast.27, bf16[256,2560]{1,0:T(8,128)(2,1)} %bitcast.18, f32[1,2560]{1,0:T(1,128)} %reshape.46.gain_ref), custom_call_target="tpu_custom_call" | custom-call | flops 40000000000 | bytes 15728640 | tf_op jit(solution)/shard_map/scatter_norm/pallas_call | solution.py:737
  170.0 0.0 all-gather.2.cloned.1.call-done.dy_ref
  170.0 56.4 %gather_mlp.1 = (bf16[2048,2560]{1,0:T(8,128)(2,1)}, bf16[2048,1280]{1,0:T(8,128)(2,1)}, bf16[2048,1280]{1,0:T(8,128)(2,1)}) custom-call(bf16[256,2560]{1,0:T(8,128)(2,1)} %get-tuple-element.39.x_ref, bf16[2048,2560]{1,0:T(8,128)(2,1)} %all-gather.2.cloned.1.call-done.dy_ref, bf16[2560,1280]{1,0:T(8,128)(2,1)} %up_ref.3, bf16[1280,2560]{1,0:T(8,128)(2,1)} %down_ref.3), custom_call_target="tpu_custom_call" | custom-call | flops 40000000000 | bytes 15728640 | tf_op jit(solution)/shard_map/gather_mlp/pallas_call | solution.py:425
  226.4 59.9 %scatter_mlp.1 = (bf16[256,2560]{1,0:T(8,128)(2,1)}, bf16[2048,2560]{1,0:T(8,128)(2,1)}, f32[1,2560]{1,0:T(1,128)}) custom-call(bf16[2048,1280]{1,0:T(8,128)(2,1)} %get-tuple-element.41.dz_ref, bf16[2560,1280]{1,0:T(8,128)(2,1)} %up_ref.3, bf16[2048,1280]{1,0:T(8,128)(2,1)} %get-tuple-element.42.g_ref, bf16[1280,2560]{1,0:T(8,128)(2,1)} %down_ref.3, ...), custom_call_target="tpu_custom_call" | custom-call | flops 60000002048 | bytes 15728640 | tf_op jit(solution)/shard_map/scatter_mlp/pallas_call | solution.py:912
  286.4 51.6 %gather_grads.1 = (bf16[2048,2560]{1,0:T(8,128)(2,1)}, bf16[320,2048]{1,0:T(8,128)(2,1)}, bf16[2560,1280]{1,0:T(8,128)(2,1)}, bf16[1280,2560]{1,0:T(8,128)(2,1)}) custom-call(bf16[256,2560]{1,0:T(8,128)(2,1)} %get-tuple-element.44.x_ref.dmid_ref, bf16[320,2560]{1,0:T(8,128)(2,1)} %bitcast.28, bf16[2048,2560]{1,0:T(8,128)(2,1)} %get-tuple-element.45.b_ref, ...), custom_call_target="tpu_custom_call" | custom-call | flops 60000002048 | bytes 31457280 | tf_op jit(solution)/shard_map/gather_grads/pallas_call | solution.py:554
  338.0 0.0 copy-start.5
  338.0 0.1 reduce-scatter.2.cloned.1.call-update
  338.1 0.6 copy-done.5
  338.7 0.6 broadcast_in_dim.24.gain_ref
  339.3 34.0 %attn_bwd.1 = (bf16[960,2048]{1,0:T(8,128)(2,1)}, bf16[2560,1280]{1,0:T(8,128)(2,1)}, bf16[1280,2560]{1,0:T(8,128)(2,1)}) custom-call(s32[8]{0:T(128)} %and_select_fusion.lo_ref, bf16[960,2048]{1,0:T(8,128)(2,1)} %get-tuple-element.36.qkv_ref, bf16[320,2048]{1,0:T(8,128)(2,1)} %get-tuple-element.37.x_ref.o_ref, bf16[320,2048]{1,0:T(8,128)(2,1)} %get-tuple-element.48.do_ref, ...), custom_call_target="tpu_custom_call" | custom-call | flops 53687091200 | bytes 7864320 | tf_op jit(solution)/shard_map/attn_bwd/pallas_call | solution.py:178
  373.3 75.3 %scatter_grads.1 = (bf16[256,2560]{1,0:T(8,128)(2,1)}, bf16[960,2560]{1,0:T(8,128)(2,1)}, bf16[320,2560]{1,0:T(8,128)(2,1)}, bf16[2,2560]{1,0:T(2,128)(2,1)}) custom-call(bf16[960,2048]{1,0:T(8,128)(2,1)} %get-tuple-element.52.x_ref, bf16[960,2560]{1,0:T(8,128)(2,1)} %bitcast.26, bf16[2048,2560]{1,0:T(8,128)(2,1)} %get-tuple-element.53.a_ref, ...), custom_call_target="tpu_custom_call" | custom-call | flops 60000002048 | bytes 31457280 | tf_op jit(solution)/shard_map/scatter_grads/pallas_call | solution.py:820
  448.7 0.0 copy-start.3
  448.7 1.5 slice_reduce_fusion
  450.1 0.0 reduce-scatter.2.cloned.1.call-done
  450.1 0.0 copy-start.1
  450.1 3.2 fusion.5
  453.4 0.0 copy-done.3
  453.4 1.1 copy.20
  454.4 0.0 copy-done.1
  454.4 0.0 copy-start.2
  454.4 2.3 copy.21
  456.7 0.4 copy-done.2
  457.1 1.2 copy.22
  (3 shorter events, 0.0 us)
Async XLA Ops:
  7.2 3.6 copy-start
  7.2 3.6 copy-start.4
  7.2 162.8 %all-gather.2.cloned.1.call-start = ((), (), s32[]{:S(2)}) async-start(), calls=%async_computation.1 | async-start | bytes 11796480 | tf_op jit(solution)/shard_map/all_gather | solution.py:937
  12.3 56.0 %copy-start.7 = (s32[1,2048]{1,0:T(1,128)S(1)}, s32[1,2048]{1,0:T(1,128)}, u32[]{:S(2)}) copy-start(s32[1,2048]{1,0:T(1,128)} %param.10) | copy-start | bytes 24580
  12.3 57.8 %copy-start.6 = (bf16[2560]{0:T(1024)(128)(2,1)S(1)}, bf16[2560]{0:T(1024)(128)(2,1)}, u32[]{:S(2)}) copy-start(bf16[2560]{0:T(1024)(128)(2,1)} %param.14) | copy-start | bytes 15364
  68.2 382.0 %reduce-scatter.2.cloned.1.call-start = ((), (), s32[]{:S(2)}) async-start(), calls=%async_computation.2 | async-start | bytes 11796480 | tf_op jit(solution)/shard_map/reduce_scatter | solution.py:938
  70.0 1.2 copy-start.8
  338.0 0.7 copy-start.5
  448.7 4.7 %copy-start.3 = (bf16[256,2560]{1,0:T(8,128)(2,1)S(1)}, bf16[256,2560]{1,0:T(8,128)(2,1)}, u32[]{:S(2)}) copy-start(bf16[256,2560]{1,0:T(8,128)(2,1)} %get-tuple-element.56) | copy-start | bytes 3932164
  450.1 4.3 copy-start.1
  454.4 2.6 copy-start.2
Sparse Core Ops, SparseCore 0:
  68.3 81.2 all-gather.1
  338.2 77.9 reduce-scatter.1

commit v5 on v4

--- a/solution.py
+++ b/solution.py
@@ -566,22 +566,26 @@
     )(x, w, b1, dz, g, dy)
 
 
-def add_rows(dst, start, count, *terms):
+def add_rows(dst, start, count, *terms, cols=slice(None)):
     step = 32
 
     def body(i, c):
         at = rows_at(start + i * step, step)
-        total = dst[at, :].astype(jnp.float32)
+        total = dst[at, cols].astype(jnp.float32)
         for ref, first in terms:
-            total = total + ref[rows_at(first + i * step, step), :].astype(jnp.float32)
-        dst[at, :] = total.astype(jnp.bfloat16)
+            total = total + ref[rows_at(first + i * step, step), cols].astype(jnp.float32)
+        dst[at, cols] = total.astype(jnp.bfloat16)
         return c
 
     lax.fori_loop(0, count // step, body, 0)
 
 
 class Scatter:
-    def __init__(self, ring, part, pin, mid, fin, send, recv):
+    def __init__(self, ring, part, pin, mid, fin, send, recv, tile=512):
+        self.tiles, self.first_tiles = part.shape[2] // tile, 2
+        cut = self.first_tiles * tile
+        self.cols = {2: slice(0, cut), 4: slice(0, cut), 5: slice(0, cut)}
+        self.cols.update({k: slice(cut, part.shape[2]) for k in (10, 11, 12)})
         self.ring, self.part, self.pin, self.mid, self.fin, self.send, self.recv = ring, part, pin, mid, fin, send, recv
         self.rows = part.shape[1] // 2
         self.half = self.rows // 2
@@ -589,11 +593,17 @@
 
     def copy(self, k):
         r, h = self.ring, self.half
-        if k < 4:
+        cols = self.cols.get(k)
+        if k in (2, 10):
+            src, dst, dev = self.part.at[2, rows_at((1 - r.core) * self.rows, self.rows), cols], self.pin.at[2, :, cols], r.partner
+        elif k in (4, 11):
+            src, dst, dev = self.part.at[2, rows_at(self.own, h), cols], self.mid.at[0, :, cols], r.next
+        elif k in (5, 12):
+            src, dst, dev = self.part.at[2, rows_at(self.own + h, h), cols], self.mid.at[1, :, cols], r.prev
+        elif k < 4:
             src, dst, dev = self.part.at[k, rows_at((1 - r.core) * self.rows, self.rows)], self.pin.at[k], r.partner
         else:
-            d, half, dst, dev = {4: (2, 0, self.mid.at[0], r.next), 5: (2, 1, self.mid.at[1], r.prev),
-                                 6: (1, 1, self.fin.at[0, h:], r.next), 7: (1, 0, self.fin.at[0, :h], r.next),
+            d, half, dst, dev = {6: (1, 1, self.fin.at[0, h:], r.next), 7: (1, 0, self.fin.at[0, :h], r.next),
                                  8: (3, 0, self.fin.at[1, :h], r.prev), 9: (3, 1, self.fin.at[1, h:], r.prev)}[k]
             src = self.part.at[d, rows_at(self.own + half * h, h)]
         return pltpu.make_async_remote_copy(src_ref=src, dst_ref=dst, send_sem=self.send.at[k], recv_sem=self.recv.at[k],
@@ -611,25 +621,30 @@
 
     def run(self, product, filler, emit):
         h = self.half
-        product(2, self.rows - self.own, self.rows, True)
-        self.start(2)
-        product(2, self.own, self.rows, False)
-        self.join(2)
-        self.start(4)
-        self.start(5)
+        every = (0, self.tiles)
+        for lo, hi, away, up, down in ((0, self.first_tiles, 2, 4, 5), (self.first_tiles, self.tiles, 10, 11, 12)):
+            product(2, self.rows - self.own, self.rows, (lo, hi), True)
+            self.start(away)
+            product(2, self.own, self.rows, (lo, hi), False)
+            self.arrived(away)
+            add_rows(self.part.at[2], self.own, self.rows, (self.pin.at[2], 0), cols=self.cols[away])
+            self.start(up)
+            self.start(down)
         for d in (1, 3):
-            product(d, 0, 2 * self.rows, False)
+            product(d, 0, 2 * self.rows, every, False)
             self.start(d)
         self.join(1)
         self.start(6)
         self.join(3)
         self.start(8)
-        product(0, 0, 2 * self.rows, False)
+        product(0, 0, 2 * self.rows, every, False)
         self.start(0)
         self.arrived(4)
+        self.arrived(11)
         add_rows(self.part.at[1], self.own, h, (self.mid.at[0], 0))
         self.start(7)
         self.arrived(5)
+        self.arrived(12)
         add_rows(self.part.at[3], self.own + h, h, (self.mid.at[1], 0))
         self.start(9)
         self.join(0)
@@ -646,7 +661,7 @@
             return c
 
         lax.fori_loop(0, self.rows // step, body, 0)
-        for k in range(10):
+        for k in range(13):
             self.copy(k).wait_send()
 
 
@@ -657,6 +672,23 @@
     return cen * rstd, rstd
 
 
+def prepare_norm(x_s, hat_s, rstd_s):
+    step = 16
+
+    def body(i, c):
+        at = rows_at(i * step, step)
+        hat, rstd = normalized(x_s[at, :].astype(jnp.float32))
+        hat_s[at, :] = hat
+        rstd_s[at, :] = jnp.broadcast_to(rstd, (step, rstd_s.shape[1]))
+        return c
+
+    lax.fori_loop(0, x_s.shape[0] // step, body, 0)
+
+
+def norm_scratch(rows, hidden):
+    return [pltpu.VMEM((rows, hidden), jnp.float32), pltpu.VMEM((rows, 128), jnp.float32)]
+
+
 def norm_backward(hat, rstd, gain, d):
     dh = d * gain
     return rstd * (dh - jnp.mean(dh, axis=-1, keepdims=True) - hat * jnp.mean(dh * hat, axis=-1, keepdims=True))
@@ -685,8 +717,8 @@
 def product_t(ring, tile, x_s, weights, lhs, part):
     wide = part.shape[1]
 
-    def product(d, row0, count, first):
-        if first or d != 2:
+    def product(d, row0, count, tiles, first):
+        if (first and tiles[0] == 0) or d != 2:
             lhs[...] = x_s[:, rows_at(ring.ahead(d) * wide, wide)].T
         at = rows_at(row0, count)
 
@@ -697,7 +729,7 @@
             part[d, at, cols] = dot32(lhs[at, :], weights.dst[:, cols]).astype(jnp.bfloat16)
             return c
 
-        lax.fori_loop(0, weights.count, body, 0)
+        lax.fori_loop(tiles[0], tiles[1], body, 0)
 
     return product
 
@@ -705,7 +737,7 @@
 def scatter_scratch(rows, hidden, dtype):
     dma = pltpu.SemaphoreType.DMA
     return [pltpu.VMEM((4, 2 * rows, hidden), dtype), pltpu.VMEM((4, rows, hidden), dtype),
-            pltpu.VMEM((2, rows // 2, hidden), dtype), pltpu.VMEM((2, rows, hidden), dtype), dma((10,)), dma((10,))]
+            pltpu.VMEM((2, rows // 2, hidden), dtype), pltpu.VMEM((2, rows, hidden), dtype), dma((13,)), dma((13,))]
 
 
 def scatter_norm_kernel(n, tile, x_ref, w_ref, res_ref, gain_ref, mid_ref, norm_ref,
@@ -749,7 +781,7 @@
 
 def scatter_grads_kernel(n, tile, x_ref, w_ref, a_ref, o_ref, d_ref, res_ref, dmid_ref, gain_ref, dg2_ref,
                          out_ref, gq_ref, go_ref, sums_ref,
-                         x_s, w_s, lhs, o_s, a_s, d_s, gq_st, go_st, res_s, dmid_s, acc, mine, slots,
+                         x_s, w_s, lhs, o_s, a_s, d_s, gq_st, go_st, res_s, dmid_s, acc, mine, slots, hat_s, rstd_s,
                          part, pin, mid, fin, send, recv, load, wl, a_l, a_p, d_l, d_p, gsend, grecv):
     ring = Ring(n)
     peers = [lax.rem(ring.me + k, n) for k in range(1, n)]
@@ -775,11 +807,11 @@
         wo.run(0, wo.total)
         loads[2].wait()
         loads[3].wait()
+        prepare_norm(res_s, hat_s, rstd_s)
 
     def emit(at, total):
-        hat, _ = normalized(res_s[at, :].astype(jnp.float32))
         out_ref[at, :] = total
-        acc[...] += fold_rows(total.astype(jnp.float32) * hat)
+        acc[...] += fold_rows(total.astype(jnp.float32) * hat_s[at, :])
 
     sc.run(product_t(ring, tile, x_s, weights, lhs, part), filler, emit)
     mine[0:1, :] = jnp.sum(acc[...], axis=0, keepdims=True)
@@ -788,8 +820,7 @@
 
     def body(i, c):
         at = rows_at(i * step, step)
-        hat, rstd = normalized(res_s[at, :].astype(jnp.float32))
-        dx = norm_backward(hat, rstd, gain_ref[...], out_ref[at, :].astype(jnp.float32))
+        dx = norm_backward(hat_s[at, :], rstd_s[at, 0:1], gain_ref[...], out_ref[at, :].astype(jnp.float32))
         out_ref[at, :] = (dmid_s[at, :].astype(jnp.float32) + dx).astype(jnp.bfloat16)
         return c
 
@@ -826,7 +857,7 @@
         scratch_shapes=[vmem(*x.shape), vmem(*w.shape), vmem(2 * rows, m), vmem(*o.shape), vmem(2, seq, tile), vmem(2, seq, tile),
                         vmem(2, m, tile), vmem(2, o.shape[0], tile), vmem(rows, hidden), vmem(rows, hidden),
                         pltpu.VMEM((8, hidden), jnp.float32), pltpu.VMEM((2, hidden), jnp.float32),
-                        pltpu.VMEM((n, 2, hidden), jnp.float32)]
+                        pltpu.VMEM((n, 2, hidden), jnp.float32)] + norm_scratch(rows, hidden)
         + scatter_scratch(rows, hidden, x.dtype)
         + [dma((4,)), dma((hidden // tile,)), dma((2,)), dma((2,)), dma((2,)), dma((2,)), dma((n - 1,)), dma((n - 1,))],
         compiler_params=pltpu.CompilerParams(collective_id=cid, has_side_effects=True, vmem_limit_bytes=63 * 2 ** 20),
@@ -836,7 +867,7 @@
 
 
 def scatter_mlp_kernel(n, tile, dz_ref, up_ref, g_ref, down_ref, res_ref, dy_ref, gain_ref, out_ref, y_ref, dg_ref,
-                       dz_s, w_s, g_s, down_s, res_s, dy_s, acc, part, pin, mid, fin, send, recv, load, wl, zl, ystage, put):
+                       dz_s, w_s, g_s, down_s, res_s, dy_s, acc, hat_s, rstd_s, part, pin, mid, fin, send, recv, load, wl, zl, ystage, put):
     ring = Ring(n)
     loads = [pltpu.make_async_copy(a, b, load.at[i]) for i, (a, b) in
              enumerate(((res_ref, res_s), (dy_ref, dy_s), (g_ref, g_s), (down_ref, down_s)))]
@@ -856,8 +887,8 @@
     sc = Scatter(ring, part, pin, mid, fin, send, recv)
     acc[...] = jnp.zeros_like(acc)
 
-    def product(d, row0, count, first):
-        if first or d != 2:
+    def product(d, row0, count, tiles, first):
+        if (first and tiles[0] == 0) or d != 2:
             dz_loads[d].wait()
         if d == 3:
             for cp in loads:
@@ -872,12 +903,12 @@
             part[d, at, cols] = dot_nt(dz_s[src, :], w_s[cols, :]).astype(jnp.bfloat16)
             return c
 
-        lax.fori_loop(0, hidden // tile, body, 0)
+        lax.fori_loop(tiles[0], tiles[1], body, 0)
 
     def emit(at, total):
         d = total.astype(jnp.float32)
-        hat, rstd = normalized(res_s[at, :].astype(jnp.float32))
-        dx = norm_backward(hat, rstd, gain_ref[...], d)
+        hat = hat_s[at, :]
+        dx = norm_backward(hat, rstd_s[at, 0:1], gain_ref[...], d)
         out_ref[at, :] = (dy_s[at, :].astype(jnp.float32) + dx).astype(jnp.bfloat16)
         acc[...] += fold_rows(d * hat)
 
@@ -897,6 +928,7 @@
             lax.fori_loop(0, hidden // tile, body, 0)
             puts.append(pltpu.make_async_copy(ystage.at[q % 2], y_ref.at[q * wide:(q + 1) * wide], put.at[q]))
             puts[q].start()
+        prepare_norm(res_s, hat_s, rstd_s)
         for cp in puts[-2:]:
             cp.wait()
 
@@ -916,7 +948,7 @@
         out_shape=[jax.ShapeDtypeStruct((rows, hidden), dz.dtype), jax.ShapeDtypeStruct((seq, hidden), dz.dtype),
                    jax.ShapeDtypeStruct((1, hidden), jnp.float32)],
         scratch_shapes=[pltpu.VMEM(a.shape, a.dtype) for a in (dz, up, g, down, res, dy)]
-        + [pltpu.VMEM((8, hidden), jnp.float32)] + scatter_scratch(rows, hidden, dz.dtype)
+        + [pltpu.VMEM((8, hidden), jnp.float32)] + norm_scratch(rows, hidden) + scatter_scratch(rows, hidden, dz.dtype)
         + [dma((4,)), dma((hidden // tile,)), dma((4,)), pltpu.VMEM((2, 2 * rows, hidden), dz.dtype), dma((n // 2,))],
         compiler_params=pltpu.CompilerParams(collective_id=cid, has_side_effects=True, vmem_limit_bytes=63 * 2 ** 20),
         cost_estimate=pl.CostEstimate(flops=60 * 10 ** 9, bytes_accessed=3 * seq * hidden, transcendentals=0),

time: 471 us -> 464 us (0.985)
  Pallas kernels: 432 us -> 425 us
    pallas_call x1, Pallas kernels: 75.3 us -> 61 us  [scatter_grads(): pl.pallas_call(functools.partial(scatter_grads_kernel, n, tile), in_specs...]
    pallas_call x1, Pallas kernels: 34 us -> 44.7 us  [attention_bwd(): pl.pallas_call(functools.partial(attn_bwd_kernel, heads, hd), grid_spec=p...]
    pallas_call x1, Pallas kernels: 17.1 us -> 22.6 us  [attention_fwd(): pl.pallas_call(functools.partial(attn_fwd_kernel, heads, hd), grid_spec=p...]
    pallas_call x1, Pallas kernels: 81.7 us -> 76.3 us  [scatter_norm(): pl.pallas_call(functools.partial(scatter_norm_kernel, n, tile), in_specs=...]
    pallas_call x1, Pallas kernels: 59.9 us -> 55 us  [scatter_mlp(): pl.pallas_call(functools.partial(scatter_mlp_kernel, n, tile), in_specs=[...]
where the time goes in v5:
time: 464 us; the launch traced here: 458 us
  Pallas kernels  425 us (92%)
  between operations  14.7 us (3%)
  other arithmetic  10.4 us (2%)
  local copies, waits for them, and re-layouts  8.28 us (2%)
    pallas_call x1, Pallas kernels, scatter_norm(): pl.pallas_call(functools.partial(scatter_norm_kernel, n, tile), in_specs=...  76.3 us
    pallas_call x1, Pallas kernels, scatter_grads(): pl.pallas_call(functools.partial(scatter_grads_kernel, n, tile), in_specs...  61 us
    pallas_call x1, Pallas kernels, mlp(): pl.pallas_call(functools.partial(mlp_kernel, n, tile), in_specs=[pl.Block...  56.4 us
    pallas_call x1, Pallas kernels, gather_t(): pl.pallas_call(functools.partial(gather_t_kernel, n, tile), in_specs=[pl....  55.8 us
    pallas_call x1, Pallas kernels, scatter_mlp(): pl.pallas_call(functools.partial(scatter_mlp_kernel, n, tile), in_specs=[...  55 us
    pallas_call x1, Pallas kernels, gather_grads(): pl.pallas_call(functools.partial(gather_grads_kernel, n), in_specs=[pl.Bl...  53 us
    pallas_call x1, Pallas kernels, attention_bwd(): pl.pallas_call(functools.partial(attn_bwd_kernel, heads, hd), grid_spec=p...  44.7 us
    pallas_call x1, Pallas kernels, attention_fwd(): pl.pallas_call(functools.partial(attn_fwd_kernel, heads, hd), grid_spec=p...  22.6 us
  transfers between devices with their start and end apart: 2, of which 0 were waited for; matrix products, arithmetic and copies ran while one was open for 1% of the time, Pallas kernels for 45%

profile of v5, /device:TPU:81, one launch (start us, length us, event | category | flops | bytes accessed | tf_op | source)
XLA Modules:
  0.0 458.4 jit_solution(16823069330321260448)
XLA Ops:
  7.2 0.0 copy-start
  7.2 0.0 copy-start.4
  7.2 0.1 all-gather.2.cloned.1.call-start
  7.3 1.7 convert_reduce_fusion.1
  8.9 1.8 fusion.2
  10.8 0.0 copy-done.4
  10.8 0.0 copy-done
  10.8 1.5 fusion.4.x_ref
  12.3 0.0 copy-start.7
  12.3 0.0 copy-start.6
  12.3 55.8 %gather_t.1 = (bf16[2048,2560]{1,0:T(8,128)(2,1)}, bf16[960,2048]{1,0:T(8,128)(2,1)}) custom-call(bf16[256,2560]{1,0:T(8,128)(2,1)} %fusion.4.x_ref, bf16[960,2560]{1,0:T(8,128)(2,1)} %bitcast.25), custom_call_target="tpu_custom_call" | custom-call | flops 40000000000 | bytes 15728640 | tf_op jit(solution)/shard_map/gather_t/pallas_call | solution.py:326
  68.1 0.1 all-gather.2.cloned.1.call-update
  68.2 0.1 reduce-scatter.2.cloned.1.call-start
  68.3 0.0 copy-done.7
  68.3 1.7 convert_reduce_fusion
  70.0 0.0 copy-start.8
  70.0 0.1 slice.9
  70.1 0.0 copy-done.6
  70.1 0.6 reshape.46.gain_ref
  70.7 0.5 and_select_fusion.lo_ref
  71.2 0.0 copy-done.8
  71.2 22.6 %attn_fwd.1 = (bf16[320,2048]{1,0:T(8,128)(2,1)}, f32[8,2048]{1,0:T(8,128)}) custom-call(s32[8]{0:T(128)} %and_select_fusion.lo_ref, bf16[960,2048]{1,0:T(8,128)(2,1)} %get-tuple-element.36.qkv_ref, s32[1,2048]{1,0:T(1,128)} %bitcast.30), custom_call_target="tpu_custom_call" | custom-call | flops 21474836480 | bytes 3932160 | tf_op jit(solution)/shard_map/attn_fwd/pallas_call | solution.py:99
  93.8 76.3 %scatter_norm.1 = (bf16[256,2560]{1,0:T(8,128)(2,1)}, bf16[256,2560]{1,0:T(8,128)(2,1)}) custom-call(bf16[320,2048]{1,0:T(8,128)(2,1)} %get-tuple-element.37.x_ref.o_ref, bf16[320,2560]{1,0:T(8,128)(2,1)} %bitcast.27, bf16[256,2560]{1,0:T(8,128)(2,1)} %bitcast.18, f32[1,2560]{1,0:T(1,128)} %reshape.46.gain_ref), custom_call_target="tpu_custom_call" | custom-call | flops 40000000000 | bytes 15728640 | tf_op jit(solution)/shard_map/scatter_norm/pallas_call | solution.py:769
  170.1 0.0 all-gather.2.cloned.1.call-done.dy_ref
  170.1 56.4 %gather_mlp.1 = (bf16[2048,2560]{1,0:T(8,128)(2,1)}, bf16[2048,1280]{1,0:T(8,128)(2,1)}, bf16[2048,1280]{1,0:T(8,128)(2,1)}) custom-call(bf16[256,2560]{1,0:T(8,128)(2,1)} %get-tuple-element.39.x_ref, bf16[2048,2560]{1,0:T(8,128)(2,1)} %all-gather.2.cloned.1.call-done.dy_ref, bf16[2560,1280]{1,0:T(8,128)(2,1)} %up_ref.3, bf16[1280,2560]{1,0:T(8,128)(2,1)} %down_ref.3), custom_call_target="tpu_custom_call" | custom-call | flops 40000000000 | bytes 15728640 | tf_op jit(solution)/shard_map/gather_mlp/pallas_call | solution.py:425
  226.5 55.0 %scatter_mlp.1 = (bf16[256,2560]{1,0:T(8,128)(2,1)}, bf16[2048,2560]{1,0:T(8,128)(2,1)}, f32[1,2560]{1,0:T(1,128)}) custom-call(bf16[2048,1280]{1,0:T(8,128)(2,1)} %get-tuple-element.41.dz_ref, bf16[2560,1280]{1,0:T(8,128)(2,1)} %up_ref.3, bf16[2048,1280]{1,0:T(8,128)(2,1)} %get-tuple-element.42.g_ref, bf16[1280,2560]{1,0:T(8,128)(2,1)} %down_ref.3, ...), custom_call_target="tpu_custom_call" | custom-call | flops 60000002048 | bytes 15728640 | tf_op jit(solution)/shard_map/scatter_mlp/pallas_call | solution.py:944
  281.5 53.0 %gather_grads.1 = (bf16[2048,2560]{1,0:T(8,128)(2,1)}, bf16[320,2048]{1,0:T(8,128)(2,1)}, bf16[2560,1280]{1,0:T(8,128)(2,1)}, bf16[1280,2560]{1,0:T(8,128)(2,1)}) custom-call(bf16[256,2560]{1,0:T(8,128)(2,1)} %get-tuple-element.44.x_ref.dmid_ref, bf16[320,2560]{1,0:T(8,128)(2,1)} %bitcast.28, bf16[2048,2560]{1,0:T(8,128)(2,1)} %get-tuple-element.45.b_ref, ...), custom_call_target="tpu_custom_call" | custom-call | flops 60000002048 | bytes 31457280 | tf_op jit(solution)/shard_map/gather_grads/pallas_call | solution.py:554
  334.5 0.0 copy-start.5
  334.5 0.1 reduce-scatter.2.cloned.1.call-update
  334.5 0.6 copy-done.5
  335.2 0.6 broadcast_in_dim.24.gain_ref
  335.8 44.7 %attn_bwd.1 = (bf16[960,2048]{1,0:T(8,128)(2,1)}, bf16[2560,1280]{1,0:T(8,128)(2,1)}, bf16[1280,2560]{1,0:T(8,128)(2,1)}) custom-call(s32[8]{0:T(128)} %and_select_fusion.lo_ref, bf16[960,2048]{1,0:T(8,128)(2,1)} %get-tuple-element.36.qkv_ref, bf16[320,2048]{1,0:T(8,128)(2,1)} %get-tuple-element.37.x_ref.o_ref, bf16[320,2048]{1,0:T(8,128)(2,1)} %get-tuple-element.48.do_ref, ...), custom_call_target="tpu_custom_call" | custom-call | flops 53687091200 | bytes 7864320 | tf_op jit(solution)/shard_map/attn_bwd/pallas_call | solution.py:178
  380.5 61.0 %scatter_grads.1 = (bf16[256,2560]{1,0:T(8,128)(2,1)}, bf16[960,2560]{1,0:T(8,128)(2,1)}, bf16[320,2560]{1,0:T(8,128)(2,1)}, bf16[2,2560]{1,0:T(2,128)(2,1)}) custom-call(bf16[960,2048]{1,0:T(8,128)(2,1)} %get-tuple-element.52.x_ref, bf16[960,2560]{1,0:T(8,128)(2,1)} %bitcast.26, bf16[2048,2560]{1,0:T(8,128)(2,1)} %get-tuple-element.53.a_ref, ...), custom_call_target="tpu_custom_call" | custom-call | flops 60000002048 | bytes 31457280 | tf_op jit(solution)/shard_map/scatter_grads/pallas_call | solution.py:851
  441.5 0.0 copy-start.3
  441.5 1.5 slice_reduce_fusion
  443.0 0.0 reduce-scatter.2.cloned.1.call-done
  443.0 0.0 copy-start.1
  443.0 3.2 fusion.5
  446.2 0.0 copy-done.3
  446.2 1.1 copy.20
  447.3 0.0 copy-done.1
  447.3 0.0 copy-start.2
  447.3 2.3 copy.21
  449.6 0.4 copy-done.2
  449.9 1.2 copy.22
  (3 shorter events, 0.0 us)
Async XLA Ops:
  7.2 3.6 copy-start
  7.2 3.6 copy-start.4
  7.2 162.9 %all-gather.2.cloned.1.call-start = ((), (), s32[]{:S(2)}) async-start(), calls=%async_computation.1 | async-start | bytes 11796480 | tf_op jit(solution)/shard_map/all_gather | solution.py:969
  12.3 56.0 %copy-start.7 = (s32[1,2048]{1,0:T(1,128)S(1)}, s32[1,2048]{1,0:T(1,128)}, u32[]{:S(2)}) copy-start(s32[1,2048]{1,0:T(1,128)} %param.10) | copy-start | bytes 24580
  12.3 57.8 %copy-start.6 = (bf16[2560]{0:T(1024)(128)(2,1)S(1)}, bf16[2560]{0:T(1024)(128)(2,1)}, u32[]{:S(2)}) copy-start(bf16[2560]{0:T(1024)(128)(2,1)} %param.14) | copy-start | bytes 15364
  68.2 374.8 %reduce-scatter.2.cloned.1.call-start = ((), (), s32[]{:S(2)}) async-start(), calls=%async_computation.2 | async-start | bytes 11796480 | tf_op jit(solution)/shard_map/reduce_scatter | solution.py:970
  70.0 1.2 copy-start.8
  334.5 0.7 copy-start.5
  441.5 4.7 %copy-start.3 = (bf16[256,2560]{1,0:T(8,128)(2,1)S(1)}, bf16[256,2560]{1,0:T(8,128)(2,1)}, u32[]{:S(2)}) copy-start(bf16[256,2560]{1,0:T(8,128)(2,1)} %get-tuple-element.56) | copy-start | bytes 3932164
  443.0 4.3 copy-start.1
  447.3 2.6 copy-start.2
Sparse Core Ops, SparseCore 0:
  68.3 78.1 all-gather.1
  334.7 61.8 reduce-scatter.1
